TPU v7x, 128 devices: a whole 4x4x4 slice. The times are simulated.
128 devices in a mesh: section: 4 (over z), dp: 8 (over y, core), mp: 4 (over x).
Axes of the slice: x: 4, y: 4, z: 4, core: 2. Of those that a mesh axis runs over, the one named last changes fastest.
Arguments:
- text: bfloat16 [4, 4096, 4096], P('section', ('dp', 'mp')), may hold values from -6 to 6
- patches: bfloat16 [16384, 1024], P(('section', 'dp')), may hold values from -6 to 6
- segments: int32 [4, 8, 512], P('section', 'dp'), may hold values from 0 to 3, never falling along the last dimension, each value on 1 to 256 neighbouring positions
- loss_mask: int32 [4, 4096], P('section', ('dp', 'mp')), may hold values from 0 to 1, as said below
- tile_batch: int32 [8, 8], P('dp'), may hold values from 0 to 3, as said below
- tile_offset: int32 [8, 8], P('dp'), may hold values from 0 to 448, as said below
- attn_gain: float32 [4, 4096], P('section'), may hold values from 0.5 to 2
- w_query: bfloat16 [4, 4096, 2048], P('section', None, 'mp'), may hold values from -0.09375 to 0.09375
- w_kv: bfloat16 [4, 2, 4096, 512], P('section', None, None, 'mp'), may hold values from -0.09375 to 0.09375
- w_out: bfloat16 [4, 2048, 4096], P('section', 'mp'), may hold values from -0.125 to 0.125
- vis_gain: float32 [2, 1024], replicated, may hold values from 0.5 to 2
- vis_bias: float32 [2, 1024], replicated, may hold values from -3 to 3
- v_qkv: bfloat16 [3, 1024, 1024], P(None, ('section', 'dp'), 'mp'), may hold values from -0.1875 to 0.1875
- v_out: bfloat16 [1024, 1024], P('mp', ('section', 'dp')), may hold values from -0.1875 to 0.1875
- v_up: bfloat16 [1024, 4096], P(('section', 'dp'), 'mp'), may hold values from -0.1875 to 0.1875
- v_down: bfloat16 [4096, 1024], P('mp', ('section', 'dp')), may hold values from -0.09375 to 0.09375
- v_proj: bfloat16 [4096, 4096], P(('section', 'dp'), 'mp'), may hold values from -0.09375 to 0.09375
Outputs:
- hidden: bfloat16 [4, 4096, 4096], P('section', ('dp', 'mp'))
- token_weight: float32 [4, 4096], P('section', ('dp', 'mp'))
Inputs may be any that keep to these rules, and one draw needn't show every extreme that they name: `tile_batch`: in every data-parallel index, the 2 tiles of each section index go 1 to each of two different micro-batches; one micro-batch receives 1 tiles from every section index. `tile_offset`: offsets are multiples of 64; the runs of one sequence never intersect. `loss_mask`: the first position of every sequence is a one.
All inputs are finite; a program needn't handle non-finite values.
Results may differ from a plain program's by a relative error of at most 0.025.
Values may be sent and summed in bfloat16 or wider, within the bound.
A program may use at most 192 MiB of HBM per device.

v0:
```python
import jax
import jax.numpy as jnp
from jax import lax
from jax.sharding import Mesh
from jax.sharding import PartitionSpec as P

HD = 128
VHD = 64
GRID = 16
PATCH = 256
POOL = 64
SECTION_DP = ("section", "dp_0", "dp_1")
SECTION_DP_MP = ("section", "dp_0", "dp_1", "mp")
DP = ("dp_0", "dp_1")
DP_MP = ("dp_0", "dp_1", "mp")


EPS = 1e-05
ROPE_BASE = 500000.0
BLOCKED = -1e30


def copy_for_each(array, axis):
    copies = jnp.broadcast_to(array, (lax.axis_size(axis), *array.shape))
    return lax.all_to_all(copies, axis, split_axis=0, concat_axis=0, tiled=True)


def over_copies(array, axis):
    everything = copy_for_each(array, axis)
    return jnp.sum(everything.astype(jnp.float32), axis=0)


def laid_out(tiles, dim):
    lengths = list(tiles.shape[1:])
    lengths[dim] *= tiles.shape[0]
    return jnp.moveaxis(tiles, 0, dim).reshape(lengths)


def one_gather(arrays, axis, dims):
    flat = jnp.concatenate([a.reshape(-1) for a in arrays])
    lines, at, done = (lax.all_gather(flat, axis), 0, [])
    for a, dim in zip(arrays, dims):
        tiles = lines[:, at : at + a.size].reshape(-1, *a.shape)
        done.append(laid_out(tiles, dim))
        at += a.size
    return tuple(done)


def shifted(value, axis, steps):
    count = lax.axis_size(axis)
    pairs = [(source, (source + steps) % count) for source in range(count)]
    return lax.ppermute(value, axis, pairs)


def over_axes(array, axes):
    for axis in axes:
        array = lax.psum(array, axis)
    return array


def layer_norm(values, gain, bias):
    wide = values.astype(jnp.float32)
    center = wide - jnp.mean(wide, axis=-1, keepdims=True)
    spread = jnp.mean(center * center, axis=-1, keepdims=True)
    return (center * lax.rsqrt(spread + EPS) * gain + bias).astype(jnp.bfloat16)


def rms_norm(values, gain):
    wide = values.astype(jnp.float32)
    power = jnp.mean(wide * wide, axis=-1, keepdims=True)
    return (wide * lax.rsqrt(power + EPS) * gain).astype(jnp.bfloat16)


def rotate(values, positions):
    half_width = values.shape[-1] // 2
    freqs = ROPE_BASE ** (-2.0 * jnp.arange(half_width, dtype=jnp.float32) / values.shape[-1])
    angles = positions.astype(jnp.float32)[:, None] * freqs[None, :]
    cosine = jnp.cos(angles)[:, None, :]
    sinus_part = jnp.sin(angles)[:, None, :]
    first_half = values[..., :half_width]
    second_half = values[..., half_width:]
    return jnp.concatenate(
        [
            first_half * cosine - second_half * sinus_part,
            second_half * cosine + first_half * sinus_part,
        ],
        axis=-1,
    )


def pixel_shuffle(states):
    tile_count = states.shape[0] // PATCH
    side_half = GRID // 2
    width = states.shape[1]
    arranged = states.reshape(tile_count, side_half, 2, side_half, 2, width)
    return arranged.transpose(0, 1, 3, 2, 4, 5).reshape(
        tile_count * side_half * side_half, 4 * width
    )


def block_sum(partial_value):
    return over_copies(partial_value.astype(jnp.bfloat16), "mp").astype(jnp.float32)


def encode_tiles(patches, vis_gain, vis_bias, qkv_full, out_full, up_full, down_full, proj_full):
    tile_count = patches.shape[0] // PATCH
    local_width = qkv_full.shape[2]
    head_count = local_width // VHD
    normed = layer_norm(patches, vis_gain[0], vis_bias[0])
    projected = [
        jnp.dot(normed, qkv_full[index], preferred_element_type=jnp.float32)
        .astype(jnp.bfloat16)
        .reshape(tile_count, PATCH, head_count, VHD)
        for index in range(3)
    ]
    scores = jnp.einsum(
        "tqhd,tkhd->thqk", projected[0], projected[1], preferred_element_type=jnp.float32
    ) * VHD ** (-0.5)
    probs = jax.nn.softmax(scores, axis=-1).astype(jnp.bfloat16)
    mixed = (
        jnp.einsum("thqk,tkhd->tqhd", probs, projected[2], preferred_element_type=jnp.float32)
        .astype(jnp.bfloat16)
        .reshape(tile_count * PATCH, local_width)
    )
    attended = block_sum(jnp.dot(mixed, out_full, preferred_element_type=jnp.float32))
    residual = (patches.astype(jnp.float32) + attended).astype(jnp.bfloat16)
    normed_two = layer_norm(residual, vis_gain[1], vis_bias[1])
    inner = jax.nn.gelu(
        jnp.dot(normed_two, up_full, preferred_element_type=jnp.float32), approximate=False
    ).astype(jnp.bfloat16)
    fed = block_sum(jnp.dot(inner, down_full, preferred_element_type=jnp.float32))
    states = (residual.astype(jnp.float32) + fed).astype(jnp.bfloat16)
    return jnp.dot(pixel_shuffle(states), proj_full, preferred_element_type=jnp.float32).astype(
        jnp.bfloat16
    )


def decoder_layer(active, state, segment_ids, gain, w_query, w_kv, w_out):
    normed = rms_norm(state, gain)
    query_width = w_query.shape[1]
    pair_width = w_kv.shape[2]
    joined_width = query_width + 2 * pair_width
    model_width = w_out.shape[1]
    piece = lax.all_gather(normed, "mp", axis=0, tiled=True)
    row_count = piece.shape[0]

    def project_computed(rows):
        positions = jnp.arange(row_count, dtype=jnp.int32)
        query = jnp.dot(rows, w_query, preferred_element_type=jnp.float32).reshape(
            row_count, query_width // HD, HD
        )
        keyed = jnp.dot(rows, w_kv[0], preferred_element_type=jnp.float32).reshape(
            row_count, pair_width // HD, HD
        )
        valued = jnp.dot(rows, w_kv[1], preferred_element_type=jnp.float32)
        return jnp.concatenate(
            [
                rotate(query, positions).reshape(row_count, query_width),
                rotate(keyed, positions).reshape(row_count, pair_width),
                valued,
            ],
            axis=1,
        ).astype(jnp.bfloat16)

    def project_skipped(rows):
        return jnp.zeros((row_count, joined_width), jnp.bfloat16)

    joined = lax.cond(active, project_computed, project_skipped, piece)
    length = joined.shape[0]
    pair_heads = pair_width // HD
    group_size = query_width // pair_width

    def attend(joined_rows):
        query = joined_rows[:, :query_width].reshape(length, pair_heads, group_size, HD)
        keyed = joined_rows[:, query_width : query_width + pair_width].reshape(
            length, pair_heads, HD
        )
        valued = joined_rows[:, query_width + pair_width :].reshape(length, pair_heads, HD)
        scores = jnp.einsum(
            "qkgd,skd->kgqs", query, keyed, preferred_element_type=jnp.float32
        ) * HD ** (-0.5)
        row_ids = jnp.arange(length, dtype=jnp.int32)
        allowed = (segment_ids[:, None] == segment_ids[None, :]) & (
            row_ids[None, :] <= row_ids[:, None]
        )
        scores = jnp.where(allowed, scores, BLOCKED)
        probs = jax.nn.softmax(scores, axis=-1).astype(jnp.bfloat16)
        return (
            jnp.einsum("kgqs,skd->qkgd", probs, valued, preferred_element_type=jnp.float32)
            .astype(jnp.bfloat16)
            .reshape(length, query_width)
        )

    def attend_skipped(joined_rows):
        return jnp.zeros((length, query_width), jnp.bfloat16)

    mixed = lax.cond(active, attend, attend_skipped, joined)
    count = state.shape[0] * lax.axis_size("mp")

    def out_computed(values):
        return jnp.dot(values, w_out, preferred_element_type=jnp.float32)

    def out_skipped(values):
        return jnp.zeros((count, model_width), jnp.float32)

    summed = lax.psum_scatter(
        lax.cond(active, out_computed, out_skipped, mixed).astype(jnp.bfloat16),
        "mp",
        scatter_dimension=0,
        tiled=True,
    ).astype(jnp.float32)
    updated = (state.astype(jnp.float32) + summed).astype(jnp.bfloat16)
    return jnp.where(active, updated, state)


def shards(
    text,
    patches,
    segments,
    loss_mask,
    tile_batch,
    tile_offset,
    attn_gain,
    w_query,
    w_kv,
    w_out,
    vis_gain,
    vis_bias,
    v_qkv,
    v_out,
    v_up,
    v_down,
    v_proj,
):
    sections = lax.axis_size("section")
    section_at = lax.axis_index("section")
    part_at = lax.axis_index("mp")
    qkv_full, out_full, up_full, down_full, proj_full = one_gather(
        (v_qkv, v_out, v_up, v_down, v_proj), SECTION_DP, (1, 1, 0, 1, 0)
    )
    embedded = encode_tiles(
        patches, vis_gain, vis_bias, qkv_full, out_full, up_full, down_full, proj_full
    )
    length = segments.shape[2]
    tiles_here = embedded.shape[0] // POOL
    batch_all = tile_batch[0]
    offset_all = tile_offset[0]
    own_batch = lax.dynamic_slice_in_dim(batch_all, section_at * tiles_here, tiles_here, 0)
    capacity = tiles_here // 2
    block_rows = capacity * POOL
    local_ids = jnp.arange(tiles_here, dtype=jnp.int32)
    local_same = (own_batch[:, None] == own_batch[None, :]) & (
        local_ids[None, :] < local_ids[:, None]
    )
    local_rank = jnp.sum(local_same.astype(jnp.int32), axis=1)
    send_rows = jnp.arange(sections * block_rows, dtype=jnp.int32)
    send_target = send_rows // block_rows
    send_rank = send_rows % block_rows // POOL
    send_match = (own_batch[None, :] == send_target[:, None]) & (
        local_rank[None, :] == send_rank[:, None]
    )
    own_rows = jnp.arange(tiles_here * POOL, dtype=jnp.int32)
    send_pick = jnp.repeat(send_match, POOL, axis=1) & (
        (own_rows % POOL)[None, :] == (send_rows % POOL)[:, None]
    )
    blocks = jnp.dot(
        send_pick.astype(jnp.bfloat16), embedded, preferred_element_type=jnp.float32
    ).astype(jnp.bfloat16)
    arrived = lax.all_to_all(blocks, "section", split_axis=0, concat_axis=0, tiled=True)
    tile_ids = jnp.arange(batch_all.shape[0], dtype=jnp.int32)
    source_ids = tile_ids // tiles_here
    tile_same = (
        (batch_all[:, None] == batch_all[None, :])
        & (source_ids[:, None] == source_ids[None, :])
        & (tile_ids[None, :] < tile_ids[:, None])
    )
    tile_rank = jnp.sum(tile_same.astype(jnp.int32), axis=1)
    slot_rows = jnp.arange(sections * block_rows, dtype=jnp.int32)
    slot_source = slot_rows // block_rows
    slot_rank = slot_rows % block_rows // POOL
    match = (
        (batch_all[None, :] == section_at)
        & (source_ids[None, :] == slot_source[:, None])
        & (tile_rank[None, :] == slot_rank[:, None])
    )
    slot_place = jnp.sum(match.astype(jnp.int32) * offset_all[None, :], axis=1) + slot_rows % POOL
    slot_valid = jnp.any(match, axis=1)
    places = jnp.arange(length, dtype=jnp.int32)
    picker = ((places[:, None] == slot_place[None, :]) & slot_valid[None, :]).astype(jnp.bfloat16)
    image_cols = jnp.dot(picker, arrived, preferred_element_type=jnp.float32).astype(jnp.bfloat16)
    image_rows = lax.all_to_all(image_cols, "mp", split_axis=0, concat_axis=1, tiled=True)
    shard_rows = image_rows.shape[0]
    positions = part_at * shard_rows + jnp.arange(shard_rows, dtype=jnp.int32)
    covered = jnp.any(
        (batch_all[None, :] == section_at)
        & (positions[:, None] >= offset_all[None, :])
        & (positions[:, None] < offset_all[None, :] + POOL),
        axis=1,
    )
    start_state = jnp.where(covered[:, None], image_rows, text[0])
    gain_here = attn_gain[0]
    query_here = w_query[0]
    pair_here = w_kv[0]
    out_here = w_out[0]
    state = start_state
    segment_ids = segments[0, 0]
    for tick_index in range(2 * sections):
        if tick_index < 2 * sections - 1:
            micro_at = jnp.mod(section_at - tick_index, sections)
            begin_at = jnp.mod(sections - micro_at, sections)
            active = (tick_index >= begin_at) & (tick_index < begin_at + sections)
            state = decoder_layer(
                active, state, segment_ids, gain_here, query_here, pair_here, out_here
            )
        state, segment_ids = shifted((state, segment_ids), "section", 1)
    totals = over_axes(jnp.sum(loss_mask), SECTION_DP_MP)
    scaling = float(sections * lax.axis_size(DP) * length)
    token_weight = loss_mask.astype(jnp.float32) * scaling / totals.astype(jnp.float32)
    return (state[None], token_weight)


def solution(mesh):
    split = Mesh(
        mesh.devices.reshape(mesh.shape["section"], 4, 2, mesh.shape["mp"]),
        ("section", "dp_0", "dp_1", "mp"),
    )
    return jax.shard_map(
        shards,
        mesh=split,
        in_specs=(
            P("section", DP_MP, None),
            P(SECTION_DP, None),
            P("section", DP, None),
            P("section", DP_MP),
            P(DP, None),
            P(DP, None),
            P("section", None),
            P("section", None, "mp"),
            P("section", None, None, "mp"),
            P("section", "mp", None),
            P(),
            P(),
            P(None, SECTION_DP, "mp"),
            P("mp", SECTION_DP),
            P(SECTION_DP, "mp"),
            P("mp", SECTION_DP),
            P(SECTION_DP, "mp"),
        ),
        out_specs=(P("section", DP_MP, None), P("section", DP_MP)),
        check_vma=False,
    )
```

profile of v0, /device:TPU:0, one launch (start us, length us, event | category | flops | bytes accessed | tf_op | source)
XLA Modules:
  0.0 1386.7 jit_solution(4361427265575410445)
XLA Ops:
  16.4 67.2 %all-gather.24.cloned.1.call-done = bf16[7340032]{0:T(1024)(128)(2,1)} async-done(((bf16[229376]{0:T(1024)(128)(2,1)}), bf16[7340032]{0:T(1024)(128)(2,1)}) %all-gather.24.cloned.1.call-update) | async-done | bytes 14680080 | tf_op jit(solution)/shard_map/all_gather | solution.py:41
  83.6 13.2 reshape.1320
  123.5 8.0 reshape.1316
  131.4 8.2 copy.206
  141.9 27.2 %all-to-all-done = bf16[4,512,1024]{2,1,0:T(8,128)(2,1)} async-done(((bf16[4,512,1024]{2,1,0:T(8,128)(2,1)}), bf16[4,512,1024]{2,1,0:T(8,128)(2,1)}, u32[]{:S(2)}, u32[]{:S(2)}) %all-to-all-start) | async-done | bytes 4194336 | tf_op jit(solution)/shard_map/all_to_all | solution.py:25
  173.4 8.5 convolution_convert_fusion.8
  190.6 7.2 slice.282
  197.8 9.0 reshape_reshape.7
  206.7 31.9 %all-to-all-done.1 = bf16[4,512,1024]{2,1,0:T(8,128)(2,1)} async-done(((bf16[4,512,1024]{2,1,0:T(8,128)(2,1)}), bf16[4,512,1024]{2,1,0:T(8,128)(2,1)}, u32[]{:S(2)}, u32[]{:S(2)}) %all-to-all-start.1) | async-done | bytes 4194336 | tf_op jit(solution)/shard_map/all_to_all | solution.py:25
  254.5 8.0 all-to-all-done.2
  270.0 10.9 all-to-all-done.3
  287.0 45.9 %all-gather.10.cloned.1.call-done = bf16[512,4096]{1,0:T(8,128)(2,1)} async-done(((bf16[128,4096]{1,0:T(8,128)(2,1)}), bf16[512,4096]{1,0:T(8,128)(2,1)}) %all-gather.10.cloned.1.call-update) | async-done | bytes 4194320 | tf_op jit(solution)/shard_map/all_gather | solution.py:144
  333.0 10.3 conditional.21
  343.3 10.4 conditional.22
  353.7 6.7 conditional.23
  360.7 44.5 %reduce-scatter.8.cloned.1.call-done = bf16[128,4096]{1,0:T(8,128)(2,1)} async-done(((bf16[512,4096]{1,0:T(8,128)(2,1)}), bf16[128,4096]{1,0:T(8,128)(2,1)}) %reduce-scatter.8.cloned.1.call-update) | async-done | bytes 1048592 | tf_op jit(solution)/shard_map/reduce_scatter | solution.py:206
  408.9 24.5 %collective-permute-done = bf16[128,4096]{1,0:T(8,128)(2,1)S(1)} collective-permute-done((bf16[128,4096]{1,0:T(8,128)(2,1)S(1)}, bf16[128,4096]{1,0:T(8,128)(2,1)S(1)}, u32[]{:S(2)}, u32[]{:S(2)}) %collective-permute-start) | collective-permute-done | bytes 1048608 | tf_op jit(solution)/shard_map/ppermute | solution.py:52
  435.5 46.4 %all-gather.12.cloned.1.call-done = bf16[512,4096]{1,0:T(8,128)(2,1)} async-done(((bf16[128,4096]{1,0:T(8,128)(2,1)}), bf16[512,4096]{1,0:T(8,128)(2,1)}) %all-gather.12.cloned.1.call-update) | async-done | bytes 4194320 | tf_op jit(solution)/shard_map/all_gather | solution.py:144
  481.9 10.1 conditional.24
  492.1 10.4 conditional.25
  502.5 7.1 conditional.26
  502.9 6.7 fusion.357
  509.7 45.7 %reduce-scatter.10.cloned.1.call-done = bf16[128,4096]{1,0:T(8,128)(2,1)} async-done(((bf16[512,4096]{1,0:T(8,128)(2,1)}), bf16[128,4096]{1,0:T(8,128)(2,1)}) %reduce-scatter.10.cloned.1.call-update) | async-done | bytes 1048592 | tf_op jit(solution)/shard_map/reduce_scatter | solution.py:206
  558.5 24.5 %collective-permute-done.2 = bf16[128,4096]{1,0:T(8,128)(2,1)S(1)} collective-permute-done((bf16[128,4096]{1,0:T(8,128)(2,1)S(1)}, bf16[128,4096]{1,0:T(8,128)(2,1)S(1)}, u32[]{:S(2)}, u32[]{:S(2)}) %collective-permute-start.2) | collective-permute-done | bytes 1048608 | tf_op jit(solution)/shard_map/ppermute | solution.py:52
  585.1 46.4 %all-gather.14.cloned.1.call-done = bf16[512,4096]{1,0:T(8,128)(2,1)} async-done(((bf16[128,4096]{1,0:T(8,128)(2,1)}), bf16[512,4096]{1,0:T(8,128)(2,1)}) %all-gather.14.cloned.1.call-update) | async-done | bytes 4194320 | tf_op jit(solution)/shard_map/all_gather | solution.py:144
  631.5 10.1 conditional.27
  641.6 10.6 conditional.28
  652.2 6.7 conditional.29
  659.0 47.3 %reduce-scatter.12.cloned.1.call-done = bf16[128,4096]{1,0:T(8,128)(2,1)} async-done(((bf16[512,4096]{1,0:T(8,128)(2,1)}), bf16[128,4096]{1,0:T(8,128)(2,1)}) %reduce-scatter.12.cloned.1.call-update) | async-done | bytes 1048592 | tf_op jit(solution)/shard_map/reduce_scatter | solution.py:206
  709.4 24.5 %collective-permute-done.4 = bf16[128,4096]{1,0:T(8,128)(2,1)S(1)} collective-permute-done((bf16[128,4096]{1,0:T(8,128)(2,1)S(1)}, bf16[128,4096]{1,0:T(8,128)(2,1)S(1)}, u32[]{:S(2)}, u32[]{:S(2)}) %collective-permute-start.4) | collective-permute-done | bytes 1048608 | tf_op jit(solution)/shard_map/ppermute | solution.py:52
  736.0 46.4 %all-gather.16.cloned.1.call-done = bf16[512,4096]{1,0:T(8,128)(2,1)} async-done(((bf16[128,4096]{1,0:T(8,128)(2,1)}), bf16[512,4096]{1,0:T(8,128)(2,1)}) %all-gather.16.cloned.1.call-update) | async-done | bytes 4194320 | tf_op jit(solution)/shard_map/all_gather | solution.py:144
  782.4 10.4 conditional.30
  792.8 10.5 conditional.31
  803.3 6.7 conditional.32
  810.4 46.8 %reduce-scatter.14.cloned.1.call-done = bf16[128,4096]{1,0:T(8,128)(2,1)} async-done(((bf16[512,4096]{1,0:T(8,128)(2,1)}), bf16[128,4096]{1,0:T(8,128)(2,1)}) %reduce-scatter.14.cloned.1.call-update) | async-done | bytes 1048592 | tf_op jit(solution)/shard_map/reduce_scatter | solution.py:206
  860.5 24.5 %collective-permute-done.6 = bf16[128,4096]{1,0:T(8,128)(2,1)S(1)} collective-permute-done((bf16[128,4096]{1,0:T(8,128)(2,1)S(1)}, bf16[128,4096]{1,0:T(8,128)(2,1)S(1)}, u32[]{:S(2)}, u32[]{:S(2)}) %collective-permute-start.6) | collective-permute-done | bytes 1048608 | tf_op jit(solution)/shard_map/ppermute | solution.py:52
  887.0 46.4 %all-gather.18.cloned.1.call-done = bf16[512,4096]{1,0:T(8,128)(2,1)} async-done(((bf16[128,4096]{1,0:T(8,128)(2,1)}), bf16[512,4096]{1,0:T(8,128)(2,1)}) %all-gather.18.cloned.1.call-update) | async-done | bytes 4194320 | tf_op jit(solution)/shard_map/all_gather | solution.py:144
  937.9 70.3 %reduce-scatter.16.cloned.1.call-done = bf16[128,4096]{1,0:T(8,128)(2,1)} async-done(((bf16[512,4096]{1,0:T(8,128)(2,1)}), bf16[128,4096]{1,0:T(8,128)(2,1)}) %reduce-scatter.16.cloned.1.call-update) | async-done | bytes 1048592 | tf_op jit(solution)/shard_map/reduce_scatter | solution.py:206
  1011.4 24.5 %collective-permute-done.8 = bf16[128,4096]{1,0:T(8,128)(2,1)S(1)} collective-permute-done((bf16[128,4096]{1,0:T(8,128)(2,1)S(1)}, bf16[128,4096]{1,0:T(8,128)(2,1)S(1)}, u32[]{:S(2)}, u32[]{:S(2)}) %collective-permute-start.8) | collective-permute-done | bytes 1048608 | tf_op jit(solution)/shard_map/ppermute | solution.py:52
  1038.0 46.4 %all-gather.20.cloned.1.call-done = bf16[512,4096]{1,0:T(8,128)(2,1)} async-done(((bf16[128,4096]{1,0:T(8,128)(2,1)}), bf16[512,4096]{1,0:T(8,128)(2,1)}) %all-gather.20.cloned.1.call-update) | async-done | bytes 4194320 | tf_op jit(solution)/shard_map/all_gather | solution.py:144
  1089.0 70.3 %reduce-scatter.18.cloned.1.call-done = bf16[128,4096]{1,0:T(8,128)(2,1)} async-done(((bf16[512,4096]{1,0:T(8,128)(2,1)}), bf16[128,4096]{1,0:T(8,128)(2,1)}) %reduce-scatter.18.cloned.1.call-update) | async-done | bytes 1048592 | tf_op jit(solution)/shard_map/reduce_scatter | solution.py:206
  1162.4 24.5 %collective-permute-done.10 = bf16[128,4096]{1,0:T(8,128)(2,1)S(1)} collective-permute-done((bf16[128,4096]{1,0:T(8,128)(2,1)S(1)}, bf16[128,4096]{1,0:T(8,128)(2,1)S(1)}, u32[]{:S(2)}, u32[]{:S(2)}) %collective-permute-start.10) | collective-permute-done | bytes 1048608 | tf_op jit(solution)/shard_map/ppermute | solution.py:52
  1189.0 46.4 %all-gather.22.cloned.1.call-done = bf16[512,4096]{1,0:T(8,128)(2,1)} async-done(((bf16[128,4096]{1,0:T(8,128)(2,1)}), bf16[512,4096]{1,0:T(8,128)(2,1)}) %all-gather.22.cloned.1.call-update) | async-done | bytes 4194320 | tf_op jit(solution)/shard_map/all_gather | solution.py:144
  1238.3 65.9 %reduce-scatter.20.cloned.1.call-done = bf16[128,4096]{1,0:T(8,128)(2,1)} async-done(((bf16[512,4096]{1,0:T(8,128)(2,1)}), bf16[128,4096]{1,0:T(8,128)(2,1)}) %reduce-scatter.20.cloned.1.call-update) | async-done | bytes 1048592 | tf_op jit(solution)/shard_map/reduce_scatter | solution.py:206
  1307.4 24.5 %collective-permute-done.12 = bf16[128,4096]{1,0:T(8,128)(2,1)S(1)} collective-permute-done((bf16[128,4096]{1,0:T(8,128)(2,1)S(1)}, bf16[128,4096]{1,0:T(8,128)(2,1)S(1)}, u32[]{:S(2)}, u32[]{:S(2)}) %collective-permute-start.12) | collective-permute-done | bytes 1048608 | tf_op jit(solution)/shard_map/ppermute | solution.py:52
  1332.8 24.9 %psum.28 = s32[]{:T(128)} all-reduce(s32[]{:T(128)} %reduce_sum.242), channel_id=1, replica_groups=mesh['section'=4,'dp_0'=4,'dp_1'=2,'mp'=4] {'section'}, use_global_device_ids=true, to_apply=%region_84.85 | all-reduce | flops 1 | bytes 8 | tf_op jit(solution)/shard_map/psum | solution.py:57
  1357.7 9.5 psum.29
  1369.6 7.9 psum.31
  (294 shorter events, 246.1 us)
Async XLA Ops:
  7.2 7.3 copy-start.8
  7.2 7.7 copy-start.17
  7.2 7.7 copy-start.18
  7.2 76.4 %all-gather.24.cloned.1.call-start = ((), (), s32[]{:S(2)}) async-start(), calls=%async_computation.25 | async-start | bytes 15138816 | tf_op jit(solution)/shard_map/all_gather | solution.py:41
  114.6 54.6 %all-to-all-start = ((bf16[4,512,1024]{2,1,0:T(8,128)(2,1)}), bf16[4,512,1024]{2,1,0:T(8,128)(2,1)}, u32[]{:S(2)}, u32[]{:S(2)}) async-start(bf16[4,512,1024]{2,1,0:T(8,128)(2,1)} %broadcast_in_dim.76), calls=%async_computation | async-start | bytes 8388608 | tf_op jit(solution)/shard_map/all_to_all | solution.py:25
  131.4 8.2 copy-start.11
  184.5 5.4 copy-start.20
  184.5 54.1 %all-to-all-start.1 = ((bf16[4,512,1024]{2,1,0:T(8,128)(2,1)}), bf16[4,512,1024]{2,1,0:T(8,128)(2,1)}, u32[]{:S(2)}, u32[]{:S(2)}) async-start(bf16[4,512,1024]{2,1,0:T(8,128)(2,1)} %broadcast_in_dim.85), calls=%async_computation.1 | async-start | bytes 8388608 | tf_op jit(solution)/shard_map/all_to_all | solution.py:25
  244.6 9.8 copy-start.19
  250.2 18.1 %copy-start.9 = (bf16[1,128,4096]{2,1,0:T(8,128)(2,1)S(1)}, bf16[1,128,4096]{2,1,0:T(8,128)(2,1)}, u32[]{:S(2)}) copy-start(bf16[1,128,4096]{2,1,0:T(8,128)(2,1)} %param.59) | copy-start | bytes 3145732
  250.2 12.2 all-to-all-start.2
  263.9 21.6 %copy-start.14 = (f32[1,4096]{1,0:T(1,128)S(1)}, f32[1,4096]{1,0:T(1,128)}, u32[]{:S(2)}) copy-start(f32[1,4096]{1,0:T(1,128)} %param.65) | copy-start | bytes 49156
  263.9 17.1 %all-to-all-start.3 = ((bf16[4,128,1024]{2,1,0:T(8,128)(2,1)}), bf16[4,128,1024]{2,1,0:T(8,128)(2,1)}, u32[]{:S(2)}, u32[]{:S(2)}) async-start(bf16[4,128,1024]{2,1,0:T(8,128)(2,1)} %bitcast.135), calls=%async_computation.3 | async-start | bytes 2097152 | tf_op jit(solution)/shard_map/all_to_all | solution.py:291
  268.3 64.7 %all-gather.10.cloned.1.call-start = ((), (), s32[]{:S(2)}) async-start(), calls=%async_computation.11 | async-start | bytes 5242880 | tf_op jit(solution)/shard_map/all_gather | solution.py:144
  270.0 62.9 %copy-start = (bf16[1,2,4096,128]{3,2,1,0:T(8,128)(2,1)S(1)}, bf16[1,2,4096,128]{3,2,1,0:T(8,128)(2,1)}, u32[]{:S(2)}) copy-start(bf16[1,2,4096,128]{3,2,1,0:T(8,128)(2,1)} %param.67) | copy-start | bytes 6291460
  287.0 118.2 %reduce-scatter.8.cloned.1.call-start = ((), (), s32[]{:S(2)}) async-start(), calls=%async_computation.12 | async-start | bytes 5242880 | tf_op jit(solution)/shard_map/reduce_scatter | solution.py:206
  333.0 10.3 copy-start.16
  333.1 3.9 copy-start.7
  360.4 121.5 %all-gather.12.cloned.1.call-start = ((), (), s32[]{:S(2)}) async-start(), calls=%async_computation.13 | async-start | bytes 5242880 | tf_op jit(solution)/shard_map/all_gather | solution.py:144
  407.3 26.1 %collective-permute-start = (bf16[128,4096]{1,0:T(8,128)(2,1)S(1)}, bf16[128,4096]{1,0:T(8,128)(2,1)S(1)}, u32[]{:S(2)}, u32[]{:S(2)}) collective-permute-start(bf16[128,4096]{1,0:T(8,128)(2,1)S(1)} %fusion.241), channel_id=1, source_target_pairs={{0,32},{32,64},{64,96},{96,0},{1,33},{33,65},{65,97},{97,1},{2,34}... | collective-permute-start | bytes 3145736 | tf_op jit(solution)/shard_map/ppermute | solution.py:52
  435.1 120.3 %reduce-scatter.10.cloned.1.call-start = ((), (), s32[]{:S(2)}) async-start(), calls=%async_computation.14 | async-start | bytes 5242880 | tf_op jit(solution)/shard_map/reduce_scatter | solution.py:206
  435.1 57.0 %collective-permute-start.1 = (s32[512]{0:T(512)S(1)}, s32[512]{0:T(512)S(1)}, u32[]{:S(2)}, u32[]{:S(2)}) collective-permute-start(s32[512]{0:T(512)S(1)} %bitcast.536), channel_id=1, source_target_pairs={{0,32},{32,64},{64,96},{96,0},{1,33},{33,65},{65,97},{97,1},{2,34}... | collective-permute-start | bytes 6152 | tf_op jit(solution)/shard_map/ppermute | solution.py:52
  481.9 3.9 copy-start.2
  509.6 121.9 %all-gather.14.cloned.1.call-start = ((), (), s32[]{:S(2)}) async-start(), calls=%async_computation.15 | async-start | bytes 5242880 | tf_op jit(solution)/shard_map/all_gather | solution.py:144
  556.9 26.1 %collective-permute-start.2 = (bf16[128,4096]{1,0:T(8,128)(2,1)S(1)}, bf16[128,4096]{1,0:T(8,128)(2,1)S(1)}, u32[]{:S(2)}, u32[]{:S(2)}) collective-permute-start(bf16[128,4096]{1,0:T(8,128)(2,1)S(1)} %fusion.240), channel_id=1, source_target_pairs={{0,32},{32,64},{64,96},{96,0},{1,33},{33,65},{65,97},{97,1},{2,34}... | collective-permute-start | bytes 3145736 | tf_op jit(solution)/shard_map/ppermute | solution.py:52
  584.6 121.6 %reduce-scatter.12.cloned.1.call-start = ((), (), s32[]{:S(2)}) async-start(), calls=%async_computation.16 | async-start | bytes 5242880 | tf_op jit(solution)/shard_map/reduce_scatter | solution.py:206
  584.7 56.9 %collective-permute-start.3 = (s32[512]{0:T(512)S(1)}, s32[512]{0:T(512)S(1)}, u32[]{:S(2)}, u32[]{:S(2)}) collective-permute-start(s32[512]{0:T(512)S(1)} %collective-permute-done.1), channel_id=1, source_target_pairs={{0,32},{32,64},{64,96},{96,0},{1,33},{33,65},{65,97},{97,1},{2,34}... | collective-permute-start | bytes 6152 | tf_op jit(solution)/shard_map/ppermute | solution.py:52
  631.5 3.9 copy-start.3
  659.0 123.4 %all-gather.16.cloned.1.call-start = ((), (), s32[]{:S(2)}) async-start(), calls=%async_computation.17 | async-start | bytes 5242880 | tf_op jit(solution)/shard_map/all_gather | solution.py:144
  707.8 26.1 %collective-permute-start.4 = (bf16[128,4096]{1,0:T(8,128)(2,1)S(1)}, bf16[128,4096]{1,0:T(8,128)(2,1)S(1)}, u32[]{:S(2)}, u32[]{:S(2)}) collective-permute-start(bf16[128,4096]{1,0:T(8,128)(2,1)S(1)} %fusion.239), channel_id=1, source_target_pairs={{0,32},{32,64},{64,96},{96,0},{1,33},{33,65},{65,97},{97,1},{2,34}... | collective-permute-start | bytes 3145736 | tf_op jit(solution)/shard_map/ppermute | solution.py:52
  735.6 121.7 %reduce-scatter.14.cloned.1.call-start = ((), (), s32[]{:S(2)}) async-start(), calls=%async_computation.18 | async-start | bytes 5242880 | tf_op jit(solution)/shard_map/reduce_scatter | solution.py:206
  735.6 57.2 %collective-permute-start.5 = (s32[512]{0:T(512)S(1)}, s32[512]{0:T(512)S(1)}, u32[]{:S(2)}, u32[]{:S(2)}) collective-permute-start(s32[512]{0:T(512)S(1)} %collective-permute-done.3), channel_id=1, source_target_pairs={{0,32},{32,64},{64,96},{96,0},{1,33},{33,65},{65,97},{97,1},{2,34}... | collective-permute-start | bytes 6152 | tf_op jit(solution)/shard_map/ppermute | solution.py:52
  782.6 3.9 copy-start.5
  810.0 123.4 %all-gather.18.cloned.1.call-start = ((), (), s32[]{:S(2)}) async-start(), calls=%async_computation.19 | async-start | bytes 5242880 | tf_op jit(solution)/shard_map/all_gather | solution.py:144
  858.8 26.1 %collective-permute-start.6 = (bf16[128,4096]{1,0:T(8,128)(2,1)S(1)}, bf16[128,4096]{1,0:T(8,128)(2,1)S(1)}, u32[]{:S(2)}, u32[]{:S(2)}) collective-permute-start(bf16[128,4096]{1,0:T(8,128)(2,1)S(1)} %fusion.238), channel_id=1, source_target_pairs={{0,32},{32,64},{64,96},{96,0},{1,33},{33,65},{65,97},{97,1},{2,34}... | collective-permute-start | bytes 3145736 | tf_op jit(solution)/shard_map/ppermute | solution.py:52
  886.6 121.7 %reduce-scatter.16.cloned.1.call-start = ((), (), s32[]{:S(2)}) async-start(), calls=%async_computation.20 | async-start | bytes 5242880 | tf_op jit(solution)/shard_map/reduce_scatter | solution.py:206
  886.6 47.7 %collective-permute-start.7 = (s32[512]{0:T(512)S(1)}, s32[512]{0:T(512)S(1)}, u32[]{:S(2)}, u32[]{:S(2)}) collective-permute-start(s32[512]{0:T(512)S(1)} %collective-permute-done.5), channel_id=1, source_target_pairs={{0,32},{32,64},{64,96},{96,0},{1,33},{33,65},{65,97},{97,1},{2,34}... | collective-permute-start | bytes 6152 | tf_op jit(solution)/shard_map/ppermute | solution.py:52
  937.9 146.5 %all-gather.20.cloned.1.call-start = ((), (), s32[]{:S(2)}) async-start(), calls=%async_computation.21 | async-start | bytes 5242880 | tf_op jit(solution)/shard_map/all_gather | solution.py:144
  1009.8 26.1 %collective-permute-start.8 = (bf16[128,4096]{1,0:T(8,128)(2,1)S(1)}, bf16[128,4096]{1,0:T(8,128)(2,1)S(1)}, u32[]{:S(2)}, u32[]{:S(2)}) collective-permute-start(bf16[128,4096]{1,0:T(8,128)(2,1)S(1)} %fusion.237), channel_id=1, source_target_pairs={{0,32},{32,64},{64,96},{96,0},{1,33},{33,65},{65,97},{97,1},{2,34}... | collective-permute-start | bytes 3145736 | tf_op jit(solution)/shard_map/ppermute | solution.py:52
  1037.6 121.7 %reduce-scatter.18.cloned.1.call-start = ((), (), s32[]{:S(2)}) async-start(), calls=%async_computation.22 | async-start | bytes 5242880 | tf_op jit(solution)/shard_map/reduce_scatter | solution.py:206
  1037.6 47.7 %collective-permute-start.9 = (s32[512]{0:T(512)S(1)}, s32[512]{0:T(512)S(1)}, u32[]{:S(2)}, u32[]{:S(2)}) collective-permute-start(s32[512]{0:T(512)S(1)} %collective-permute-done.7), channel_id=1, source_target_pairs={{0,32},{32,64},{64,96},{96,0},{1,33},{33,65},{65,97},{97,1},{2,34}... | collective-permute-start | bytes 6152 | tf_op jit(solution)/shard_map/ppermute | solution.py:52
  1088.9 146.5 %all-gather.22.cloned.1.call-start = ((), (), s32[]{:S(2)}) async-start(), calls=%async_computation.23 | async-start | bytes 5242880 | tf_op jit(solution)/shard_map/all_gather | solution.py:144
  1160.8 26.1 %collective-permute-start.10 = (bf16[128,4096]{1,0:T(8,128)(2,1)S(1)}, bf16[128,4096]{1,0:T(8,128)(2,1)S(1)}, u32[]{:S(2)}, u32[]{:S(2)}) collective-permute-start(bf16[128,4096]{1,0:T(8,128)(2,1)S(1)} %fusion.236), channel_id=1, source_target_pairs={{0,32},{32,64},{64,96},{96,0},{1,33},{33,65},{65,97},{97,1},{2,34}... | collective-permute-start | bytes 3145736 | tf_op jit(solution)/shard_map/ppermute | solution.py:52
  1188.5 115.7 %reduce-scatter.20.cloned.1.call-start = ((), (), s32[]{:S(2)}) async-start(), calls=%async_computation.24 | async-start | bytes 5242880 | tf_op jit(solution)/shard_map/reduce_scatter | solution.py:206
  1188.6 47.1 %collective-permute-start.11 = (s32[512]{0:T(512)S(1)}, s32[512]{0:T(512)S(1)}, u32[]{:S(2)}, u32[]{:S(2)}) collective-permute-start(s32[512]{0:T(512)S(1)} %collective-permute-done.9), channel_id=1, source_target_pairs={{0,32},{32,64},{64,96},{96,0},{1,33},{33,65},{65,97},{97,1},{2,34}... | collective-permute-start | bytes 6152 | tf_op jit(solution)/shard_map/ppermute | solution.py:52
  1238.3 93.9 %copy-start.28 = (s32[1,128]{1,0:T(1,128)S(1)}, s32[1,128]{1,0:T(1,128)}, u32[]{:S(2)}) copy-start(s32[1,128]{1,0:T(1,128)} %param.62) | copy-start | bytes 1540
  1305.7 26.1 %collective-permute-start.12 = (bf16[128,4096]{1,0:T(8,128)(2,1)S(1)}, bf16[128,4096]{1,0:T(8,128)(2,1)S(1)}, u32[]{:S(2)}, u32[]{:S(2)}) collective-permute-start(bf16[128,4096]{1,0:T(8,128)(2,1)S(1)} %fusion.235), channel_id=1, source_target_pairs={{0,32},{32,64},{64,96},{96,0},{1,33},{33,65},{65,97},{97,1},{2,34}... | collective-permute-start | bytes 3145736 | tf_op jit(solution)/shard_map/ppermute | solution.py:52
  1331.9 46.9 %collective-permute-start.13 = (bf16[128,4096]{1,0:T(8,128)(2,1)S(1)}, bf16[128,4096]{1,0:T(8,128)(2,1)S(1)}, u32[]{:S(2)}, u32[]{:S(2)}) collective-permute-start(bf16[128,4096]{1,0:T(8,128)(2,1)S(1)} %collective-permute-done.12), channel_id=1, source_target_pairs={{0,32},{32,64},{64,96},{96,0},{1,33},{33,65},{65,97},{97,1},{2,34}... | collective-permute-start | bytes 3145736 | tf_op jit(solution)/shard_map/ppermute | solution.py:52
  (10 other events, 18.6 us)
Sparse Core Ops, SparseCore 0:
  13.2 70.3 all-gather.23
  287.1 45.8 all-gather.9
  360.6 44.5 reduce-scatter.7
  435.2 46.6 all-gather.11
  509.8 45.5 reduce-scatter.9
  584.8 46.6 all-gather.13
  659.1 47.1 reduce-scatter.11
  735.7 46.6 all-gather.15
  810.1 47.1 reduce-scatter.13
  886.7 46.6 all-gather.17
  938.0 70.2 reduce-scatter.15
  1037.7 46.6 all-gather.19
  1089.0 70.1 reduce-scatter.17
  1188.7 46.6 all-gather.21
  1238.4 65.7 reduce-scatter.19
where the time goes:
time: 1400 us; the launch traced here: 1390 us
  waiting for transfers between devices  1030 us (74%)
  local copies, waits for them, and re-layouts  106 us (8%)
  matrix products  101 us (7%)
  other arithmetic  51.4 us (4%)
  blocking collectives  44.8 us (3%)
  starting transfers between devices  34.2 us (2%)
  between operations  15.6 us (1%)
    reduce_scatter x7, waiting for transfers between devices, decoder_layer(): lax.psum_scatter(lax.cond(active, out_computed, out_skipped, mixed).astyp...  391 us
    all_gather x7, waiting for transfers between devices, decoder_layer(): piece = lax.all_gather(normed, 'mp', axis=0, tiled=True)  324 us
    ppermute x14, waiting for transfers between devices, shifted(): return lax.ppermute(value, axis, pairs)  172 us
    all_gather x1, waiting for transfers between devices, one_gather(): lines, at, done = (lax.all_gather(flat, axis), 0, [])  67.2 us
    all_to_all x2, waiting for transfers between devices, copy_for_each(): return lax.all_to_all(copies, axis, split_axis=0, concat_axis=0, tiled=True)  59.1 us
    psum x4, blocking collectives, over_axes(): array = lax.psum(array, axis)  44.8 us
  transfers between devices with their start and end apart: 33, of which 26 were waited for; matrix products, arithmetic and copies ran while one was open for 6% of the time, Pallas kernels for 0%

commit v1 on v0

v1 whole, which is shorter than its diff:
```python
import jax
import jax.numpy as jnp
from jax import lax
from jax.sharding import Mesh
from jax.sharding import PartitionSpec as P

HD = 128
VHD = 64
GRID = 16
PATCH = 256
POOL = 64
SECTION_DP = ("section", "dp_0", "dp_1")
SECTION_DP_MP = ("section", "dp_0", "dp_1", "mp")
DP = ("dp_0", "dp_1")
DP_MP = ("dp_0", "dp_1", "mp")


EPS = 1e-05
ROPE_BASE = 500000.0
BLOCKED = -1e30


def layer_norm(values, gain, bias):
    wide = values.astype(jnp.float32)
    center = wide - jnp.mean(wide, axis=-1, keepdims=True)
    spread = jnp.mean(center * center, axis=-1, keepdims=True)
    return (center * lax.rsqrt(spread + EPS) * gain + bias).astype(jnp.bfloat16)


def rms_norm(values, gain):
    wide = values.astype(jnp.float32)
    power = jnp.mean(wide * wide, axis=-1, keepdims=True)
    return (wide * lax.rsqrt(power + EPS) * gain).astype(jnp.bfloat16)


def pixel_shuffle(states):
    tile_count = states.shape[0] // PATCH
    side_half = GRID // 2
    width = states.shape[1]
    arranged = states.reshape(tile_count, side_half, 2, side_half, 2, width)
    return arranged.transpose(0, 1, 3, 2, 4, 5).reshape(
        tile_count * side_half * side_half, 4 * width
    )


def gathered(array, axis):
    copies = jnp.broadcast_to(array, (lax.axis_size(axis), *array.shape))
    return lax.all_to_all(copies, axis, split_axis=0, concat_axis=0, tiled=True)


def block_sum(partial_value):
    everything = gathered(partial_value.astype(jnp.bfloat16), "mp")
    return jnp.sum(everything.astype(jnp.float32), axis=0)


def transposed_dot(left, right):
    return lax.dot_general(
        left, right, (((1,), (1,)), ((), ())), preferred_element_type=jnp.float32
    )


def rope_tables(length):
    half_width = HD // 2
    freqs = ROPE_BASE ** (-2.0 * jnp.arange(half_width, dtype=jnp.float32) / HD)
    angles = jnp.arange(length, dtype=jnp.float32)[:, None] * freqs[None, :]
    cosine, sinus = jnp.cos(angles), jnp.sin(angles)
    return (
        jnp.concatenate([cosine, cosine], axis=1),
        jnp.concatenate([-sinus, sinus], axis=1),
    )


def encode_tiles(patches, vis_gain, vis_bias, small, proj_full):
    tile_count = patches.shape[0] // PATCH
    width = patches.shape[1]
    local = width // lax.axis_size("mp")
    head_count = local // VHD
    normed = layer_norm(patches, vis_gain[0], vis_bias[0])
    joined = jnp.dot(normed, small[:, : 3 * local], preferred_element_type=jnp.float32)
    joined = joined.astype(jnp.bfloat16).reshape(tile_count, PATCH, 3, head_count, VHD)
    query, keyed, valued = (joined[:, :, index] for index in range(3))
    scores = jnp.einsum("tqhd,tkhd->thqk", query, keyed, preferred_element_type=jnp.float32)
    probs = jax.nn.softmax(scores * VHD ** (-0.5), axis=-1).astype(jnp.bfloat16)
    mixed = jnp.einsum("thqk,tkhd->tqhd", probs, valued, preferred_element_type=jnp.float32)
    mixed = mixed.astype(jnp.bfloat16).reshape(tile_count * PATCH, local)
    attended = block_sum(transposed_dot(mixed, small[:, 3 * local : 4 * local]))
    residual = (patches.astype(jnp.float32) + attended).astype(jnp.bfloat16)
    normed_two = layer_norm(residual, vis_gain[1], vis_bias[1])
    hidden = small.shape[1] // 2 - 2 * local
    up = small[:, 4 * local : 4 * local + hidden]
    down = small[:, 4 * local + hidden :]
    inner = jax.nn.gelu(
        jnp.dot(normed_two, up, preferred_element_type=jnp.float32), approximate=False
    ).astype(jnp.bfloat16)
    fed = block_sum(transposed_dot(inner, down))
    states = (residual.astype(jnp.float32) + fed).astype(jnp.bfloat16)
    return jnp.dot(pixel_shuffle(states), proj_full, preferred_element_type=jnp.float32).astype(
        jnp.bfloat16
    )


def decoder_layer(state, allowed, cosine, sinus, w_joined, w_out):
    blocks = gathered(state, "mp")
    count, length, block_width = blocks.shape
    query_width = w_out.shape[0] // count
    rows = jnp.moveaxis(blocks, 0, 1).reshape(length, count * block_width)
    wide = rows.astype(jnp.float32)
    scale = lax.rsqrt(jnp.mean(wide * wide, axis=-1, keepdims=True) + EPS)
    joined = jnp.dot(rows, w_joined, preferred_element_type=jnp.float32) * scale
    heads = joined.reshape(length, joined.shape[1] // HD, HD)
    turned = heads * cosine[:, None] + jnp.roll(heads, HD // 2, axis=-1) * sinus[:, None]
    query_heads = query_width // HD
    query = turned[:, :query_heads].astype(jnp.bfloat16)
    keyed = turned[:, query_heads].astype(jnp.bfloat16)
    valued = heads[:, query_heads + 1].astype(jnp.bfloat16)
    scores = jnp.einsum("qgd,sd->gqs", query, keyed, preferred_element_type=jnp.float32)
    scores = jnp.where(allowed, scores * HD ** (-0.5), BLOCKED)
    probs = jax.nn.softmax(scores, axis=-1).astype(jnp.bfloat16)
    mixed = (
        jnp.einsum("gqs,sd->qgd", probs, valued, preferred_element_type=jnp.float32)
        .astype(jnp.bfloat16)
        .reshape(length, query_width)
    )
    parts = jnp.moveaxis(gathered(mixed, "mp"), 0, 1).reshape(length, count * query_width)
    added = jnp.dot(parts, w_out, preferred_element_type=jnp.float32)
    return (state.astype(jnp.float32) + added).astype(jnp.bfloat16)


def shards(
    text,
    patches,
    segments,
    loss_mask,
    tile_batch,
    tile_offset,
    attn_gain,
    w_query,
    w_kv,
    w_out,
    vis_gain,
    vis_bias,
    v_qkv,
    v_out,
    v_up,
    v_down,
    v_proj,
):
    sections = lax.axis_size("section")
    section_at = lax.axis_index("section")
    parts = lax.axis_size("mp")
    copies = lax.axis_size(DP)
    copy_at = lax.axis_index(DP)
    small = jnp.concatenate([v_qkv[0], v_qkv[1], v_qkv[2], v_out.T, v_up, v_down.T], axis=1)
    small = lax.all_gather(small, SECTION_DP, axis=0, tiled=True)
    proj_full = lax.all_gather(v_proj, SECTION_DP, axis=0, tiled=True)
    model_width = w_query.shape[1]
    row_share = model_width // copies
    pick = lambda array: lax.dynamic_slice_in_dim(array, copy_at * row_share, row_share, 0)
    own_rows = jnp.concatenate([pick(w_query[0]), pick(w_kv[0, 0]), pick(w_kv[0, 1])], axis=1)
    own_gain = lax.dynamic_slice_in_dim(attn_gain[0], copy_at * row_share, row_share, 0)
    own_rows = (own_rows.astype(jnp.float32) * own_gain[:, None]).astype(jnp.bfloat16)
    block_width = model_width // parts
    col_share = block_width // copies
    own_out = w_out[0].reshape(w_out.shape[1], parts, copies, col_share)
    own_out = lax.dynamic_slice_in_dim(own_out, copy_at, 1, 2)[:, :, 0]
    own_out = lax.all_to_all(
        jnp.moveaxis(own_out, 1, 0), "mp", split_axis=0, concat_axis=0, tiled=True
    )
    joined_all = lax.all_gather(own_rows, SECTION_DP).reshape(
        sections, model_width, own_rows.shape[1]
    )
    out_all = lax.all_gather(own_out, SECTION_DP).reshape(
        sections, copies, parts * w_out.shape[1], col_share
    )
    text_blocks = lax.all_to_all(
        jnp.moveaxis(text[0].reshape(text.shape[1], parts, block_width), 1, 0),
        "mp",
        split_axis=0,
        concat_axis=0,
        tiled=True,
    ).reshape(text.shape[1] * parts, block_width)
    embedded = encode_tiles(patches, vis_gain, vis_bias, small, proj_full)
    length = segments.shape[2]
    tiles_here = embedded.shape[0] // POOL
    batch_all = tile_batch[0]
    offset_all = tile_offset[0]
    own_batch = lax.dynamic_slice_in_dim(batch_all, section_at * tiles_here, tiles_here, 0)
    capacity = tiles_here // 2
    block_rows = capacity * POOL
    local_ids = jnp.arange(tiles_here, dtype=jnp.int32)
    local_same = (own_batch[:, None] == own_batch[None, :]) & (
        local_ids[None, :] < local_ids[:, None]
    )
    local_rank = jnp.sum(local_same.astype(jnp.int32), axis=1)
    send_rows = jnp.arange(sections * block_rows, dtype=jnp.int32)
    send_target = send_rows // block_rows
    send_rank = send_rows % block_rows // POOL
    send_match = (own_batch[None, :] == send_target[:, None]) & (
        local_rank[None, :] == send_rank[:, None]
    )
    own_rows = jnp.arange(tiles_here * POOL, dtype=jnp.int32)
    send_pick = jnp.repeat(send_match, POOL, axis=1) & (
        (own_rows % POOL)[None, :] == (send_rows % POOL)[:, None]
    )
    blocks = jnp.dot(
        send_pick.astype(jnp.bfloat16), embedded, preferred_element_type=jnp.float32
    ).astype(jnp.bfloat16)
    arrived = lax.all_to_all(blocks, "section", split_axis=0, concat_axis=0, tiled=True)
    tile_ids = jnp.arange(batch_all.shape[0], dtype=jnp.int32)
    source_ids = tile_ids // tiles_here
    tile_same = (
        (batch_all[:, None] == batch_all[None, :])
        & (source_ids[:, None] == source_ids[None, :])
        & (tile_ids[None, :] < tile_ids[:, None])
    )
    tile_rank = jnp.sum(tile_same.astype(jnp.int32), axis=1)
    slot_rows = jnp.arange(sections * block_rows, dtype=jnp.int32)
    slot_source = slot_rows // block_rows
    slot_rank = slot_rows % block_rows // POOL
    match = (
        (batch_all[None, :] == section_at)
        & (source_ids[None, :] == slot_source[:, None])
        & (tile_rank[None, :] == slot_rank[:, None])
    )
    slot_place = jnp.sum(match.astype(jnp.int32) * offset_all[None, :], axis=1) + slot_rows % POOL
    slot_valid = jnp.any(match, axis=1)
    places = jnp.arange(length, dtype=jnp.int32)
    picker = ((places[:, None] == slot_place[None, :]) & slot_valid[None, :]).astype(jnp.bfloat16)
    image_cols = jnp.dot(picker, arrived, preferred_element_type=jnp.float32).astype(jnp.bfloat16)
    covered = jnp.any(
        (batch_all[None, :] == section_at)
        & (places[:, None] >= offset_all[None, :])
        & (places[:, None] < offset_all[None, :] + POOL),
        axis=1,
    )
    state = jnp.where(covered[:, None], image_cols, text_blocks)
    segment_ids = segments[0, 0]
    allowed = (segment_ids[:, None] == segment_ids[None, :]) & (places[None, :] <= places[:, None])
    cosine, sinus = rope_tables(length)
    for layer in range(sections):
        w_layer = jnp.moveaxis(out_all[layer], 0, 1).reshape(out_all.shape[2], block_width)
        state = decoder_layer(state, allowed, cosine, sinus, joined_all[layer], w_layer)
    hidden = lax.all_to_all(
        state.reshape(parts, length // parts, block_width),
        "mp",
        split_axis=0,
        concat_axis=0,
        tiled=True,
    )
    hidden = jnp.moveaxis(hidden, 0, 1).reshape(length // parts, model_width)
    totals = lax.psum(jnp.sum(loss_mask), SECTION_DP_MP)
    scaling = float(sections * lax.axis_size(DP) * length)
    token_weight = loss_mask.astype(jnp.float32) * scaling / totals.astype(jnp.float32)
    return (hidden[None], token_weight)


def solution(mesh):
    split = Mesh(
        mesh.devices.reshape(mesh.shape["section"], 4, 2, mesh.shape["mp"]),
        ("section", "dp_0", "dp_1", "mp"),
    )
    return jax.shard_map(
        shards,
        mesh=split,
        in_specs=(
            P("section", DP_MP, None),
            P(SECTION_DP, None),
            P("section", DP, None),
            P("section", DP_MP),
            P(DP, None),
            P(DP, None),
            P("section", None),
            P("section", None, "mp"),
            P("section", None, None, "mp"),
            P("section", "mp", None),
            P(),
            P(),
            P(None, SECTION_DP, "mp"),
            P("mp", SECTION_DP),
            P(SECTION_DP, "mp"),
            P("mp", SECTION_DP),
            P(SECTION_DP, "mp"),
        ),
        out_specs=(P("section", DP_MP, None), P("section", DP_MP)),
        check_vma=False,
    )
```

time: 1400 us -> 708 us (0.51)
  waiting for transfers between devices: 1030 us -> 164 us
  blocking collectives: 44.8 us -> 269 us
  matrix products: 101 us -> 70.7 us
  other arithmetic: 51.4 us -> 27.5 us
    reduce_scatter x7 -> x0, waiting for transfers between devices: 391 us -> none  [decoder_layer(): lax.psum_scatter(lax.cond(active, out_computed, out_skipped, mixed).astyp...]
    all_gather x8 -> x4, waiting for transfers between devices: 391 us -> 24.4 us  [the longest x1 24.4 us: shards(): small = lax.all_gather(small, SECTION_DP, axis=0, tiled=True)]
    all_to_all x0 -> x5, blocking collectives: none -> 202 us  [the longest x4 188 us: gathered(): return lax.all_to_all(copies, axis, split_axis=0, concat_axis=0, tiled=True)]
    ppermute x14 -> x0, waiting for transfers between devices: 172 us -> none  [shifted(): return lax.ppermute(value, axis, pairs)]
    all_to_all x3 -> x8, waiting for transfers between devices: 70.1 us -> 131 us  [the longest x6 129 us: gathered(): return lax.all_to_all(copies, axis, split_axis=0, concat_axis=0, tiled=True)]
    dot_general x30 -> x20, matrix products: 91.8 us -> 61 us  [the longest x4 22.1 us: decoder_layer(): added = jnp.dot(parts, w_out, preferred_element_type=jnp.float32)]
    another operation x15 -> x3, local copies, waits for them, and re-layouts: 31.6 us -> 3.67 us  [the longest x2 2.08 us: shards(): text[0].reshape(text.shape[1], parts, block_width)]
    psum x4 -> x1, blocking collectives: 44.8 us -> 66.9 us  [shards(): totals = lax.psum(jnp.sum(loss_mask), SECTION_DP_MP)]
  transfers between devices with their start and end apart: 33 -> 13, of which waited for: 26 -> 9; matrix products, arithmetic and copies ran while one was open for 6% -> 19% of each run, Pallas kernels for 0% -> 0%
where the time goes in v1:
time: 708 us; the launch traced here: 700 us
  blocking collectives  269 us (38%)
  waiting for transfers between devices  164 us (23%)
  local copies, waits for them, and re-layouts  114 us (16%)
  matrix products  70.7 us (10%)
  starting transfers between devices  39.1 us (6%)
  other arithmetic  27.5 us (4%)
  between operations  15.7 us (2%)
    all_to_all x4, blocking collectives, gathered(): return lax.all_to_all(copies, axis, split_axis=0, concat_axis=0, tiled=True)  188 us
    all_to_all x6, waiting for transfers between devices, gathered(): return lax.all_to_all(copies, axis, split_axis=0, concat_axis=0, tiled=True)  129 us
    psum x1, blocking collectives, shards(): totals = lax.psum(jnp.sum(loss_mask), SECTION_DP_MP)  66.9 us
    all_to_all x6, starting transfers between devices, gathered(): return lax.all_to_all(copies, axis, split_axis=0, concat_axis=0, tiled=True)  27.3 us
    transpose x4, local copies, waits for them, and re-layouts, shards(): jnp.moveaxis(out_all[layer], 0, 1).reshape(out_all.shape[2], block_width)  26.2 us
    all_gather x1, waiting for transfers between devices, shards(): small = lax.all_gather(small, SECTION_DP, axis=0, tiled=True)  24.4 us
    dot_general x4, matrix products, decoder_layer(): added = jnp.dot(parts, w_out, preferred_element_type=jnp.float32)  22.1 us
    slice x1, local copies, waits for them, and re-layouts, shards(): joined_all[layer]  15.8 us
  transfers between devices with their start and end apart: 13, of which 9 were waited for; matrix products, arithmetic and copies ran while one was open for 19% of the time, Pallas kernels for 0%

profile of v1, /device:TPU:0, one launch (start us, length us, event | category | flops | bytes accessed | tf_op | source)
XLA Modules:
  0.0 699.7 jit_solution(4039534892102669239)
XLA Ops:
  17.3 6.5 copy.169
  25.3 13.9 %all_to_all.77 = bf16[4,512,128]{2,1,0:T(8,128)(2,1)} all-to-all(bf16[4,512,128]{2,1,0:T(8,128)(2,1)S(1)} %bitcast.271), channel_id=1, replica_groups=mesh['section'=4,'dp_0'=4,'dp_1'=2,'mp'=4] {'mp'}, dimensions={0} | all-to-all | bytes 1048576 | tf_op jit(solution)/shard_map/all_to_all | solution.py:166
  39.9 24.4 %all-gather.6.cloned.1.call-done = bf16[1024,3072]{1,0:T(8,128)(2,1)} async-done(((bf16[32,3072]{1,0:T(8,128)(2,1)}), bf16[1024,3072]{1,0:T(8,128)(2,1)}) %all-gather.6.cloned.1.call-update) | async-done | bytes 6291472 | tf_op jit(solution)/shard_map/all_gather | solution.py:154
  64.3 2.5 fusion.67
  72.0 2.1 fusion.228
  78.6 53.4 %all_to_all.78 = bf16[4,512,1024]{2,1,0:T(8,128)(2,1)S(1)} all-to-all(bf16[4,512,1024]{2,1,0:T(8,128)(2,1)S(1)} %broadcast_in_dim.44), channel_id=1, replica_groups=mesh['section'=4,'dp_0'=4,'dp_1'=2,'mp'=4] {'mp'}, dimensions={0} | all-to-all | bytes 8388608 | tf_op jit(solution)/shard_map/all_to_all | solution.py:48
  133.7 8.5 %fusion.64 = bf16[512,1024]{1,0:T(8,128)(2,1)S(1)} fusion(bf16[1024,3072]{1,0:T(8,128)(2,1)} %all-gather.6.cloned.1.call-done, bf16[512,1024]{1,0:T(8,128)(2,1)S(1)} %get-tuple-element.3, f32[1024]{0:T(1024)S(1)} %bitcast.283, f32[1024]{0:T(1024)S(1)} %bitcast.282, f32[512]{0:T(512)S(1)} %add_rsqrt_fusion.4, f32[512]{0:T(512)S(1)} %broadcast_multiply_fusion), kind=kOutput, calls=%fused_computation.109 | convolution fusion | flops 2185232384 | bytes 6303744 | tf_op jit(solution)/shard_map/dot_general | solution.py:57
  142.3 2.5 broadcast_in_dim.45
  144.8 5.0 all-to-all-start.1
  152.6 45.5 %all-to-all-done.1 = bf16[4,512,1024]{2,1,0:T(8,128)(2,1)} async-done(((bf16[4,512,1024]{2,1,0:T(8,128)(2,1)}), bf16[4,512,1024]{2,1,0:T(8,128)(2,1)}, u32[]{:S(2)}, u32[]{:S(2)}) %all-to-all-start.1) | async-done | bytes 4194336 | tf_op jit(solution)/shard_map/all_to_all | solution.py:48
  198.1 4.5 all-to-all-start.3
  202.7 3.4 convert_reduce_fusion
  208.7 5.9 convolution_convert_fusion.2
  216.5 3.5 all-to-all-start.2
  220.1 7.9 %all-to-all-done.2 = bf16[4,64,1024]{2,1,0:T(8,128)(2,1)S(1)} async-done(((bf16[4,64,1024]{2,1,0:T(8,128)(2,1)}), bf16[4,64,1024]{2,1,0:T(8,128)(2,1)S(1)}, u32[]{:S(2)}, u32[]{:S(2)}) %all-to-all-start.2) | async-done | bytes 524320 | tf_op jit(solution)/shard_map/all_to_all | solution.py:208
  230.3 2.2 broadcast_in_dim.46
  232.5 5.4 all-to-all-start.4
  239.3 44.1 %all-to-all-done.4 = bf16[4,512,1024]{1,2,0:T(8,128)(2,1)} async-done(((bf16[4,512,1024]{1,2,0:T(8,128)(2,1)}), bf16[4,512,1024]{1,2,0:T(8,128)(2,1)}, u32[]{:S(2)}, u32[]{:S(2)}) %all-to-all-start.4) | async-done | bytes 4194336 | tf_op jit(solution)/shard_map/all_to_all | solution.py:48
  283.4 3.3 multiply_reduce_fusion.3
  286.8 15.8 %fusion.218 = (bf16[8,512,768]{2,1,0:T(8,128)(2,1)}, bf16[8,512,768]{2,1,0:T(8,128)(2,1)}, bf16[8,512,768]{2,1,0:T(8,128)(2,1)}, bf16[8,512,768]{2,1,0:T(8,128)(2,1)S(1)}) fusion(bf16[32,512,768]{2,1,0:T(8,128)(2,1)} %all-gather.10.cloned.1.call-done), kind=kLoop, calls=%fused_computation.300 | loop fusion | bytes 50331648 | tf_op jit(solution)/shard_map/slice | solution.py:242
  302.6 5.3 convolution_multiply_fusion.3
  313.2 2.1 fusion.233
  318.2 4.4 all-to-all-start.5
  322.7 12.2 %fusion.219 = (bf16[32,512,128]{2,1,0:T(8,128)(2,1)}, bf16[32,512,128]{2,1,0:T(8,128)(2,1)}, bf16[32,512,128]{2,1,0:T(8,128)(2,1)}, bf16[32,512,128]{2,1,0:T(8,128)(2,1)}) fusion(bf16[128,512,128]{2,1,0:T(8,128)(2,1)} %all-gather.12.cloned.1.call-done), kind=kLoop, calls=%fused_computation.301 | loop fusion | bytes 33554432 | tf_op jit(solution)/shard_map/slice | solution.py:241
  334.9 6.5 copy.171
  341.4 3.5 all-to-all-done.5
  344.9 6.2 add_convert_fusion.3
  353.0 46.8 %all_to_all.79 = bf16[4,512,1024]{1,2,0:T(8,128)(2,1)S(1)} all-to-all(bf16[4,512,1024]{1,2,0:T(8,128)(2,1)S(1)} %broadcast_in_dim.52), channel_id=1, replica_groups=mesh['section'=4,'dp_0'=4,'dp_1'=2,'mp'=4] {'mp'}, dimensions={0} | all-to-all | bytes 8388608 | tf_op jit(solution)/shard_map/all_to_all | solution.py:48
  400.8 3.5 convolution_multiply_fusion.2
  409.6 2.1 fusion.234
  414.6 4.4 all-to-all-start.8
  419.0 6.6 copy.178
  425.7 13.9 %all-to-all-done.8 = bf16[4,512,512]{1,2,0:T(8,128)(2,1)} async-done(((bf16[4,512,512]{1,2,0:T(8,128)(2,1)}), bf16[4,512,512]{1,2,0:T(8,128)(2,1)}, u32[]{:S(2)}, u32[]{:S(2)}) %all-to-all-start.8) | async-done | bytes 2097184 | tf_op jit(solution)/shard_map/all_to_all | solution.py:48
  439.6 5.2 add_convert_fusion.2
  445.8 44.8 %all_to_all.80 = bf16[4,512,1024]{1,2,0:T(8,128)(2,1)S(1)} all-to-all(bf16[4,512,1024]{1,2,0:T(8,128)(2,1)S(1)} %broadcast_in_dim.54), channel_id=1, replica_groups=mesh['section'=4,'dp_0'=4,'dp_1'=2,'mp'=4] {'mp'}, dimensions={0} | all-to-all | bytes 8388608 | tf_op jit(solution)/shard_map/all_to_all | solution.py:48
  491.6 3.5 convolution_multiply_fusion.1
  505.5 4.5 all-to-all-start.10
  510.0 6.6 copy.185
  516.5 11.9 %all-to-all-done.10 = bf16[4,512,512]{1,2,0:T(8,128)(2,1)} async-done(((bf16[4,512,512]{1,2,0:T(8,128)(2,1)}), bf16[4,512,512]{1,2,0:T(8,128)(2,1)}, u32[]{:S(2)}, u32[]{:S(2)}) %all-to-all-start.10) | async-done | bytes 2097184 | tf_op jit(solution)/shard_map/all_to_all | solution.py:48
  528.5 5.2 add_convert_fusion.1
  534.6 42.8 %all_to_all.81 = bf16[4,512,1024]{1,2,0:T(8,128)(2,1)S(1)} all-to-all(bf16[4,512,1024]{1,2,0:T(8,128)(2,1)S(1)} %broadcast_in_dim.56), channel_id=1, replica_groups=mesh['section'=4,'dp_0'=4,'dp_1'=2,'mp'=4] {'mp'}, dimensions={0} | all-to-all | bytes 8388608 | tf_op jit(solution)/shard_map/all_to_all | solution.py:48
  578.4 3.5 convolution_multiply_fusion
  592.3 3.6 all-to-all-start.12
  595.9 6.5 copy.192
  602.4 9.9 %all-to-all-done.12 = bf16[4,512,512]{1,2,0:T(8,128)(2,1)S(1)} async-done(((bf16[4,512,512]{1,2,0:T(8,128)(2,1)}), bf16[4,512,512]{1,2,0:T(8,128)(2,1)S(1)}, u32[]{:S(2)}, u32[]{:S(2)}) %all-to-all-start.12) | async-done | bytes 2097184 | tf_op jit(solution)/shard_map/all_to_all | solution.py:48
  612.4 5.5 add_convert_fusion
  617.9 3.6 all-to-all-start.13
  622.2 66.9 %psum.7 = s32[]{:T(128)} all-reduce(s32[]{:T(128)} %reduce_sum.189), channel_id=1, replica_groups=mesh['section'=4,'dp_0'=4,'dp_1'=2,'mp'=4] {'section','dp_0','dp_1','mp'}, use_global_device_ids=true, to_apply=%region_26.27 | all-reduce | flops 1 | bytes 8 | tf_op jit(solution)/shard_map/psum | solution.py:251
  (164 shorter events, 81.7 us)
Async XLA Ops:
  7.2 6.1 copy-start
  7.2 57.1 %all-gather.6.cloned.1.call-start = ((), (), s32[]{:S(2)}) async-start(), calls=%async_computation.14 | async-start | bytes 6488064 | tf_op jit(solution)/shard_map/all_gather | solution.py:154
  11.8 0.7 copy-start.7
  12.5 196.2 %all-gather.8.cloned.1.call-start = ((), (), s32[]{:S(2)}) async-start(), calls=%async_computation.15 | async-start | bytes 8650752 | tf_op jit(solution)/shard_map/all_gather | solution.py:155
  13.2 273.5 %all-gather.10.cloned.1.call-start = ((), (), s32[]{:S(2)}) async-start(), calls=%async_computation.16 | async-start | bytes 25952256 | tf_op jit(solution)/shard_map/all_gather | solution.py:169
  17.3 305.5 %all-gather.12.cloned.1.call-start = ((), (), s32[]{:S(2)}) async-start(), calls=%async_computation.17 | async-start | bytes 17301504 | tf_op jit(solution)/shard_map/all_gather | solution.py:172
  23.8 15.4 %copy-start.2 = (bf16[512,1024]{1,0:T(8,128)(2,1)S(1)}, bf16[512,1024]{1,0:T(8,128)(2,1)}, u32[]{:S(2)}) copy-start(bf16[512,1024]{1,0:T(8,128)(2,1)} %param.18) | copy-start | bytes 3145732
  25.3 14.6 %copy-start.9 = (f32[2,1024]{1,0:T(2,128)S(1)}, f32[2,1024]{1,0:T(2,128)}, u32[]{:S(2)}) copy-start(f32[2,1024]{1,0:T(2,128)} %param.27) | copy-start | bytes 24580
  25.3 14.6 %copy-start.10 = (f32[2,1024]{1,0:T(2,128)S(1)}, f32[2,1024]{1,0:T(2,128)}, u32[]{:S(2)}) copy-start(f32[2,1024]{1,0:T(2,128)} %param.28) | copy-start | bytes 24580
  144.8 5.0 copy-start.3
  144.8 53.4 %all-to-all-start.1 = ((bf16[4,512,1024]{2,1,0:T(8,128)(2,1)}), bf16[4,512,1024]{2,1,0:T(8,128)(2,1)}, u32[]{:S(2)}, u32[]{:S(2)}) async-start(bf16[4,512,1024]{2,1,0:T(8,128)(2,1)} %broadcast_in_dim.45), calls=%async_computation.1 | async-start | bytes 8388608 | tf_op jit(solution)/shard_map/all_to_all | solution.py:48
  149.8 2.1 copy-start.11
  149.8 2.8 copy-start.12
  198.1 18.3 %all-to-all-start.3 = ((bf16[4,128,1024]{2,1,0:T(8,128)(2,1)}), bf16[4,128,1024]{2,1,0:T(8,128)(2,1)}, u32[]{:S(2)}, u32[]{:S(2)}) async-start(bf16[4,128,1024]{2,1,0:T(8,128)(2,1)} %bitcast.236), calls=%async_computation.3 | async-start | bytes 2097152 | tf_op jit(solution)/shard_map/all_to_all | solution.py:175
  216.5 11.5 %all-to-all-start.2 = ((bf16[4,64,1024]{2,1,0:T(8,128)(2,1)}), bf16[4,64,1024]{2,1,0:T(8,128)(2,1)S(1)}, u32[]{:S(2)}, u32[]{:S(2)}) async-start(bf16[4,64,1024]{2,1,0:T(8,128)(2,1)} %bitcast.20), calls=%async_computation.2 | async-start | bytes 1048576 | tf_op jit(solution)/shard_map/all_to_all | solution.py:208
  232.5 50.9 %all-to-all-start.4 = ((bf16[4,512,1024]{1,2,0:T(8,128)(2,1)}), bf16[4,512,1024]{1,2,0:T(8,128)(2,1)}, u32[]{:S(2)}, u32[]{:S(2)}) async-start(bf16[4,512,1024]{1,2,0:T(8,128)(2,1)} %broadcast_in_dim.46), calls=%async_computation.4 | async-start | bytes 8388608 | tf_op jit(solution)/shard_map/all_to_all | solution.py:48
  237.9 1.2 copy-start.8
  318.2 26.7 %all-to-all-start.5 = ((bf16[4,512,512]{1,2,0:T(8,128)(2,1)}), bf16[4,512,512]{1,2,0:T(8,128)(2,1)}, u32[]{:S(2)}, u32[]{:S(2)}) async-start(bf16[4,512,512]{1,2,0:T(8,128)(2,1)} %broadcast_in_dim.49), calls=%async_computation.5 | async-start | bytes 4194304 | tf_op jit(solution)/shard_map/all_to_all | solution.py:48
  352.6 48.1 %slice-start.4 = ((s8[6291456]{0:T(1024)(128)(4,1)}), s8[4194304]{0:T(1024)(128)(4,1)S(1)}, s32[]{:S(2)}) async-start(s8[6291456]{0:T(1024)(128)(4,1)} %bitcast.251), calls=%async_computation.22 | async-start | bytes 8388608
  353.0 47.8 %slice-start.5 = ((s8[6291456]{0:T(1024)(128)(4,1)}), s8[2097152]{0:T(1024)(128)(4,1)S(1)}, s32[]{:S(2)}) async-start(s8[6291456]{0:T(1024)(128)(4,1)} %bitcast.251), calls=%async_computation.23 | async-start | bytes 4194304
  414.6 25.0 %all-to-all-start.8 = ((bf16[4,512,512]{1,2,0:T(8,128)(2,1)}), bf16[4,512,512]{1,2,0:T(8,128)(2,1)}, u32[]{:S(2)}, u32[]{:S(2)}) async-start(bf16[4,512,512]{1,2,0:T(8,128)(2,1)} %broadcast_in_dim.53), calls=%async_computation.8 | async-start | bytes 4194304 | tf_op jit(solution)/shard_map/all_to_all | solution.py:48
  419.0 20.5 %copy-start.4 = (bf16[512,1024]{1,0:T(8,128)(2,1)S(1)}, bf16[512,1024]{1,0:T(8,128)(2,1)}, u32[]{:S(2)}) copy-start(bf16[512,1024]{1,0:T(8,128)(2,1)} %add_convert_fusion.3) | copy-start | bytes 3145732
  444.8 1.0 copy-start.5
  445.4 46.2 %slice-start.2 = ((s8[6291456]{0:T(1024)(128)(4,1)}), s8[4194304]{0:T(1024)(128)(4,1)S(1)}, s32[]{:S(2)}) async-start(s8[6291456]{0:T(1024)(128)(4,1)} %bitcast.248), calls=%async_computation.20 | async-start | bytes 8388608
  445.8 45.8 %slice-start.3 = ((s8[6291456]{0:T(1024)(128)(4,1)}), s8[2097152]{0:T(1024)(128)(4,1)S(1)}, s32[]{:S(2)}) async-start(s8[6291456]{0:T(1024)(128)(4,1)} %bitcast.248), calls=%async_computation.21 | async-start | bytes 4194304
  505.5 23.0 %all-to-all-start.10 = ((bf16[4,512,512]{1,2,0:T(8,128)(2,1)}), bf16[4,512,512]{1,2,0:T(8,128)(2,1)}, u32[]{:S(2)}, u32[]{:S(2)}) async-start(bf16[4,512,512]{1,2,0:T(8,128)(2,1)} %broadcast_in_dim.55), calls=%async_computation.10 | async-start | bytes 4194304 | tf_op jit(solution)/shard_map/all_to_all | solution.py:48
  509.9 18.5 %copy-start.6 = (bf16[512,1024]{1,0:T(8,128)(2,1)S(1)}, bf16[512,1024]{1,0:T(8,128)(2,1)}, u32[]{:S(2)}) copy-start(bf16[512,1024]{1,0:T(8,128)(2,1)} %copy-done.5) | copy-start | bytes 3145732
  534.2 44.1 %slice-start = ((s8[6291456]{0:T(1024)(128)(4,1)}), s8[4194304]{0:T(1024)(128)(4,1)S(1)}, s32[]{:S(2)}) async-start(s8[6291456]{0:T(1024)(128)(4,1)} %bitcast.245), calls=%async_computation.18 | async-start | bytes 8388608
  534.6 43.8 %slice-start.1 = ((s8[6291456]{0:T(1024)(128)(4,1)}), s8[2097152]{0:T(1024)(128)(4,1)S(1)}, s32[]{:S(2)}) async-start(s8[6291456]{0:T(1024)(128)(4,1)} %bitcast.245), calls=%async_computation.19 | async-start | bytes 4194304
  592.3 20.1 %all-to-all-start.12 = ((bf16[4,512,512]{1,2,0:T(8,128)(2,1)}), bf16[4,512,512]{1,2,0:T(8,128)(2,1)S(1)}, u32[]{:S(2)}, u32[]{:S(2)}) async-start(bf16[4,512,512]{1,2,0:T(8,128)(2,1)} %broadcast_in_dim.57), calls=%async_computation.12 | async-start | bytes 4194304 | tf_op jit(solution)/shard_map/all_to_all | solution.py:48
  617.9 3.7 copy-start.13
  617.9 72.3 %all-to-all-start.13 = ((bf16[4,128,1024]{2,1,0:T(8,128)(2,1)}), bf16[4,128,1024]{2,1,0:T(8,128)(2,1)S(1)}, u32[]{:S(2)}, u32[]{:S(2)}) async-start(bf16[4,128,1024]{2,1,0:T(8,128)(2,1)} %bitcast.273), calls=%async_computation.13 | async-start | bytes 2097152 | tf_op jit(solution)/shard_map/all_to_all | solution.py:243
  690.3 2.4 copy-start.1
Sparse Core Ops, SparseCore 0:
  12.6 51.6 all-gather.5
  66.6 51.5 all-gather.7
  120.4 91.5 all-gather.9
  214.1 71.9 all-gather.11

commit v2 on v1

--- a/solution.py
+++ b/solution.py
@@ -1,6 +1,8 @@
 import jax
 import jax.numpy as jnp
 from jax import lax
+from jax.experimental import pallas as pl
+from jax.experimental.pallas import tpu as pltpu
 from jax.sharding import Mesh
 from jax.sharding import PartitionSpec as P
 
@@ -18,6 +20,7 @@
 EPS = 1e-05
 ROPE_BASE = 500000.0
 BLOCKED = -1e30
+MESH = pl.DeviceIdType.MESH
 
 
 def layer_norm(values, gain, bias):
@@ -99,31 +102,328 @@
     )
 
 
-def decoder_layer(state, allowed, cosine, sinus, w_joined, w_out):
-    blocks = gathered(state, "mp")
-    count, length, block_width = blocks.shape
-    query_width = w_out.shape[0] // count
-    rows = jnp.moveaxis(blocks, 0, 1).reshape(length, count * block_width)
-    wide = rows.astype(jnp.float32)
-    scale = lax.rsqrt(jnp.mean(wide * wide, axis=-1, keepdims=True) + EPS)
-    joined = jnp.dot(rows, w_joined, preferred_element_type=jnp.float32) * scale
-    heads = joined.reshape(length, joined.shape[1] // HD, HD)
-    turned = heads * cosine[:, None] + jnp.roll(heads, HD // 2, axis=-1) * sinus[:, None]
-    query_heads = query_width // HD
-    query = turned[:, :query_heads].astype(jnp.bfloat16)
-    keyed = turned[:, query_heads].astype(jnp.bfloat16)
-    valued = heads[:, query_heads + 1].astype(jnp.bfloat16)
-    scores = jnp.einsum("qgd,sd->gqs", query, keyed, preferred_element_type=jnp.float32)
-    scores = jnp.where(allowed, scores * HD ** (-0.5), BLOCKED)
-    probs = jax.nn.softmax(scores, axis=-1).astype(jnp.bfloat16)
-    mixed = (
-        jnp.einsum("gqs,sd->qgd", probs, valued, preferred_element_type=jnp.float32)
-        .astype(jnp.bfloat16)
-        .reshape(length, query_width)
-    )
-    parts = jnp.moveaxis(gathered(mixed, "mp"), 0, 1).reshape(length, count * query_width)
-    added = jnp.dot(parts, w_out, preferred_element_type=jnp.float32)
-    return (state.astype(jnp.float32) + added).astype(jnp.bfloat16)
+def decoder_kernel(
+    seg_col,
+    seg_row,
+    cos_ref,
+    sin_ref,
+    s0_ref,
+    w_any,
+    out_ref,
+    xbuf,
+    mbuf,
+    wjb,
+    wob,
+    acc,
+    ssq,
+    kb,
+    vb,
+    bias,
+    fin,
+    hid,
+    xs,
+    xr,
+    ms,
+    mr,
+    js,
+    os,
+    fs,
+    fr,
+):
+    parts = 4
+    layers = 4
+    copies = w_any.shape[0] // layers
+    length, block = s0_ref.shape
+    half = length // 2
+    joined = wjb.shape[2]
+    query_width = wob.shape[1] // parts
+    heads = query_width // HD
+    depth = w_any.shape[1]
+    col_share = wob.shape[2] // copies
+    token_share = length // parts
+    me = lax.axis_index("mp")
+    right, opposite, left = (lax.rem(me + step, parts) for step in (1, 2, 3))
+
+    def weight_copies(layer, par):
+        found = []
+        for d in range(copies):
+            found.append(
+                pltpu.make_async_copy(
+                    w_any.at[layer * copies + d, :, pl.ds(0, joined)],
+                    wjb.at[par, pl.ds(d * depth, depth), :],
+                    js.at[par, d],
+                )
+            )
+        for d in range(copies):
+            for part in range(parts):
+                found.append(
+                    pltpu.make_async_copy(
+                        w_any.at[
+                            layer * copies + d, :, pl.ds(joined + part * col_share, col_share)
+                        ],
+                        wob.at[par, pl.ds(part * depth, depth), pl.ds(d * col_share, col_share)],
+                        os.at[par, d * parts + part],
+                    )
+                )
+        return found[:copies], found[copies:]
+
+    def piece(buf, width, sends, recvs, par, h, kind, source, half_at, target):
+        cols = pl.ds(pl.multiple_of(source * width + half_at * (width // 2), width // 2), width // 2)
+        ref = buf.at[par, pl.ds(h * half, half), cols]
+        return pltpu.make_async_remote_copy(
+            src_ref=ref,
+            dst_ref=ref,
+            send_sem=sends.at[par, h, kind],
+            recv_sem=recvs.at[par, h, kind],
+            device_id={"mp": target},
+            device_id_type=MESH,
+        )
+
+    def sent(kind, buf, width, sends, recvs, par, h):
+        source, half_at, target = (
+            (me, 0, right),
+            (me, 1, right),
+            (me, 1, left),
+            (me, 0, left),
+            (left, 0, right),
+            (right, 1, left),
+        )[kind]
+        return piece(buf, width, sends, recvs, par, h, kind, source, half_at, target)
+
+    def landed(kind, buf, width, sends, recvs, par, h):
+        source, half_at = (
+            (left, 0),
+            (left, 1),
+            (right, 1),
+            (right, 0),
+            (opposite, 0),
+            (opposite, 1),
+        )[kind]
+        return piece(buf, width, sends, recvs, par, h, kind, source, half_at, right)
+
+    x_args = (xbuf, block, xs, xr)
+    m_args = (mbuf, query_width, ms, mr)
+
+    def forward(args, par, h):
+        landed(0, *args, par, h).wait_recv()
+        sent(4, *args, par, h).start()
+        landed(2, *args, par, h).wait_recv()
+        sent(5, *args, par, h).start()
+
+    def waits(args, par, h, kinds):
+        for kind in kinds:
+            landed(kind, *args, par, h).wait_recv()
+
+    def wait_sends(args, par, h):
+        for kind in range(6):
+            sent(kind, *args, par, h).wait_send()
+
+    def start_own(par, h):
+        for kind in (0, 2, 1, 3):
+            sent(kind, *x_args, par, h).start()
+
+    first_joined, first_out = weight_copies(0, 0)
+    for copy in first_joined + first_out:
+        copy.start()
+    barrier = pltpu.get_barrier_semaphore()
+    for target in (right, opposite, left):
+        pl.semaphore_signal(barrier, inc=1, device_id={"mp": target}, device_id_type=MESH)
+    own_cols = pl.ds(pl.multiple_of(me * block, block), block)
+    xbuf[0, :, own_cols] = s0_ref[...]
+    pl.semaphore_wait(barrier, 3)
+    for h in range(2):
+        start_own(0, h)
+
+    rows_at = lax.broadcasted_iota(jnp.int32, (length, length), 0)
+    cols_at = lax.broadcasted_iota(jnp.int32, (length, length), 1)
+    allowed = (seg_col[...] == seg_row[...]) & (cols_at <= rows_at)
+    bias[...] = jnp.where(allowed, 0.0, BLOCKED)
+
+    def project(par, h):
+        rows = pl.ds(h * half, half)
+
+        def add(source, first):
+            cols = pl.ds(pl.multiple_of(source * block, block), block)
+            values = xbuf[par, rows, cols]
+            product = jnp.dot(values, wjb[par, cols, :], preferred_element_type=jnp.float32)
+            wide = values.astype(jnp.float32)
+            wide = wide * wide
+            power = wide[:, :HD]
+            for at in range(1, block // HD):
+                power = power + wide[:, at * HD : (at + 1) * HD]
+            if first:
+                acc[:, :joined] = product
+                ssq[...] = power
+            else:
+                acc[:, :joined] += product
+                ssq[...] += power
+
+        add(me, True)
+        forward(x_args, par, h)
+        waits(x_args, par, h, (1,))
+        add(left, False)
+        waits(x_args, par, h, (3,))
+        add(right, False)
+        waits(x_args, par, h, (4, 5))
+        add(opposite, False)
+
+    def attend(par, h):
+        rows = pl.ds(h * half, half)
+        keys = half * (h + 1)
+        power = jnp.sum(ssq[...], axis=1, keepdims=True) * (1.0 / (parts * block))
+        scale = lax.rsqrt(power + EPS)
+        cosine = cos_ref[rows, :] * scale
+        sinus = sin_ref[rows, :] * scale
+
+        def turned(at):
+            values = acc[:, at * HD : (at + 1) * HD]
+            return values * cosine + pltpu.roll(values, HD // 2, 1) * sinus
+
+        kb[rows, :] = turned(heads).astype(jnp.bfloat16)
+        vb[rows, :] = (acc[:, (heads + 1) * HD : (heads + 2) * HD] * scale).astype(jnp.bfloat16)
+        for head in range(heads):
+            query = (turned(head) * HD ** (-0.5)).astype(jnp.bfloat16)
+            scores = lax.dot_general(
+                query,
+                kb[:keys, :],
+                (((1,), (1,)), ((), ())),
+                preferred_element_type=jnp.float32,
+            )
+            scores = scores + bias[rows, :keys]
+            top = jnp.max(scores, axis=1, keepdims=True)
+            probs = jnp.exp(scores - top)
+            total = jnp.sum(probs, axis=1, keepdims=True)
+            mixed = jnp.dot(
+                probs.astype(jnp.bfloat16), vb[:keys, :], preferred_element_type=jnp.float32
+            )
+            cols = pl.ds(pl.multiple_of(me * query_width + head * HD, HD), HD)
+            mbuf[par, rows, cols] = (mixed / total).astype(jnp.bfloat16)
+            if head == heads // 2 - 1:
+                sent(0, *m_args, par, h).start()
+                sent(3, *m_args, par, h).start()
+                if h == 1:
+                    forward(m_args, par, 0)
+        sent(2, *m_args, par, h).start()
+        sent(1, *m_args, par, h).start()
+
+    def leave(par, h, layer):
+        rows = pl.ds(h * half, half)
+        if h == 1:
+            forward(m_args, par, h)
+
+        def term(source):
+            cols = pl.ds(pl.multiple_of(source * query_width, query_width), query_width)
+            return jnp.dot(
+                mbuf[par, rows, cols], wob[par, cols, :], preferred_element_type=jnp.float32
+            )
+
+        acc[...] = xbuf[par, rows, own_cols].astype(jnp.float32) + term(me)
+        waits(m_args, par, h, (1,))
+        acc[...] += term(left)
+        waits(m_args, par, h, (3,))
+        acc[...] += term(right)
+        waits(m_args, par, h, (4, 5))
+        wait_sends(x_args, par, h)
+        result = (acc[...] + term(opposite)).astype(jnp.bfloat16)
+
+        @pl.when(layer < layers - 1)
+        def _():
+            xbuf[1 - par, rows, own_cols] = result
+            start_own(1 - par, h)
+
+        @pl.when(layer == layers - 1)
+        def _():
+            fin[rows, :] = result
+
+    def one_layer(layer, carry):
+        par = lax.rem(layer, 2)
+        joined_copies, out_copies = weight_copies(layer, par)
+        for copy in joined_copies:
+            copy.wait()
+
+        @pl.when(layer < layers - 1)
+        def _():
+            for copies_of in weight_copies(layer + 1, 1 - par):
+                for copy in copies_of:
+                    copy.start()
+
+        for h in range(2):
+            project(par, h)
+
+            @pl.when(layer > 0)
+            def _():
+                wait_sends(m_args, 1 - par, h)
+
+            attend(par, h)
+        for copy in out_copies:
+            copy.wait()
+        for h in range(2):
+            leave(par, h, layer)
+        return carry
+
+    lax.fori_loop(0, layers, one_layer, 0)
+    last = (layers - 1) % 2
+
+    def shared(step):
+        target = lax.rem(me + step, parts)
+        return pltpu.make_async_remote_copy(
+            src_ref=fin.at[pl.ds(pl.multiple_of(target * token_share, token_share), token_share), :],
+            dst_ref=hid.at[:, own_cols],
+            send_sem=fs.at[step - 1],
+            recv_sem=fr.at[step - 1],
+            device_id={"mp": target},
+            device_id_type=MESH,
+        )
+
+    for step in (2, 1, 3):
+        shared(step).start()
+    hid[:, own_cols] = fin[pl.ds(pl.multiple_of(me * token_share, token_share), token_share), :]
+    for h in range(2):
+        wait_sends(m_args, last, h)
+    for step in (2, 1, 3):
+        shared(step).wait()
+    out_ref[...] = hid[...]
+
+
+def decode(state, segment_ids, weights):
+    length, block = state.shape
+    parts = lax.axis_size("mp")
+    copies = lax.axis_size(DP)
+    depth = weights.shape[1]
+    joined = weights.shape[2] - parts * (block // copies)
+    cosine, sinus = rope_tables(length)
+    dma = pltpu.SemaphoreType.DMA
+    vmem = pl.BlockSpec(memory_space=pltpu.VMEM)
+    return pl.pallas_call(
+        decoder_kernel,
+        out_shape=jax.ShapeDtypeStruct((length // parts, parts * block), jnp.bfloat16),
+        in_specs=[vmem] * 5 + [pl.BlockSpec(memory_space=pl.ANY)],
+        out_specs=vmem,
+        scratch_shapes=[
+            pltpu.VMEM((2, length, parts * block), jnp.bfloat16),
+            pltpu.VMEM((2, length, parts * depth), jnp.bfloat16),
+            pltpu.VMEM((2, copies * depth, joined), jnp.bfloat16),
+            pltpu.VMEM((2, parts * depth, block), jnp.bfloat16),
+            pltpu.VMEM((length // 2, block), jnp.float32),
+            pltpu.VMEM((length // 2, HD), jnp.float32),
+            pltpu.VMEM((length, HD), jnp.bfloat16),
+            pltpu.VMEM((length, HD), jnp.bfloat16),
+            pltpu.VMEM((length, length), jnp.float32),
+            pltpu.VMEM((length, block), jnp.bfloat16),
+            pltpu.VMEM((length // parts, parts * block), jnp.bfloat16),
+            dma((2, 2, 6)),
+            dma((2, 2, 6)),
+            dma((2, 2, 6)),
+            dma((2, 2, 6)),
+            dma((2, copies)),
+            dma((2, copies * parts)),
+            dma((3,)),
+            dma((3,)),
+        ],
+        compiler_params=pltpu.CompilerParams(
+            collective_id=0, has_side_effects=True, vmem_limit_bytes=60 * 1024 * 1024
+        ),
+    )(segment_ids[:, None], segment_ids[None, :], cosine, sinus, state, weights)
 
 
 def shards(
@@ -150,6 +450,9 @@
     parts = lax.axis_size("mp")
     copies = lax.axis_size(DP)
     copy_at = lax.axis_index(DP)
+    totals = jnp.sum(loss_mask)
+    for axis in SECTION_DP_MP:
+        totals = lax.psum(totals, axis)
     small = jnp.concatenate([v_qkv[0], v_qkv[1], v_qkv[2], v_out.T, v_up, v_down.T], axis=1)
     small = lax.all_gather(small, SECTION_DP, axis=0, tiled=True)
     proj_full = lax.all_gather(v_proj, SECTION_DP, axis=0, tiled=True)
@@ -166,12 +469,9 @@
     own_out = lax.all_to_all(
         jnp.moveaxis(own_out, 1, 0), "mp", split_axis=0, concat_axis=0, tiled=True
     )
-    joined_all = lax.all_gather(own_rows, SECTION_DP).reshape(
-        sections, model_width, own_rows.shape[1]
-    )
-    out_all = lax.all_gather(own_out, SECTION_DP).reshape(
-        sections, copies, parts * w_out.shape[1], col_share
-    )
+    own_out, totals = lax.optimization_barrier((own_out, totals))
+    own_out = jnp.moveaxis(own_out, 0, 1).reshape(w_out.shape[1], parts * col_share)
+    weights = lax.all_gather(jnp.concatenate([own_rows, own_out], axis=1), SECTION_DP)
     text_blocks = lax.all_to_all(
         jnp.moveaxis(text[0].reshape(text.shape[1], parts, block_width), 1, 0),
         "mp",
@@ -179,6 +479,7 @@
         concat_axis=0,
         tiled=True,
     ).reshape(text.shape[1] * parts, block_width)
+    patches, totals, text_blocks = lax.optimization_barrier((patches, totals, text_blocks))
     embedded = encode_tiles(patches, vis_gain, vis_bias, small, proj_full)
     length = segments.shape[2]
     tiles_here = embedded.shape[0] // POOL
@@ -235,20 +536,7 @@
     )
     state = jnp.where(covered[:, None], image_cols, text_blocks)
     segment_ids = segments[0, 0]
-    allowed = (segment_ids[:, None] == segment_ids[None, :]) & (places[None, :] <= places[:, None])
-    cosine, sinus = rope_tables(length)
-    for layer in range(sections):
-        w_layer = jnp.moveaxis(out_all[layer], 0, 1).reshape(out_all.shape[2], block_width)
-        state = decoder_layer(state, allowed, cosine, sinus, joined_all[layer], w_layer)
-    hidden = lax.all_to_all(
-        state.reshape(parts, length // parts, block_width),
-        "mp",
-        split_axis=0,
-        concat_axis=0,
-        tiled=True,
-    )
-    hidden = jnp.moveaxis(hidden, 0, 1).reshape(length // parts, model_width)
-    totals = lax.psum(jnp.sum(loss_mask), SECTION_DP_MP)
+    hidden = decode(state, segment_ids, weights)
     scaling = float(sections * lax.axis_size(DP) * length)
     token_weight = loss_mask.astype(jnp.float32) * scaling / totals.astype(jnp.float32)
     return (hidden[None], token_weight)

time: 708 us -> 524 us (0.74)
  Pallas kernels: 0 us -> 253 us
  blocking collectives: 269 us -> 82 us
  local copies, waits for them, and re-layouts: 114 us -> 31.4 us
  waiting for transfers between devices: 164 us -> 87.7 us
  matrix products: 70.7 us -> 24.7 us
  starting transfers between devices: 39.1 us -> 16.7 us
  other arithmetic: 27.5 us -> 12.7 us
    pallas_call x0 -> x1, Pallas kernels: none -> 253 us  [decode(): pl.pallas_call(decoder_kernel, out_shape=jax.ShapeDtypeStruct((length //...]
    all_to_all x4 -> x1, blocking collectives: 188 us -> 49.4 us  [gathered(): return lax.all_to_all(copies, axis, split_axis=0, concat_axis=0, tiled=True)]
    all_to_all x6 -> x1, waiting for transfers between devices: 129 us -> 43.9 us  [gathered(): return lax.all_to_all(copies, axis, split_axis=0, concat_axis=0, tiled=True)]
    dot_general x16 -> x0, matrix products: 46.4 us -> none  [the longest x4 22.1 us: decoder_layer(): added = jnp.dot(parts, w_out, preferred_element_type=jnp.float32)]
    psum x1 -> x4, blocking collectives: 66.9 us -> 32.7 us  [shards(): totals = lax.psum(totals, axis)]
    slice x6 -> x0, local copies, waits for them, and re-layouts: 30.1 us -> none  [the longest x1 15.8 us: shards(): joined_all[layer]]
    transpose x5 -> x1, local copies, waits for them, and re-layouts: 27 us -> 0.21 us  [shards(): jnp.moveaxis(own_out, 0, 1).reshape(w_out.shape[1], parts * col_share)]
    all_gather x1, waiting for transfers between devices: 24.4 us -> 0.02 us  [shards(): small = lax.all_gather(small, SECTION_DP, axis=0, tiled=True)]
  transfers between devices with their start and end apart: 13 -> 7, of which waited for: 9 -> 4; matrix products, arithmetic and copies ran while one was open for 19% -> 12% of each run, Pallas kernels for 0% -> 0%
where the time goes in v2:
time: 524 us; the launch traced here: 523 us
  Pallas kernels  253 us (48%)
  waiting for transfers between devices  87.7 us (17%)
  blocking collectives  82 us (16%)
  local copies, waits for them, and re-layouts  31.4 us (6%)
  matrix products  24.7 us (5%)
  starting transfers between devices  16.7 us (3%)
  between operations  14.8 us (3%)
  other arithmetic  12.7 us (2%)
    pallas_call x1, Pallas kernels, decode(): pl.pallas_call(decoder_kernel, out_shape=jax.ShapeDtypeStruct((length //...  253 us
    all_to_all x1, blocking collectives, gathered(): return lax.all_to_all(copies, axis, split_axis=0, concat_axis=0, tiled=True)  49.4 us
    all_to_all x1, waiting for transfers between devices, gathered(): return lax.all_to_all(copies, axis, split_axis=0, concat_axis=0, tiled=True)  43.9 us
    psum x4, blocking collectives, shards(): totals = lax.psum(totals, axis)  32.7 us
    all_gather x1, waiting for transfers between devices, shards(): lax.all_gather(jnp.concatenate([own_rows, own_out], axis=1), SECTION_DP)  17.9 us
    unnamed x39, local copies, waits for them, and re-layouts  14.5 us
    all_to_all x1, waiting for transfers between devices, shards(): lax.all_to_all(jnp.moveaxis(text[0].reshape(text.shape[1], parts, block_w...  14.1 us
    all_to_all x1, waiting for transfers between devices, shards(): lax.all_to_all(blocks, 'section', split_axis=0, concat_axis=0, tiled=True)  11 us
  transfers between devices with their start and end apart: 7, of which 4 were waited for; matrix products, arithmetic and copies ran while one was open for 12% of the time, Pallas kernels for 0%

profile of v2, /device:TPU:0, one launch (start us, length us, event | category | flops | bytes accessed | tf_op | source)
XLA Modules:
  0.0 522.6 jit_solution(1523924533807942166)
XLA Ops:
  7.2 0.7 bitcast_dynamic-update-slice_fusion.4
  7.9 0.7 bitcast_dynamic-update-slice_fusion.3
  8.7 0.7 bitcast_dynamic-update-slice_fusion.2
  9.4 0.7 bitcast_dynamic-update-slice_fusion.1
  10.1 0.8 constant_dynamic-update-slice_fusion
  10.9 0.8 bitcast_dynamic-update-slice_fusion
  11.8 0.7 copy-done.7
  12.5 0.7 all-gather.7.cloned.1.call-update
  13.2 1.3 reduce_sum.102
  14.5 10.5 %psum.28 = s32[]{:T(128)} all-reduce(s32[]{:T(128)} %reduce_sum.102), channel_id=1, replica_groups=mesh['section'=4,'dp_0'=4,'dp_1'=2,'mp'=4] {'section'}, use_global_device_ids=true, to_apply=%region_6.0 | all-reduce | flops 1 | bytes 8 | tf_op jit(solution)/shard_map/psum | solution.py:455
  25.0 9.7 %psum.29 = s32[]{:T(128)} all-reduce(s32[]{:T(128)} %psum.28), channel_id=1, replica_groups=mesh['section'=4,'dp_0'=4,'dp_1'=2,'mp'=4] {'dp_0'}, use_global_device_ids=true, to_apply=%region_7.0 | all-reduce | flops 1 | bytes 8 | tf_op jit(solution)/shard_map/psum | solution.py:455
  34.7 6.5 %copy.46 = bf16[1,512,4096]{1,2,0:T(8,128)(2,1)} copy(bf16[1,512,4096]{2,1,0:T(8,128)(2,1)} %param.26) | data formatting | bytes 8388608 | tf_op args[9]
  41.2 1.2 constant_dynamic-slice_fusion
  42.4 1.0 copy.47
  43.4 4.3 all-to-all-start
  47.7 2.4 psum.30
  50.3 10.1 %psum.31 = s32[]{:T(128)} all-reduce(s32[]{:T(128)} %psum.30), channel_id=1, replica_groups=mesh['section'=4,'dp_0'=4,'dp_1'=2,'mp'=4] {'mp'}, use_global_device_ids=true, to_apply=%region_9.0 | all-reduce | flops 1 | bytes 8 | tf_op jit(solution)/shard_map/psum | solution.py:455
  60.4 1.1 dynamic-slice_bitcast_fusion
  62.1 1.2 pad_maximum_fusion
  63.8 0.8 reshape_squeeze.7
  64.7 1.3 copy.69
  65.9 3.5 all-to-all-start.1
  69.5 14.1 %all-to-all-done.1 = bf16[4,128,1024]{2,1,0:T(8,128)(2,1)S(1)} async-done(((bf16[4,128,1024]{2,1,0:T(8,128)(2,1)}), bf16[4,128,1024]{2,1,0:T(8,128)(2,1)S(1)}, u32[]{:S(2)}, u32[]{:S(2)}) %all-to-all-start.1) | async-done | bytes 1048608 | tf_op jit(solution)/shard_map/all_to_all | solution.py:475
  84.3 2.5 fusion.35
  86.8 1.8 reshape.167
  88.6 1.9 fusion.158
  91.3 2.1 fusion.161
  93.4 1.9 fusion.39
  95.6 1.7 convolution_convert_fusion.1
  97.9 49.4 %all_to_all.32 = bf16[4,512,1024]{2,1,0:T(8,128)(2,1)S(1)} all-to-all(bf16[4,512,1024]{2,1,0:T(8,128)(2,1)S(1)} %broadcast_in_dim.15), channel_id=1, replica_groups=mesh['section'=4,'dp_0'=4,'dp_1'=2,'mp'=4] {'mp'}, dimensions={0} | all-to-all | bytes 8388608 | tf_op jit(solution)/shard_map/all_to_all | solution.py:51
  147.2 0.9 convert_reduce_fusion.1
  149.0 8.6 %fusion.32 = bf16[512,1024]{1,0:T(8,128)(2,1)S(1)} fusion(bf16[1024,3072]{1,0:T(8,128)(2,1)} %all-gather.5.cloned.1.call-done, bf16[512,1024]{1,0:T(8,128)(2,1)S(1)} %get-tuple-element.13, f32[1024]{0:T(1024)S(1)} %bitcast.101, f32[1024]{0:T(1024)S(1)} %bitcast.100, f32[512]{0:T(512)S(1)} %add_rsqrt_fusion, f32[512]{0:T(512)S(1)} %broadcast_multiply_fusion), kind=kOutput, calls=%fused_computation.53 | convolution fusion | flops 2185232384 | bytes 6303744 | tf_op jit(solution)/shard_map/dot_general | solution.py:60
  157.6 2.5 broadcast_in_dim.16
  160.1 5.0 all-to-all-start.3
  166.0 1.0 fusion.110
  167.0 43.9 %all-to-all-done.3 = bf16[4,512,1024]{2,1,0:T(8,128)(2,1)} async-done(((bf16[4,512,1024]{2,1,0:T(8,128)(2,1)}), bf16[4,512,1024]{2,1,0:T(8,128)(2,1)}, u32[]{:S(2)}, u32[]{:S(2)}) %all-to-all-start.3) | async-done | bytes 4194336 | tf_op jit(solution)/shard_map/all_to_all | solution.py:51
  210.9 3.9 convert_reduce_fusion
  215.7 0.9 copy.68
  216.6 0.8 reshape.164
  217.4 6.4 %convolution_convert_fusion.2 = bf16[256,1024]{1,0:T(8,128)(2,1)} fusion(pred[256,128]{0,1:T(32,128)(4,1)S(1)} %bitcast_and_fusion, bf16[128,4096]{1,0:T(8,128)(2,1)S(1)} %reshape.164, bf16[4096,1024]{1,0:T(8,128)(2,1)} %all-gather.7.cloned.1.call-done), kind=kOutput, calls=%fused_computation.59 | convolution fusion | flops 1141243904 | bytes 9994240 | tf_op jit(solution)/shard_map/dot_general | solution.py:506
  223.8 3.8 all-to-all-start.4
  227.8 0.8 copy.58.seg_col
  228.6 1.0 pad_maximum_fusion.1
  230.8 11.0 %all-to-all-done.4 = bf16[4,64,1024]{2,1,0:T(8,128)(2,1)S(1)} async-done(((bf16[4,64,1024]{2,1,0:T(8,128)(2,1)}), bf16[4,64,1024]{2,1,0:T(8,128)(2,1)S(1)}, u32[]{:S(2)}, u32[]{:S(2)}) %all-to-all-start.4) | async-done | bytes 524320 | tf_op jit(solution)/shard_map/all_to_all | solution.py:509
  241.8 1.4 fusion.38.s0_ref
  243.2 17.9 %all-gather.9.cloned.1.call-done = bf16[16384,1280]{1,0:T(8,128)(2,1)} async-done(((bf16[512,1280]{1,0:T(8,128)(2,1)}), bf16[16384,1280]{1,0:T(8,128)(2,1)}) %all-gather.9.cloned.1.call-update) | async-done | bytes 41943056 | tf_op jit(solution)/shard_map/all_gather | solution.py:474
  261.2 252.6 %shard_map.176 = bf16[128,4096]{1,0:T(8,128)(2,1)} custom-call(s32[512,1]{1,0:T(8,128)} %copy.58.seg_col, s32[1,512]{1,0:T(1,128)} %bitcast.97, f32[512,128]{1,0:T(8,128)} %get-tuple-element.28.cos_ref, f32[512,128]{1,0:T(8,128)} %get-tuple-element.29.sin_ref, bf16[512,1024]{1,0:T(8,128)(2,1)} %fusion.38.s0_ref, bf16[32,512,1280]{2,1,0:T(8,128)(2,1)} %bitcast.87), custom_call_target="tpu_custom_call" | custom-call | tf_op jit(solution)/shard_map/pallas_call | solution.py:397
  513.7 2.3 copy.78
  (76 shorter events, 6.9 us)
Async XLA Ops:
  7.2 43.2 %copy-start = (f32[1,4096]{1,0:T(1,128)S(1)}, f32[1,4096]{1,0:T(1,128)}, u32[]{:S(2)}) copy-start(f32[1,4096]{1,0:T(1,128)} %param.23) | copy-start | bytes 49156
  7.2 77.1 %all-gather.5.cloned.1.call-start = ((), (), s32[]{:S(2)}) async-start(), calls=%async_computation.5 | async-start | bytes 6488064 | tf_op jit(solution)/shard_map/all_gather | solution.py:457
  11.8 0.7 copy-start.7
  12.5 204.9 %all-gather.7.cloned.1.call-start = ((), (), s32[]{:S(2)}) async-start(), calls=%async_computation.6 | async-start | bytes 8650752 | tf_op jit(solution)/shard_map/all_gather | solution.py:458
  41.2 9.0 %copy-start.3 = (bf16[1,2,4096,128]{3,2,1,0:T(8,128)(2,1)S(1)}, bf16[1,2,4096,128]{3,2,1,0:T(8,128)(2,1)}, u32[]{:S(2)}) copy-start(bf16[1,2,4096,128]{3,2,1,0:T(8,128)(2,1)} %param.25) | copy-start | bytes 6291460
  43.4 18.3 %all-to-all-start = ((bf16[4,512,128]{2,1,0:T(8,128)(2,1)}), bf16[4,512,128]{2,1,0:T(8,128)(2,1)S(1)}, u32[]{:S(2)}, u32[]{:S(2)}) async-start(bf16[4,512,128]{2,1,0:T(8,128)(2,1)} %bitcast.10), calls=%async_computation | async-start | bytes 1048576 | tf_op jit(solution)/shard_map/all_to_all | solution.py:469
  47.7 213.5 %all-gather.9.cloned.1.call-start = ((), (), s32[]{:S(2)}) async-start(), calls=%async_computation.7 | async-start | bytes 43253760 | tf_op jit(solution)/shard_map/all_gather | solution.py:474
  62.1 1.7 copy-start.4
  64.6 4.8 copy-start.9
  64.6 4.9 copy-start.10
  64.7 18.9 %copy-start.2 = (bf16[512,1024]{1,0:T(8,128)(2,1)S(1)}, bf16[512,1024]{1,0:T(8,128)(2,1)}, u32[]{:S(2)}) copy-start(bf16[512,1024]{1,0:T(8,128)(2,1)} %param.18) | copy-start | bytes 3145732
  65.9 17.6 %all-to-all-start.1 = ((bf16[4,128,1024]{2,1,0:T(8,128)(2,1)}), bf16[4,128,1024]{2,1,0:T(8,128)(2,1)S(1)}, u32[]{:S(2)}, u32[]{:S(2)}) async-start(bf16[4,128,1024]{2,1,0:T(8,128)(2,1)} %bitcast.86), calls=%async_computation.1 | async-start | bytes 2097152 | tf_op jit(solution)/shard_map/all_to_all | solution.py:475
  83.6 3.2 copy-start.5
  160.1 5.0 copy-start.11
  160.1 5.8 %copy-start.12 = (s32[1,8]{1,0:T(1,128)S(1)}, s32[1,8]{1,0:T(1,128)}, u32[]{:S(2)}) copy-start(s32[1,8]{1,0:T(1,128)} %param.22) | copy-start | bytes 100
  160.1 50.8 %all-to-all-start.3 = ((bf16[4,512,1024]{2,1,0:T(8,128)(2,1)}), bf16[4,512,1024]{2,1,0:T(8,128)(2,1)}, u32[]{:S(2)}, u32[]{:S(2)}) async-start(bf16[4,512,1024]{2,1,0:T(8,128)(2,1)} %broadcast_in_dim.16), calls=%async_computation.3 | async-start | bytes 8388608 | tf_op jit(solution)/shard_map/all_to_all | solution.py:51
  217.4 10.4 %copy-start.8 = (s32[1,1,512]{2,1,0:T(1,128)S(1)}, s32[1,1,512]{2,1,0:T(1,128)}, u32[]{:S(2)}) copy-start(s32[1,1,512]{2,1,0:T(1,128)} %param.19) | copy-start | bytes 6148
  223.8 6.5 %copy-start.13 = (s32[1,128]{1,0:T(1,128)S(1)}, s32[1,128]{1,0:T(1,128)}, u32[]{:S(2)}) copy-start(s32[1,128]{1,0:T(1,128)} %param.20) | copy-start | bytes 1540
  223.8 18.0 %copy-start.6 = (bf16[4,128,1024]{2,1,0:T(8,128)(2,1)S(1)}, bf16[4,128,1024]{2,1,0:T(8,128)(2,1)}, u32[]{:S(2)}) copy-start(bf16[4,128,1024]{2,1,0:T(8,128)(2,1)} %copy-done.5) | copy-start | bytes 3145732
  223.8 18.0 %all-to-all-start.4 = ((bf16[4,64,1024]{2,1,0:T(8,128)(2,1)}), bf16[4,64,1024]{2,1,0:T(8,128)(2,1)S(1)}, u32[]{:S(2)}, u32[]{:S(2)}) async-start(bf16[4,64,1024]{2,1,0:T(8,128)(2,1)} %bitcast.27), calls=%async_computation.4 | async-start | bytes 1048576 | tf_op jit(solution)/shard_map/all_to_all | solution.py:509
  261.2 254.9 %copy-start.1 = (f32[1,4096]{1,0:T(1,128)S(1)}, f32[1,4096]{1,0:T(1,128)}, u32[]{:S(2)}) copy-start(f32[1,4096]{1,0:T(1,128)} %param.23) | copy-start | bytes 49156
Sparse Core Ops, SparseCore 0:
  12.6 51.6 all-gather.4
  66.5 51.5 all-gather.6
  120.4 140.7 all-gather.8

commit v3 on v2

--- a/solution.py
+++ b/solution.py
@@ -23,45 +23,6 @@
 MESH = pl.DeviceIdType.MESH
 
 
-def layer_norm(values, gain, bias):
-    wide = values.astype(jnp.float32)
-    center = wide - jnp.mean(wide, axis=-1, keepdims=True)
-    spread = jnp.mean(center * center, axis=-1, keepdims=True)
-    return (center * lax.rsqrt(spread + EPS) * gain + bias).astype(jnp.bfloat16)
-
-
-def rms_norm(values, gain):
-    wide = values.astype(jnp.float32)
-    power = jnp.mean(wide * wide, axis=-1, keepdims=True)
-    return (wide * lax.rsqrt(power + EPS) * gain).astype(jnp.bfloat16)
-
-
-def pixel_shuffle(states):
-    tile_count = states.shape[0] // PATCH
-    side_half = GRID // 2
-    width = states.shape[1]
-    arranged = states.reshape(tile_count, side_half, 2, side_half, 2, width)
-    return arranged.transpose(0, 1, 3, 2, 4, 5).reshape(
-        tile_count * side_half * side_half, 4 * width
-    )
-
-
-def gathered(array, axis):
-    copies = jnp.broadcast_to(array, (lax.axis_size(axis), *array.shape))
-    return lax.all_to_all(copies, axis, split_axis=0, concat_axis=0, tiled=True)
-
-
-def block_sum(partial_value):
-    everything = gathered(partial_value.astype(jnp.bfloat16), "mp")
-    return jnp.sum(everything.astype(jnp.float32), axis=0)
-
-
-def transposed_dot(left, right):
-    return lax.dot_general(
-        left, right, (((1,), (1,)), ((), ())), preferred_element_type=jnp.float32
-    )
-
-
 def rope_tables(length):
     half_width = HD // 2
     freqs = ROPE_BASE ** (-2.0 * jnp.arange(half_width, dtype=jnp.float32) / HD)
@@ -73,33 +34,432 @@
     )
 
 
-def encode_tiles(patches, vis_gain, vis_bias, small, proj_full):
-    tile_count = patches.shape[0] // PATCH
-    width = patches.shape[1]
-    local = width // lax.axis_size("mp")
-    head_count = local // VHD
-    normed = layer_norm(patches, vis_gain[0], vis_bias[0])
-    joined = jnp.dot(normed, small[:, : 3 * local], preferred_element_type=jnp.float32)
-    joined = joined.astype(jnp.bfloat16).reshape(tile_count, PATCH, 3, head_count, VHD)
-    query, keyed, valued = (joined[:, :, index] for index in range(3))
-    scores = jnp.einsum("tqhd,tkhd->thqk", query, keyed, preferred_element_type=jnp.float32)
-    probs = jax.nn.softmax(scores * VHD ** (-0.5), axis=-1).astype(jnp.bfloat16)
-    mixed = jnp.einsum("thqk,tkhd->tqhd", probs, valued, preferred_element_type=jnp.float32)
-    mixed = mixed.astype(jnp.bfloat16).reshape(tile_count * PATCH, local)
-    attended = block_sum(transposed_dot(mixed, small[:, 3 * local : 4 * local]))
-    residual = (patches.astype(jnp.float32) + attended).astype(jnp.bfloat16)
-    normed_two = layer_norm(residual, vis_gain[1], vis_bias[1])
-    hidden = small.shape[1] // 2 - 2 * local
-    up = small[:, 4 * local : 4 * local + hidden]
-    down = small[:, 4 * local + hidden :]
-    inner = jax.nn.gelu(
-        jnp.dot(normed_two, up, preferred_element_type=jnp.float32), approximate=False
-    ).astype(jnp.bfloat16)
-    fed = block_sum(transposed_dot(inner, down))
-    states = (residual.astype(jnp.float32) + fed).astype(jnp.bfloat16)
-    return jnp.dot(pixel_shuffle(states), proj_full, preferred_element_type=jnp.float32).astype(
-        jnp.bfloat16
+def vision_kernel(
+    patches_ref,
+    gain_ref,
+    bias_ref,
+    text_ref,
+    mask_ref,
+    own_ref,
+    place_ref,
+    small_ref,
+    proj_ref,
+    state_ref,
+    weight_ref,
+    sm,
+    pj,
+    joined,
+    mix,
+    part,
+    rsb,
+    res,
+    n2,
+    pooled,
+    blk,
+    arrived,
+    txt,
+    cbuf,
+    gs,
+    gr,
+    xs,
+    xr,
+    zs,
+    zr,
+    ts,
+    tr,
+    cs,
+    cr,
+    loc,
+):
+    parts = 4
+    z, y, c, me = (lax.axis_index(name) for name in ("section", "dp_0", "dp_1", "mp"))
+    rows, width = patches_ref.shape
+    tiles = rows // PATCH
+    share = PATCH // parts
+    local = width // parts
+    hidden = small_ref.shape[1] // 2 - 2 * local
+    block = text_ref.shape[1] // parts
+    token_share = text_ref.shape[0]
+    pool_share = POOL // parts
+
+    def place_of(core, first, second):
+        return first * (8 - 6 * core) + second * (2 + 6 * core) + core
+
+    a, b = z * (1 - c) + y * c, y * (1 - c) + z * c
+    pa, pb = z * c + y * (1 - c), y * c + z * (1 - c)
+
+    def along_a(step):
+        return {"section": lax.rem(z + (1 - c) * step, 4), "dp_0": lax.rem(y + c * step, 4)}
+
+    def along_b(step):
+        return {"section": lax.rem(z + c * step, 4), "dp_0": lax.rem(y + (1 - c) * step, 4)}
+
+    def along_x(step):
+        return {"mp": lax.rem(me + step, parts)}
+
+    partner = {"dp_1": 1 - c}
+    full, own_piece = (sm, pj), (small_ref, proj_ref)
+
+    def remote(src, dst, send, recv, target):
+        return pltpu.make_async_remote_copy(
+            src_ref=src,
+            dst_ref=dst,
+            send_sem=send,
+            recv_sem=recv,
+            device_id=target,
+            device_id_type=MESH,
+        )
+
+    def region(arr, core, first, second):
+        count = own_piece[arr].shape[0]
+        at = place_of(core, lax.rem(first, 4), lax.rem(second, 4))
+        return full[arr].at[pl.ds(pl.multiple_of(at * count, count), count), :]
+
+    def share_out(arr, kind, ra, rb, target):
+        dst = region(arr, c, a + ra, b + rb)
+        src = own_piece[arr] if (ra, rb) == (0, 0) else dst
+        return remote(src, dst, gs.at[arr, kind], gr.at[arr, kind], target)
+
+    started = ([], [])
+
+    def give(arr, kind, ra, rb, target):
+        copy = share_out(arr, kind, ra, rb, target)
+        copy.start()
+        started[arr].append(copy)
+
+    def take(arr, kind, ra, rb):
+        share_out(arr, kind, ra, rb, partner).wait_recv()
+
+    def to_both(arr, ra):
+        give(arr, 3 + ra, ra, 0, along_b(1))
+        give(arr, 7 + ra, ra, 0, along_b(3))
+        give(arr, 15 + ra * 4, ra, 0, partner)
+
+    def gather_start(arr):
+        give(arr, 0, 0, 0, along_a(1))
+        give(arr, 1, 0, 0, along_a(3))
+        to_both(arr, 0)
+        pltpu.make_async_copy(own_piece[arr], region(arr, c, a, b), loc.at[arr]).start()
+
+    def gather_a(arr):
+        take(arr, 0, 3, 0)
+        if arr == 0:
+            give(arr, 2, 3, 0, along_a(1))
+        to_both(arr, 3)
+        take(arr, 1, 1, 0)
+        if arr == 1:
+            give(arr, 2, 1, 0, along_a(3))
+        to_both(arr, 1)
+        take(arr, 2, 2, 0)
+        to_both(arr, 2)
+
+    def gather_b(arr):
+        for ra in (0, 3, 1, 2):
+            take(arr, 3 + ra, ra, 3)
+            if ra < 2:
+                give(arr, 11 + ra, ra, 3, along_b(1))
+            give(arr, 15 + ra * 4 + 3, ra, 3, partner)
+            take(arr, 7 + ra, ra, 1)
+            if ra >= 2:
+                give(arr, 11 + ra, ra, 1, along_b(3))
+            give(arr, 15 + ra * 4 + 1, ra, 1, partner)
+
+    def gather_b2(arr):
+        for ra in (0, 3, 1, 2):
+            take(arr, 11 + ra, ra, 2)
+            give(arr, 15 + ra * 4 + 2, ra, 2, partner)
+
+    def gather_end(arr):
+        for ra in range(4):
+            for rb in range(4):
+                kind = 15 + ra * 4 + rb
+                dst = region(arr, 1 - c, pa + ra, pb + rb)
+                remote(dst, dst, gs.at[arr, kind], gr.at[arr, kind], partner).wait_recv()
+        pltpu.make_async_copy(own_piece[arr], region(arr, c, a, b), loc.at[arr]).wait()
+
+    def count_copy(stage, step):
+        name = ("mp", "dp_1", "dp_0", "section")[stage]
+        at = (me, c, y, z)[stage]
+        size = (4, 2, 4, 4)[stage]
+        return remote(
+            cbuf.at[stage, 3],
+            cbuf.at[stage, step - 1],
+            cs.at[stage, step - 1],
+            cr.at[stage, step - 1],
+            {name: lax.rem(at + step, size)},
+        )
+
+    def count_steps(stage):
+        return (1,) if stage == 1 else (1, 2, 3)
+
+    def count_send(stage):
+        for step in count_steps(stage):
+            count_copy(stage, step).start()
+
+    def count_sum(stage):
+        total = cbuf[stage, 3]
+        for step in count_steps(stage):
+            count_copy(stage, step).wait()
+            total = total + cbuf[stage, step - 1]
+        return total
+
+    def text_copy(step):
+        target = lax.rem(me + step, parts)
+        return remote(
+            text_ref.at[:, pl.ds(pl.multiple_of(target * block, block), block)],
+            txt.at[pl.ds(pl.multiple_of(me * token_share, token_share), token_share), :],
+            ts.at[step - 1],
+            tr.at[step - 1],
+            along_x(step),
+        )
+
+    def scatter_copy(stage, tile, step):
+        target = lax.rem(me + step, parts)
+        return remote(
+            part.at[stage, tile, pl.ds(pl.multiple_of(target * share, share), share), :],
+            rsb.at[stage, tile, step - 1],
+            xs.at[2 * stage, tile, step - 1],
+            xr.at[2 * stage, tile, step - 1],
+            along_x(step),
+        )
+
+    def spread_copy(stage, tile, step):
+        if stage == 0:
+            ref = n2.at[tile, pl.ds(pl.multiple_of(me * share, share), share), :]
+        else:
+            ref = pooled.at[
+                pl.ds(pl.multiple_of(tile * POOL + me * pool_share, pool_share), pool_share), :
+            ]
+        return remote(
+            ref, ref, xs.at[2 * stage + 1, tile, step - 1], xr.at[2 * stage + 1, tile, step - 1], along_x(step)
+        )
+
+    def normed(wide, at):
+        center = wide - jnp.mean(wide, axis=1, keepdims=True)
+        spread = jnp.mean(center * center, axis=1, keepdims=True)
+        scaled = center * lax.rsqrt(spread + EPS) * gain_ref[at : at + 1, :]
+        return (scaled + bias_ref[at : at + 1, :]).astype(jnp.bfloat16)
+
+    def own_sum(stage, tile):
+        mine = pl.ds(pl.multiple_of(me * share, share), share)
+        total = part[stage, tile, mine, :].astype(jnp.float32)
+        for step in (1, 3, 2):
+            scatter_copy(stage, tile, step).wait()
+            total = total + rsb[stage, tile, step - 1].astype(jnp.float32)
+        return total
+
+    barrier = pltpu.get_barrier_semaphore()
+    others = [{"section": lax.rem(z + step, 4)} for step in (1, 2, 3)]
+    others += [{"dp_0": lax.rem(y + step, 4)} for step in (1, 2, 3)]
+    others += [along_x(step) for step in (1, 2, 3)] + [partner]
+    for target in others:
+        pl.semaphore_signal(barrier, inc=1, device_id=target, device_id_type=MESH)
+    mask = mask_ref[...].astype(jnp.float32)
+    cbuf[0, 3] = jnp.broadcast_to(jnp.sum(mask, axis=1, keepdims=True), cbuf.shape[2:])
+    pl.semaphore_wait(barrier, len(others))
+    gather_start(0)
+    gather_start(1)
+    for step in (1, 3, 2):
+        text_copy(step).start()
+    count_send(0)
+    own_rows = pl.ds(pl.multiple_of(me * token_share, token_share), token_share)
+    txt[own_rows, :] = text_ref[:, pl.ds(pl.multiple_of(me * block, block), block)]
+    first = normed(patches_ref[...].astype(jnp.float32), 0)
+    gather_a(0)
+    gather_a(1)
+    gather_b(0)
+    gather_b2(0)
+    cbuf[1, 3] = count_sum(0)
+    count_send(1)
+    gather_end(0)
+    joined[...] = jnp.dot(first, sm[:, : 3 * local], preferred_element_type=jnp.float32)
+    low = lax.broadcasted_iota(jnp.int32, (PATCH, 2 * VHD), 1) < VHD
+
+    def attend(tile):
+        at = pl.ds(tile * PATCH, PATCH)
+        for pair in range(local // (2 * VHD)):
+            start = pair * 2 * VHD
+            query = joined[at, start : start + 2 * VHD]
+            keyed = joined[at, local + start : local + start + 2 * VHD].astype(jnp.bfloat16)
+            valued = joined[at, 2 * local + start : 2 * local + start + 2 * VHD]
+            valued = valued.astype(jnp.bfloat16)
+            found = []
+            for side in (low, jnp.logical_not(low)):
+                masked = jnp.where(side, query, 0.0).astype(jnp.bfloat16)
+                scores = lax.dot_general(
+                    masked, keyed, (((1,), (1,)), ((), ())), preferred_element_type=jnp.float32
+                )
+                scores = scores * VHD ** (-0.5)
+                probs = jnp.exp(scores - jnp.max(scores, axis=1, keepdims=True))
+                total = jnp.sum(probs, axis=1, keepdims=True)
+                product = jnp.dot(
+                    probs.astype(jnp.bfloat16), valued, preferred_element_type=jnp.float32
+                )
+                found.append(product / total)
+            mix[at, start : start + 2 * VHD] = jnp.where(low, *found).astype(jnp.bfloat16)
+        partial_sum = lax.dot_general(
+            mix[at, :],
+            sm[:, 3 * local : 4 * local],
+            (((1,), (1,)), ((), ())),
+            preferred_element_type=jnp.float32,
+        )
+        part[0, tile] = partial_sum.astype(jnp.bfloat16)
+        for step in (1, 3, 2):
+            scatter_copy(0, tile, step).start()
+
+    def middle(tile):
+        mine = pl.ds(pl.multiple_of(tile * PATCH + me * share, share), share)
+        total = patches_ref[mine, :].astype(jnp.float32) + own_sum(0, tile)
+        kept = total.astype(jnp.bfloat16)
+        res[tile] = kept
+        rows_here = pl.ds(pl.multiple_of(me * share, share), share)
+        n2[tile, rows_here, :] = normed(kept.astype(jnp.float32), 1)
+        for step in (1, 3, 2):
+            spread_copy(0, tile, step).start()
+
+    def expand(tile):
+        for step in (1, 3, 2):
+            spread_copy(0, tile, step).wait()
+        inner = jnp.dot(
+            n2[tile],
+            sm[:, 4 * local : 4 * local + hidden],
+            preferred_element_type=jnp.float32,
+        )
+        inner = (0.5 * inner * (1.0 + lax.erf(inner * 0.5**0.5))).astype(jnp.bfloat16)
+        partial_sum = lax.dot_general(
+            inner,
+            sm[:, 4 * local + hidden :],
+            (((1,), (1,)), ((), ())),
+            preferred_element_type=jnp.float32,
+        )
+        part[1, tile] = partial_sum.astype(jnp.bfloat16)
+        for step in (1, 3, 2):
+            scatter_copy(1, tile, step).start()
+
+    row_at = lax.broadcasted_iota(jnp.int32, (share, share), 0)
+    col_at = lax.broadcasted_iota(jnp.int32, (share, share), 1)
+    quad, token = row_at // pool_share, row_at % pool_share
+    side = GRID // 2
+    origin = 2 * GRID * (token // side) + GRID * (quad // 2) + 2 * (token % side) + quad % 2
+    shuffle = (col_at == origin).astype(jnp.float32).astype(jnp.bfloat16)
+
+    def pool(tile):
+        kept = (res[tile].astype(jnp.float32) + own_sum(1, tile)).astype(jnp.bfloat16)
+        moved = jnp.dot(shuffle, kept, preferred_element_type=jnp.float32).astype(jnp.bfloat16)
+        mine = pl.ds(pl.multiple_of(tile * POOL + me * pool_share, pool_share), pool_share)
+        for at in range(4):
+            pooled[mine, at * width : (at + 1) * width] = moved[
+                at * pool_share : (at + 1) * pool_share, :
+            ]
+        for step in (1, 3, 2):
+            spread_copy(1, tile, step).start()
+
+    attend(0)
+    gather_b(1)
+    attend(1)
+    middle(0)
+    gather_b2(1)
+    middle(1)
+    cbuf[2, 3] = count_sum(1)
+    count_send(2)
+    for tile in range(tiles):
+        expand(tile)
+    for tile in range(tiles):
+        pool(tile)
+    cbuf[3, 3] = count_sum(2)
+    count_send(3)
+    gather_end(1)
+    for tile in range(tiles):
+        for step in (1, 3, 2):
+            spread_copy(1, tile, step).wait()
+    image = jnp.dot(pooled[...], pj[...], preferred_element_type=jnp.float32).astype(jnp.bfloat16)
+    send_row = lax.broadcasted_iota(jnp.int32, (4 * POOL, tiles * POOL), 0)
+    send_col = lax.broadcasted_iota(jnp.int32, (4 * POOL, tiles * POOL), 1)
+    chosen = (own_ref[...] == send_row // POOL) & (send_row % POOL == send_col % POOL)
+    chosen = chosen.astype(jnp.float32).astype(jnp.bfloat16)
+    blk[...] = jnp.dot(chosen, image, preferred_element_type=jnp.float32).astype(jnp.bfloat16)
+
+    def home_copy(step):
+        target = lax.rem(z + step, 4)
+        return remote(
+            blk.at[pl.ds(pl.multiple_of(target * POOL, POOL), POOL), :],
+            arrived.at[pl.ds(pl.multiple_of(z * POOL, POOL), POOL), :],
+            zs.at[step - 1],
+            zr.at[step - 1],
+            {"section": target},
+        )
+
+    for step in (2, 1, 3):
+        home_copy(step).start()
+    here = pl.ds(pl.multiple_of(z * POOL, POOL), POOL)
+    arrived[here, :] = blk[here, :]
+    count = count_sum(3)
+    scaling = float(4 * 8 * parts * token_share)
+    weight_ref[...] = mask * scaling / count[:1, :]
+    length = state_ref.shape[0]
+    picked = lax.broadcasted_iota(jnp.int32, (length, 4 * POOL), 0) == place_ref[...]
+    picked = picked.astype(jnp.float32)
+    covered = jnp.max(picked, axis=1, keepdims=True) > 0.5
+    for step in (1, 3, 2):
+        text_copy(step).wait()
+    for copies_of in started:
+        for copy in copies_of:
+            copy.wait_send()
+    for step in (1, 3, 2):
+        home_copy(step).wait()
+    placed = jnp.dot(
+        picked.astype(jnp.bfloat16), arrived[...], preferred_element_type=jnp.float32
     )
+    state_ref[...] = jnp.where(covered, placed, txt[...].astype(jnp.float32)).astype(jnp.bfloat16)
+
+
+def encode(patches, vis_gain, vis_bias, text, mask, own, place, small, proj):
+    rows, width = patches.shape
+    tiles = rows // PATCH
+    block = text.shape[1] // 4
+    length = text.shape[0] * 4
+    share = PATCH // 4
+    dma = pltpu.SemaphoreType.DMA
+    vmem = pl.BlockSpec(memory_space=pltpu.VMEM)
+    bf16 = jnp.bfloat16
+    return pl.pallas_call(
+        vision_kernel,
+        out_shape=(
+            jax.ShapeDtypeStruct((length, block), bf16),
+            jax.ShapeDtypeStruct(mask.shape, jnp.float32),
+        ),
+        in_specs=[vmem] * 9,
+        out_specs=(vmem, vmem),
+        scratch_shapes=[
+            pltpu.VMEM((small.shape[0] * 32, small.shape[1]), bf16),
+            pltpu.VMEM((proj.shape[0] * 32, proj.shape[1]), bf16),
+            pltpu.VMEM((rows, 3 * width // 4), jnp.float32),
+            pltpu.VMEM((rows, width // 4), bf16),
+            pltpu.VMEM((2, tiles, PATCH, width), bf16),
+            pltpu.VMEM((2, tiles, 3, share, width), bf16),
+            pltpu.VMEM((tiles, share, width), bf16),
+            pltpu.VMEM((tiles, PATCH, width), bf16),
+            pltpu.VMEM((tiles * POOL, 4 * width), bf16),
+            pltpu.VMEM((4 * POOL, block), bf16),
+            pltpu.VMEM((4 * POOL, block), bf16),
+            pltpu.VMEM((length, block), bf16),
+            pltpu.VMEM((4, 4, 8, 128), jnp.float32),
+            dma((2, 31)),
+            dma((2, 31)),
+            dma((4, tiles, 3)),
+            dma((4, tiles, 3)),
+            dma((3,)),
+            dma((3,)),
+            dma((3,)),
+            dma((3,)),
+            dma((4, 3)),
+            dma((4, 3)),
+            dma((2,)),
+        ],
+        compiler_params=pltpu.CompilerParams(
+            collective_id=1, has_side_effects=True, vmem_limit_bytes=56 * 1024 * 1024
+        ),
+    )(patches, vis_gain, vis_bias, text, mask, own, place, small, proj)
 
 
 def decoder_kernel(
@@ -445,17 +805,10 @@
     v_down,
     v_proj,
 ):
-    sections = lax.axis_size("section")
     section_at = lax.axis_index("section")
     parts = lax.axis_size("mp")
     copies = lax.axis_size(DP)
     copy_at = lax.axis_index(DP)
-    totals = jnp.sum(loss_mask)
-    for axis in SECTION_DP_MP:
-        totals = lax.psum(totals, axis)
-    small = jnp.concatenate([v_qkv[0], v_qkv[1], v_qkv[2], v_out.T, v_up, v_down.T], axis=1)
-    small = lax.all_gather(small, SECTION_DP, axis=0, tiled=True)
-    proj_full = lax.all_gather(v_proj, SECTION_DP, axis=0, tiled=True)
     model_width = w_query.shape[1]
     row_share = model_width // copies
     pick = lambda array: lax.dynamic_slice_in_dim(array, copy_at * row_share, row_share, 0)
@@ -469,76 +822,30 @@
     own_out = lax.all_to_all(
         jnp.moveaxis(own_out, 1, 0), "mp", split_axis=0, concat_axis=0, tiled=True
     )
-    own_out, totals = lax.optimization_barrier((own_out, totals))
     own_out = jnp.moveaxis(own_out, 0, 1).reshape(w_out.shape[1], parts * col_share)
-    weights = lax.all_gather(jnp.concatenate([own_rows, own_out], axis=1), SECTION_DP)
-    text_blocks = lax.all_to_all(
-        jnp.moveaxis(text[0].reshape(text.shape[1], parts, block_width), 1, 0),
-        "mp",
-        split_axis=0,
-        concat_axis=0,
-        tiled=True,
-    ).reshape(text.shape[1] * parts, block_width)
-    patches, totals, text_blocks = lax.optimization_barrier((patches, totals, text_blocks))
-    embedded = encode_tiles(patches, vis_gain, vis_bias, small, proj_full)
-    length = segments.shape[2]
-    tiles_here = embedded.shape[0] // POOL
-    batch_all = tile_batch[0]
-    offset_all = tile_offset[0]
-    own_batch = lax.dynamic_slice_in_dim(batch_all, section_at * tiles_here, tiles_here, 0)
-    capacity = tiles_here // 2
-    block_rows = capacity * POOL
-    local_ids = jnp.arange(tiles_here, dtype=jnp.int32)
-    local_same = (own_batch[:, None] == own_batch[None, :]) & (
-        local_ids[None, :] < local_ids[:, None]
+    own = jnp.concatenate([own_rows, own_out], axis=1)
+    weights = lax.all_gather(own, SECTION_DP)
+    small = jnp.concatenate([v_qkv[0], v_qkv[1], v_qkv[2], v_out.T, v_up, v_down.T], axis=1)
+    sections = lax.axis_size("section")
+    batch_all = tile_batch[0].reshape(sections, -1)
+    offset_all = tile_offset[0].reshape(sections, -1)
+    own_batch = lax.dynamic_slice_in_dim(batch_all, section_at, 1, 0)
+    own_batch = jnp.repeat(own_batch, POOL, axis=1)
+    starts = jnp.max(jnp.where(batch_all == section_at, offset_all, -POOL), axis=1)
+    place = jnp.repeat(starts, POOL) + jnp.tile(jnp.arange(POOL, dtype=jnp.int32), sections)
+    patches, own = lax.optimization_barrier((patches, own))
+    state, token_weight = encode(
+        patches,
+        vis_gain,
+        vis_bias,
+        text[0],
+        loss_mask,
+        own_batch,
+        place[None, :],
+        small,
+        v_proj,
     )
-    local_rank = jnp.sum(local_same.astype(jnp.int32), axis=1)
-    send_rows = jnp.arange(sections * block_rows, dtype=jnp.int32)
-    send_target = send_rows // block_rows
-    send_rank = send_rows % block_rows // POOL
-    send_match = (own_batch[None, :] == send_target[:, None]) & (
-        local_rank[None, :] == send_rank[:, None]
-    )
-    own_rows = jnp.arange(tiles_here * POOL, dtype=jnp.int32)
-    send_pick = jnp.repeat(send_match, POOL, axis=1) & (
-        (own_rows % POOL)[None, :] == (send_rows % POOL)[:, None]
-    )
-    blocks = jnp.dot(
-        send_pick.astype(jnp.bfloat16), embedded, preferred_element_type=jnp.float32
-    ).astype(jnp.bfloat16)
-    arrived = lax.all_to_all(blocks, "section", split_axis=0, concat_axis=0, tiled=True)
-    tile_ids = jnp.arange(batch_all.shape[0], dtype=jnp.int32)
-    source_ids = tile_ids // tiles_here
-    tile_same = (
-        (batch_all[:, None] == batch_all[None, :])
-        & (source_ids[:, None] == source_ids[None, :])
-        & (tile_ids[None, :] < tile_ids[:, None])
-    )
-    tile_rank = jnp.sum(tile_same.astype(jnp.int32), axis=1)
-    slot_rows = jnp.arange(sections * block_rows, dtype=jnp.int32)
-    slot_source = slot_rows // block_rows
-    slot_rank = slot_rows % block_rows // POOL
-    match = (
-        (batch_all[None, :] == section_at)
-        & (source_ids[None, :] == slot_source[:, None])
-        & (tile_rank[None, :] == slot_rank[:, None])
-    )
-    slot_place = jnp.sum(match.astype(jnp.int32) * offset_all[None, :], axis=1) + slot_rows % POOL
-    slot_valid = jnp.any(match, axis=1)
-    places = jnp.arange(length, dtype=jnp.int32)
-    picker = ((places[:, None] == slot_place[None, :]) & slot_valid[None, :]).astype(jnp.bfloat16)
-    image_cols = jnp.dot(picker, arrived, preferred_element_type=jnp.float32).astype(jnp.bfloat16)
-    covered = jnp.any(
-        (batch_all[None, :] == section_at)
-        & (places[:, None] >= offset_all[None, :])
-        & (places[:, None] < offset_all[None, :] + POOL),
-        axis=1,
-    )
-    state = jnp.where(covered[:, None], image_cols, text_blocks)
-    segment_ids = segments[0, 0]
-    hidden = decode(state, segment_ids, weights)
-    scaling = float(sections * lax.axis_size(DP) * length)
-    token_weight = loss_mask.astype(jnp.float32) * scaling / totals.astype(jnp.float32)
+    hidden = decode(state, segments[0, 0], weights)
     return (hidden[None], token_weight)
 
 

time: 524 us -> 460 us (0.88)
  Pallas kernels: 253 us -> 385 us
  blocking collectives: 82 us -> 0 us
  waiting for transfers between devices: 87.7 us -> 31.6 us
  matrix products: 24.7 us -> 0 us
  local copies, waits for them, and re-layouts: 31.4 us -> 19.1 us
  starting transfers between devices: 16.7 us -> 4.41 us
  other arithmetic: 12.7 us -> 4.86 us
    pallas_call x0 -> x1, Pallas kernels: none -> 133 us  [encode(): pl.pallas_call(vision_kernel, out_shape=(jax.ShapeDtypeStruct((length, bl...]
    all_to_all x3 -> x0, waiting for transfers between devices: 69 us -> none  [the longest x1 43.9 us: gathered(): return lax.all_to_all(copies, axis, split_axis=0, concat_axis=0, tiled=True)]
    all_to_all x1 -> x0, blocking collectives: 49.4 us -> none  [gathered(): return lax.all_to_all(copies, axis, split_axis=0, concat_axis=0, tiled=True)]
    psum x4 -> x0, blocking collectives: 32.7 us -> none  [shards(): totals = lax.psum(totals, axis)]
    dot_general x6 -> x0, matrix products: 22.6 us -> none  [the longest x2 10.3 us: transposed_dot(): lax.dot_general(left, right, (((1,), (1,)), ((), ())), preferred_element_...]
    all_to_all x3 -> x0, starting transfers between devices: 12.3 us -> none  [the longest x1 4.98 us: gathered(): return lax.all_to_all(copies, axis, split_axis=0, concat_axis=0, tiled=True)]
    reduce_sum x10 -> x0, other arithmetic: 7.99 us -> none  [the longest x2 4.85 us: block_sum(): return jnp.sum(everything.astype(jnp.float32), axis=0)]
    all_gather x3 -> x1, waiting for transfers between devices: 18 us -> 25.9 us  [shards(): weights = lax.all_gather(own, SECTION_DP)]
  transfers between devices with their start and end apart: 7 -> 2, of which waited for: 4 -> 2; matrix products, arithmetic and copies ran while one was open for 12% -> 2% of each run, Pallas kernels for 0% -> 29%
where the time goes in v3:
time: 460 us; the launch traced here: 459 us
  Pallas kernels  385 us (84%)
  waiting for transfers between devices  31.6 us (7%)
  local copies, waits for them, and re-layouts  19.1 us (4%)
  between operations  14.3 us (3%)
  other arithmetic  4.86 us (1%)
    pallas_call x1, Pallas kernels, decode(): pl.pallas_call(decoder_kernel, out_shape=jax.ShapeDtypeStruct((length //...  252 us
    pallas_call x1, Pallas kernels, encode(): pl.pallas_call(vision_kernel, out_shape=(jax.ShapeDtypeStruct((length, bl...  133 us
    all_gather x1, waiting for transfers between devices, shards(): weights = lax.all_gather(own, SECTION_DP)  25.9 us
    unnamed x33, local copies, waits for them, and re-layouts  10.5 us
  transfers between devices with their start and end apart: 2, of which 2 were waited for; matrix products, arithmetic and copies ran while one was open for 2% of the time, Pallas kernels for 29%

profile of v3, /device:TPU:0, one launch (start us, length us, event | category | flops | bytes accessed | tf_op | source)
XLA Modules:
  0.0 459.3 jit_solution(5180965407706998234)
XLA Ops:
  7.2 0.0 copy-start
  7.2 6.5 %copy.20 = bf16[1,512,4096]{1,2,0:T(8,128)(2,1)} copy(bf16[1,512,4096]{2,1,0:T(8,128)(2,1)} %param.26) | data formatting | bytes 8388608 | tf_op args[9]
  13.7 1.2 constant_dynamic-slice_fusion.1
  14.9 1.0 copy.21
  15.9 4.4 all-to-all-start
  20.3 0.0 all-gather.3.cloned.1.call-start
  20.4 0.0 copy-done.2
  20.4 1.5 fusion.4
  21.8 1.0 dynamic-slice_bitcast_fusion.1
  22.8 0.0 copy-done
  22.8 1.1 dynamic-slice_bitcast_fusion
  23.9 0.2 multiply_convert_fusion
  24.1 5.7 %all-to-all-done = bf16[4,512,128]{2,1,0:T(8,128)(2,1)S(1)} async-done(((bf16[4,512,128]{2,1,0:T(8,128)(2,1)}), bf16[4,512,128]{2,1,0:T(8,128)(2,1)S(1)}, u32[]{:S(2)}, u32[]{:S(2)}) %all-to-all-start) | async-done | bytes 524320 | tf_op jit(solution)/shard_map/all_to_all | solution.py:822
  29.8 0.2 copy.22
  30.0 0.2 copy.23
  30.3 0.0 copy-start.9
  30.3 0.0 copy-start.10
  30.3 0.0 copy-start.8
  30.3 0.0 copy-start.6
  30.3 0.0 copy-start.7
  30.3 0.0 copy-start.4
  30.3 1.1 pad_maximum_fusion
  31.5 0.0 all-gather.3.cloned.1.call-update
  31.5 0.0 copy-start.5
  31.5 0.5 broadcast.28
  32.0 0.0 copy-done.9
  32.0 0.7 reduce.6
  32.7 0.0 copy-done.10
  32.7 0.7 reduce.7
  33.4 0.1 reshape_squeeze.10
  33.5 0.1 broadcast_in_dim.19
  33.5 0.6 broadcast_in_dim.20.own_ref
  34.1 0.1 reshape_squeeze.11
  34.2 0.1 select_reduce_fusion
  34.3 0.1 iota_add_fusion
  34.4 0.7 add.33.place_ref
  35.1 0.0 copy-done.8
  35.1 0.9 copy.24.seg_col
  36.0 0.0 copy-done.6
  36.0 1.0 fusion.2
  37.0 1.0 pad_maximum_fusion.1
  38.0 0.0 copy-done.5
  38.1 0.7 copy-done.3
  38.7 133.0 %shard_map.176 = (bf16[512,1024]{1,0:T(8,128)(2,1)}, f32[1,128]{1,0:T(1,128)}) custom-call(bf16[512,1024]{1,0:T(8,128)(2,1)} %patches_ref, f32[2,1024]{1,0:T(2,128)} %gain_ref.1, f32[2,1024]{1,0:T(2,128)} %bias_ref.1, bf16[128,4096]{1,0:T(8,128)(2,1)} %bitcast.35, s32[1,128]{1,0:T(1,128)} %mask_ref.1, s32[1,128]{1,0:T(1,128)} %broadcast_in_dim.20.own_ref, ...), custom_call_target="tpu_custom_call" | custom-call | tf_op jit(solution)/shard_map/pallas_call | solution.py:425
  171.7 25.9 %all-gather.3.cloned.1.call-done = bf16[16384,1280]{1,0:T(8,128)(2,1)} async-done(((bf16[512,1280]{1,0:T(8,128)(2,1)}), bf16[16384,1280]{1,0:T(8,128)(2,1)}) %all-gather.3.cloned.1.call-update) | async-done | bytes 41943056 | tf_op jit(solution)/shard_map/all_gather | solution.py:827
  197.6 252.0 %shard_map.177 = bf16[128,4096]{1,0:T(8,128)(2,1)} custom-call(s32[512,1]{1,0:T(8,128)} %copy.24.seg_col, s32[1,512]{1,0:T(1,128)} %bitcast.36, f32[512,128]{1,0:T(8,128)} %get-tuple-element.13.cos_ref, f32[512,128]{1,0:T(8,128)} %get-tuple-element.14.sin_ref, bf16[512,1024]{1,0:T(8,128)(2,1)} %get-tuple-element.6.s0_ref, bf16[32,512,1280]{2,1,0:T(8,128)(2,1)} %bitcast.30), custom_call_target="tpu_custom_call" | custom-call | tf_op jit(solution)/shard_map/pallas_call | solution.py:757
  449.6 2.3 copy.32
  451.9 0.5 copy.33
  (17 shorter events, 0.1 us)
Async XLA Ops:
  7.2 15.6 %copy-start = (f32[1,4096]{1,0:T(1,128)S(1)}, f32[1,4096]{1,0:T(1,128)}, u32[]{:S(2)}) copy-start(f32[1,4096]{1,0:T(1,128)} %param.23) | copy-start | bytes 49156
  13.7 6.7 %copy-start.2 = (bf16[1,2,4096,128]{3,2,1,0:T(8,128)(2,1)S(1)}, bf16[1,2,4096,128]{3,2,1,0:T(8,128)(2,1)}, u32[]{:S(2)}) copy-start(bf16[1,2,4096,128]{3,2,1,0:T(8,128)(2,1)} %param.25) | copy-start | bytes 6291460
  15.9 13.9 %all-to-all-start = ((bf16[4,512,128]{2,1,0:T(8,128)(2,1)}), bf16[4,512,128]{2,1,0:T(8,128)(2,1)S(1)}, u32[]{:S(2)}, u32[]{:S(2)}) async-start(bf16[4,512,128]{2,1,0:T(8,128)(2,1)} %bitcast.8), calls=%async_computation | async-start | bytes 1048576 | tf_op jit(solution)/shard_map/all_to_all | solution.py:822
  20.3 177.3 %all-gather.3.cloned.1.call-start = ((), (), s32[]{:S(2)}) async-start(), calls=%async_computation.1 | async-start | bytes 43253760 | tf_op jit(solution)/shard_map/all_gather | solution.py:827
  30.3 1.8 copy-start.9
  30.3 2.4 copy-start.10
  30.3 4.8 %copy-start.8 = (s32[1,1,512]{2,1,0:T(1,128)S(1)}, s32[1,1,512]{2,1,0:T(1,128)}, u32[]{:S(2)}) copy-start(s32[1,1,512]{2,1,0:T(1,128)} %param.19) | copy-start | bytes 6148
  30.3 5.7 %copy-start.6 = (bf16[3,32,256]{2,1,0:T(8,128)(2,1)S(1)}, bf16[3,32,256]{2,1,0:T(8,128)(2,1)}, u32[]{:S(2)}) copy-start(bf16[3,32,256]{2,1,0:T(8,128)(2,1)} %param.29) | copy-start | bytes 147460
  30.3 5.7 %copy-start.7 = (bf16[256,32]{0,1:T(8,128)(2,1)S(1)}, bf16[256,32]{0,1:T(8,128)(2,1)}, u32[]{:S(2)}) copy-start(bf16[256,32]{0,1:T(8,128)(2,1)} %param.30) | copy-start | bytes 49156
  30.3 5.7 %copy-start.4 = (bf16[32,1024]{1,0:T(8,128)(2,1)S(1)}, bf16[32,1024]{1,0:T(8,128)(2,1)}, u32[]{:S(2)}) copy-start(bf16[32,1024]{1,0:T(8,128)(2,1)} %param.31) | copy-start | bytes 196612
  31.5 6.5 %copy-start.5 = (bf16[1024,32]{0,1:T(8,128)(2,1)S(1)}, bf16[1024,32]{0,1:T(8,128)(2,1)}, u32[]{:S(2)}) copy-start(bf16[1024,32]{0,1:T(8,128)(2,1)} %param.32) | copy-start | bytes 196612
  38.0 0.7 copy-start.3
  197.6 254.8 %copy-start.1 = (f32[1,4096]{1,0:T(1,128)S(1)}, f32[1,4096]{1,0:T(1,128)}, u32[]{:S(2)}) copy-start(f32[1,4096]{1,0:T(1,128)} %param.23) | copy-start | bytes 49156
  449.6 2.3 copy-start.11
Sparse Core Ops, SparseCore 0:
  31.6 165.9 all-gather.2

commit v4 on v3

--- a/solution.py
+++ b/solution.py
@@ -70,6 +70,9 @@
     cs,
     cr,
     loc,
+    whole,
+    hs,
+    hr,
 ):
     parts = 4
     z, y, c, me = (lax.axis_index(name) for name in ("section", "dp_0", "dp_1", "mp"))
@@ -410,7 +413,30 @@
     placed = jnp.dot(
         picked.astype(jnp.bfloat16), arrived[...], preferred_element_type=jnp.float32
     )
-    state_ref[...] = jnp.where(covered, placed, txt[...].astype(jnp.float32)).astype(jnp.bfloat16)
+    half = block // 2
+
+    def state_copy(kind, incoming):
+        if incoming:
+            back = (3, 3, 1, 1, 2, 2)[kind]
+        else:
+            back = (0, 0, 0, 0, 3, 1)[kind]
+        at = lax.rem(me + back, parts) * block + (0, 1, 1, 0, 0, 1)[kind] * half
+        ref = whole.at[:, pl.ds(pl.multiple_of(at, half), half)]
+        return remote(ref, ref, hs.at[kind], hr.at[kind], along_x((1, 1, 3, 3, 1, 3)[kind]))
+
+    first_state = jnp.where(covered, placed, txt[...].astype(jnp.float32)).astype(jnp.bfloat16)
+    whole[:, pl.ds(pl.multiple_of(me * block, block), block)] = first_state
+    for kind in (0, 2, 1, 3):
+        state_copy(kind, False).start()
+    state_copy(0, True).wait_recv()
+    state_copy(4, False).start()
+    state_copy(2, True).wait_recv()
+    state_copy(5, False).start()
+    for kind in (1, 3, 4, 5):
+        state_copy(kind, True).wait_recv()
+    for kind in range(6):
+        state_copy(kind, False).wait_send()
+    state_ref[...] = whole[...]
 
 
 def encode(patches, vis_gain, vis_bias, text, mask, own, place, small, proj):
@@ -425,7 +451,7 @@
     return pl.pallas_call(
         vision_kernel,
         out_shape=(
-            jax.ShapeDtypeStruct((length, block), bf16),
+            jax.ShapeDtypeStruct((length, 4 * block), bf16),
             jax.ShapeDtypeStruct(mask.shape, jnp.float32),
         ),
         in_specs=[vmem] * 9,
@@ -455,6 +481,9 @@
             dma((4, 3)),
             dma((4, 3)),
             dma((2,)),
+            pltpu.VMEM((length, 4 * block), bf16),
+            dma((6,)),
+            dma((6,)),
         ],
         compiler_params=pltpu.CompilerParams(
             collective_id=1, has_side_effects=True, vmem_limit_bytes=56 * 1024 * 1024
@@ -489,11 +518,13 @@
     os,
     fs,
     fr,
+    rs,
 ):
     parts = 4
     layers = 4
     copies = w_any.shape[0] // layers
-    length, block = s0_ref.shape
+    length = s0_ref.shape[0]
+    block = s0_ref.shape[1] // parts
     half = length // 2
     joined = wjb.shape[2]
     query_width = wob.shape[1] // parts
@@ -589,17 +620,16 @@
     for target in (right, opposite, left):
         pl.semaphore_signal(barrier, inc=1, device_id={"mp": target}, device_id_type=MESH)
     own_cols = pl.ds(pl.multiple_of(me * block, block), block)
-    xbuf[0, :, own_cols] = s0_ref[...]
-    pl.semaphore_wait(barrier, 3)
-    for h in range(2):
-        start_own(0, h)
-
+    ready = pltpu.make_async_copy(s0_ref, xbuf.at[0], rs.at[0])
+    ready.start()
     rows_at = lax.broadcasted_iota(jnp.int32, (length, length), 0)
     cols_at = lax.broadcasted_iota(jnp.int32, (length, length), 1)
     allowed = (seg_col[...] == seg_row[...]) & (cols_at <= rows_at)
     bias[...] = jnp.where(allowed, 0.0, BLOCKED)
-
-    def project(par, h):
+    pl.semaphore_wait(barrier, 3)
+    ready.wait()
+
+    def project(par, h, layer):
         rows = pl.ds(h * half, half)
 
         def add(source, first):
@@ -618,13 +648,21 @@
                 acc[:, :joined] += product
                 ssq[...] += power
 
+        def arrive(step):
+            @pl.when(layer > 0)
+            def _():
+                step()
+
         add(me, True)
-        forward(x_args, par, h)
-        waits(x_args, par, h, (1,))
+        if h == 1:
+            arrive(lambda: forward(x_args, par, h))
+        arrive(lambda: waits(x_args, par, h, (1,)))
         add(left, False)
-        waits(x_args, par, h, (3,))
+        arrive(lambda: waits(x_args, par, h, (3,)))
         add(right, False)
-        waits(x_args, par, h, (4, 5))
+        if h == 1:
+            forward(m_args, par, 0)
+        arrive(lambda: waits(x_args, par, h, (4, 5)))
         add(opposite, False)
 
     def attend(par, h):
@@ -661,15 +699,11 @@
             if head == heads // 2 - 1:
                 sent(0, *m_args, par, h).start()
                 sent(3, *m_args, par, h).start()
-                if h == 1:
-                    forward(m_args, par, 0)
         sent(2, *m_args, par, h).start()
         sent(1, *m_args, par, h).start()
 
     def leave(par, h, layer):
         rows = pl.ds(h * half, half)
-        if h == 1:
-            forward(m_args, par, h)
 
         def term(source):
             cols = pl.ds(pl.multiple_of(source * query_width, query_width), query_width)
@@ -683,12 +717,20 @@
         waits(m_args, par, h, (3,))
         acc[...] += term(right)
         waits(m_args, par, h, (4, 5))
-        wait_sends(x_args, par, h)
+
+        @pl.when(layer > 0)
+        def _():
+            wait_sends(x_args, par, h)
+
         result = (acc[...] + term(opposite)).astype(jnp.bfloat16)
+        if h == 0:
+            forward(m_args, par, 1)
 
         @pl.when(layer < layers - 1)
         def _():
             xbuf[1 - par, rows, own_cols] = result
+            if h == 1:
+                forward(x_args, 1 - par, 0)
             start_own(1 - par, h)
 
         @pl.when(layer == layers - 1)
@@ -708,7 +750,7 @@
                     copy.start()
 
         for h in range(2):
-            project(par, h)
+            project(par, h, layer)
 
             @pl.when(layer > 0)
             def _():
@@ -746,8 +788,8 @@
 
 
 def decode(state, segment_ids, weights):
-    length, block = state.shape
     parts = lax.axis_size("mp")
+    length, block = state.shape[0], state.shape[1] // parts
     copies = lax.axis_size(DP)
     depth = weights.shape[1]
     joined = weights.shape[2] - parts * (block // copies)
@@ -757,7 +799,7 @@
     return pl.pallas_call(
         decoder_kernel,
         out_shape=jax.ShapeDtypeStruct((length // parts, parts * block), jnp.bfloat16),
-        in_specs=[vmem] * 5 + [pl.BlockSpec(memory_space=pl.ANY)],
+        in_specs=[vmem] * 4 + [pl.BlockSpec(memory_space=pl.ANY)] * 2,
         out_specs=vmem,
         scratch_shapes=[
             pltpu.VMEM((2, length, parts * block), jnp.bfloat16),
@@ -779,6 +821,7 @@
             dma((2, copies * parts)),
             dma((3,)),
             dma((3,)),
+            dma((1,)),
         ],
         compiler_params=pltpu.CompilerParams(
             collective_id=0, has_side_effects=True, vmem_limit_bytes=60 * 1024 * 1024
@@ -824,7 +867,7 @@
     )
     own_out = jnp.moveaxis(own_out, 0, 1).reshape(w_out.shape[1], parts * col_share)
     own = jnp.concatenate([own_rows, own_out], axis=1)
-    weights = lax.all_gather(own, SECTION_DP)
+    own, v_out, v_down = lax.optimization_barrier((own, v_out, v_down))
     small = jnp.concatenate([v_qkv[0], v_qkv[1], v_qkv[2], v_out.T, v_up, v_down.T], axis=1)
     sections = lax.axis_size("section")
     batch_all = tile_batch[0].reshape(sections, -1)
@@ -833,7 +876,7 @@
     own_batch = jnp.repeat(own_batch, POOL, axis=1)
     starts = jnp.max(jnp.where(batch_all == section_at, offset_all, -POOL), axis=1)
     place = jnp.repeat(starts, POOL) + jnp.tile(jnp.arange(POOL, dtype=jnp.int32), sections)
-    patches, own = lax.optimization_barrier((patches, own))
+    weights = lax.all_gather(own, SECTION_DP)
     state, token_weight = encode(
         patches,
         vis_gain,

time: 460 us -> 423 us (0.920)
  waiting for transfers between devices: 31.6 us -> 5.75 us
  Pallas kernels: 385 us -> 372 us
    pallas_call x1, Pallas kernels: 252 us -> 202 us  [decode(): pl.pallas_call(decoder_kernel, out_shape=jax.ShapeDtypeStruct((length //...]
    pallas_call x1, Pallas kernels: 133 us -> 169 us  [encode(): pl.pallas_call(vision_kernel, out_shape=(jax.ShapeDtypeStruct((length, 4...]
    all_gather x1, waiting for transfers between devices: 25.9 us -> 0.02 us  [shards(): weights = lax.all_gather(own, SECTION_DP)]
  transfers between devices with their start and end apart: 2 -> 2, of which waited for: 2 -> 1; matrix products, arithmetic and copies ran while one was open for 2% -> 2% of each run, Pallas kernels for 29% -> 40%
where the time goes in v4:
time: 423 us; the launch traced here: 420 us
  Pallas kernels  372 us (88%)
  local copies, waits for them, and re-layouts  19.1 us (5%)
  between operations  14.2 us (3%)
  waiting for transfers between devices  5.75 us (1%)
  other arithmetic  4.91 us (1%)
  starting transfers between devices  4.41 us (1%)
    pallas_call x1, Pallas kernels, decode(): pl.pallas_call(decoder_kernel, out_shape=jax.ShapeDtypeStruct((length //...  202 us
    pallas_call x1, Pallas kernels, encode(): pl.pallas_call(vision_kernel, out_shape=(jax.ShapeDtypeStruct((length, 4...  169 us
    unnamed x33, local copies, waits for them, and re-layouts  10.5 us
  transfers between devices with their start and end apart: 2, of which 1 were waited for; matrix products, arithmetic and copies ran while one was open for 2% of the time, Pallas kernels for 40%

profile of v4, /device:TPU:0, one launch (start us, length us, event | category | flops | bytes accessed | tf_op | source)
XLA Modules:
  0.0 420.1 jit_solution(8454773867081819238)
XLA Ops:
  7.2 0.0 copy-start
  7.2 6.5 %copy.20 = bf16[1,512,4096]{1,2,0:T(8,128)(2,1)} copy(bf16[1,512,4096]{2,1,0:T(8,128)(2,1)} %param.26) | data formatting | bytes 8388608 | tf_op args[9]
  13.7 1.2 constant_dynamic-slice_fusion
  14.9 1.0 copy.21
  15.9 4.4 %all-to-all-start = ((bf16[4,512,128]{2,1,0:T(8,128)(2,1)}), bf16[4,512,128]{2,1,0:T(8,128)(2,1)S(1)}, u32[]{:S(2)}, u32[]{:S(2)}) async-start(bf16[4,512,128]{2,1,0:T(8,128)(2,1)} %bitcast.13), calls=%async_computation | async-start | bytes 1048576 | tf_op jit(solution)/shard_map/all_to_all | solution.py:865
  20.3 0.0 all-gather.3.cloned.1.call-start
  20.4 0.0 copy-done.2
  20.4 1.5 fusion.4
  21.8 1.0 dynamic-slice_bitcast_fusion.1
  22.8 0.0 copy-done
  22.8 1.1 dynamic-slice_bitcast_fusion
  23.9 0.2 multiply_convert_fusion
  24.1 5.7 %all-to-all-done = bf16[4,512,128]{2,1,0:T(8,128)(2,1)S(1)} async-done(((bf16[4,512,128]{2,1,0:T(8,128)(2,1)}), bf16[4,512,128]{2,1,0:T(8,128)(2,1)S(1)}, u32[]{:S(2)}, u32[]{:S(2)}) %all-to-all-start) | async-done | bytes 524320 | tf_op jit(solution)/shard_map/all_to_all | solution.py:865
  29.8 0.2 copy.22
  30.0 0.2 copy.23
  30.3 0.0 copy-start.9
  30.3 0.0 copy-start.10
  30.3 0.0 copy-start.8
  30.3 1.2 pad_maximum_fusion
  31.5 0.0 all-gather.3.cloned.1.call-update
  31.5 0.5 broadcast.28
  32.0 0.0 copy-done.9
  32.0 0.7 reduce.6
  32.7 0.0 copy-done.10
  32.7 0.7 reduce.7
  33.4 0.1 reshape_squeeze.9
  33.5 0.1 broadcast_in_dim.19
  33.5 0.6 broadcast_in_dim.20.own_ref
  34.1 0.1 reshape_squeeze.10
  34.2 0.1 select_reduce_fusion
  34.3 0.1 iota_add_fusion
  34.4 0.7 add.30.place_ref
  35.1 0.0 copy-done.8
  35.1 0.9 copy.24.seg_col
  35.9 1.0 fusion.2
  36.9 1.0 pad_maximum_fusion.1
  37.9 0.0 copy-done.6
  38.0 0.0 copy-done.7
  38.0 0.0 copy-done.4
  38.0 0.7 copy-done.3
  38.7 169.3 %shard_map.176 = (bf16[512,4096]{1,0:T(8,128)(2,1)}, f32[1,128]{1,0:T(1,128)}) custom-call(bf16[512,1024]{1,0:T(8,128)(2,1)} %patches_ref.1, f32[2,1024]{1,0:T(2,128)} %gain_ref.1, f32[2,1024]{1,0:T(2,128)} %bias_ref.1, bf16[128,4096]{1,0:T(8,128)(2,1)} %bitcast.35, s32[1,128]{1,0:T(1,128)} %mask_ref.1, s32[1,128]{1,0:T(1,128)} %broadcast_in_dim.20.own_ref, ...), custom_call_target="tpu_custom_call" | custom-call | tf_op jit(solution)/shard_map/pallas_call | solution.py:451
  208.1 0.0 all-gather.3.cloned.1.call-done
  208.1 0.0 copy-start.1
  208.1 202.3 %shard_map.177 = bf16[128,4096]{1,0:T(8,128)(2,1)} custom-call(s32[512,1]{1,0:T(8,128)} %copy.24.seg_col, s32[1,512]{1,0:T(1,128)} %bitcast.36, f32[512,128]{1,0:T(8,128)} %get-tuple-element.17.cos_ref, f32[512,128]{1,0:T(8,128)} %get-tuple-element.18.sin_ref, bf16[512,4096]{1,0:T(8,128)(2,1)} %get-tuple-element.9.s0_ref, bf16[32,512,1280]{2,1,0:T(8,128)(2,1)} %bitcast.30), custom_call_target="tpu_custom_call" | custom-call | tf_op jit(solution)/shard_map/pallas_call | solution.py:799
  410.4 0.0 copy-start.11
  410.4 2.3 copy.32
  412.7 0.0 copy-done.11
  412.7 0.5 copy.33
  (17 shorter events, 0.1 us)
Async XLA Ops:
  7.2 15.6 %copy-start = (f32[1,4096]{1,0:T(1,128)S(1)}, f32[1,4096]{1,0:T(1,128)}, u32[]{:S(2)}) copy-start(f32[1,4096]{1,0:T(1,128)} %param.23) | copy-start | bytes 49156
  13.7 6.7 %copy-start.2 = (bf16[1,2,4096,128]{3,2,1,0:T(8,128)(2,1)S(1)}, bf16[1,2,4096,128]{3,2,1,0:T(8,128)(2,1)}, u32[]{:S(2)}) copy-start(bf16[1,2,4096,128]{3,2,1,0:T(8,128)(2,1)} %param.25) | copy-start | bytes 6291460
  15.9 13.9 %all-to-all-start = ((bf16[4,512,128]{2,1,0:T(8,128)(2,1)}), bf16[4,512,128]{2,1,0:T(8,128)(2,1)S(1)}, u32[]{:S(2)}, u32[]{:S(2)}) async-start(bf16[4,512,128]{2,1,0:T(8,128)(2,1)} %bitcast.13), calls=%async_computation | async-start | bytes 1048576 | tf_op jit(solution)/shard_map/all_to_all | solution.py:865
  20.3 187.7 %all-gather.3.cloned.1.call-start = ((), (), s32[]{:S(2)}) async-start(), calls=%async_computation.1 | async-start | bytes 43253760 | tf_op jit(solution)/shard_map/all_gather | solution.py:879
  30.3 1.8 copy-start.9
  30.3 2.4 copy-start.10
  30.3 4.8 %copy-start.8 = (s32[1,1,512]{2,1,0:T(1,128)S(1)}, s32[1,1,512]{2,1,0:T(1,128)}, u32[]{:S(2)}) copy-start(s32[1,1,512]{2,1,0:T(1,128)} %param.19) | copy-start | bytes 6148
  31.5 6.5 %copy-start.6 = (bf16[3,32,256]{2,1,0:T(8,128)(2,1)S(1)}, bf16[3,32,256]{2,1,0:T(8,128)(2,1)}, u32[]{:S(2)}) copy-start(bf16[3,32,256]{2,1,0:T(8,128)(2,1)} %param.29) | copy-start | bytes 147460
  31.5 6.5 %copy-start.7 = (bf16[256,32]{0,1:T(8,128)(2,1)S(1)}, bf16[256,32]{0,1:T(8,128)(2,1)}, u32[]{:S(2)}) copy-start(bf16[256,32]{0,1:T(8,128)(2,1)} %param.30) | copy-start | bytes 49156
  31.5 6.5 %copy-start.4 = (bf16[32,1024]{1,0:T(8,128)(2,1)S(1)}, bf16[32,1024]{1,0:T(8,128)(2,1)}, u32[]{:S(2)}) copy-start(bf16[32,1024]{1,0:T(8,128)(2,1)} %param.31) | copy-start | bytes 196612
  31.5 6.5 %copy-start.5 = (bf16[1024,32]{0,1:T(8,128)(2,1)S(1)}, bf16[1024,32]{0,1:T(8,128)(2,1)}, u32[]{:S(2)}) copy-start(bf16[1024,32]{0,1:T(8,128)(2,1)} %param.32) | copy-start | bytes 196612
  38.0 0.7 copy-start.3
  208.1 205.1 %copy-start.1 = (f32[1,4096]{1,0:T(1,128)S(1)}, f32[1,4096]{1,0:T(1,128)}, u32[]{:S(2)}) copy-start(f32[1,4096]{1,0:T(1,128)} %param.23) | copy-start | bytes 49156
  410.4 2.3 copy-start.11
Sparse Core Ops, SparseCore 0:
  31.6 165.9 all-gather.2

commit v5 on v4

--- a/solution.py
+++ b/solution.py
@@ -57,7 +57,7 @@
     pooled,
     blk,
     arrived,
-    txt,
+    images,
     cbuf,
     gs,
     gr,
@@ -206,15 +206,29 @@
             total = total + cbuf[stage, step - 1]
         return total
 
-    def text_copy(step):
-        target = lax.rem(me + step, parts)
-        return remote(
-            text_ref.at[:, pl.ds(pl.multiple_of(target * block, block), block)],
-            txt.at[pl.ds(pl.multiple_of(me * token_share, token_share), token_share), :],
-            ts.at[step - 1],
-            tr.at[step - 1],
-            along_x(step),
-        )
+    def text_copy(kind, incoming):
+        if incoming:
+            back = (3, 3, 1, 1, 2, 2)[kind]
+        else:
+            back = (0, 0, 0, 0, 3, 1)[kind]
+        size = text_ref.shape[1] // 2
+        cols = pl.ds((0, 1, 1, 0, 0, 1)[kind] * size, size)
+        at = pl.multiple_of(lax.rem(me + back, parts) * token_share, token_share)
+        dst = whole.at[pl.ds(at, token_share), cols]
+        src = dst if incoming or kind >= 4 else text_ref.at[:, cols]
+        return remote(src, dst, ts.at[kind], tr.at[kind], along_x((1, 1, 3, 3, 1, 3)[kind]))
+
+    def text_pass():
+        text_copy(0, True).wait_recv()
+        text_copy(4, False).start()
+        text_copy(2, True).wait_recv()
+        text_copy(5, False).start()
+
+    def text_wait():
+        for kind in (1, 3, 4, 5):
+            text_copy(kind, True).wait_recv()
+        for kind in range(6):
+            text_copy(kind, False).wait_send()
 
     def scatter_copy(stage, tile, step):
         target = lax.rem(me + step, parts)
@@ -262,11 +276,11 @@
     pl.semaphore_wait(barrier, len(others))
     gather_start(0)
     gather_start(1)
-    for step in (1, 3, 2):
-        text_copy(step).start()
     count_send(0)
+    for kind in (0, 2, 1, 3):
+        text_copy(kind, False).start()
     own_rows = pl.ds(pl.multiple_of(me * token_share, token_share), token_share)
-    txt[own_rows, :] = text_ref[:, pl.ds(pl.multiple_of(me * block, block), block)]
+    whole[own_rows, :] = text_ref[...]
     first = normed(patches_ref[...].astype(jnp.float32), 0)
     gather_a(0)
     gather_a(1)
@@ -274,6 +288,7 @@
     gather_b2(0)
     cbuf[1, 3] = count_sum(0)
     count_send(1)
+    text_pass()
     gather_end(0)
     joined[...] = jnp.dot(first, sm[:, : 3 * local], preferred_element_type=jnp.float32)
     low = lax.broadcasted_iota(jnp.int32, (PATCH, 2 * VHD), 1) < VHD
@@ -365,6 +380,7 @@
     middle(1)
     cbuf[2, 3] = count_sum(1)
     count_send(2)
+    text_wait()
     for tile in range(tiles):
         expand(tile)
     for tile in range(tiles):
@@ -403,16 +419,11 @@
     picked = lax.broadcasted_iota(jnp.int32, (length, 4 * POOL), 0) == place_ref[...]
     picked = picked.astype(jnp.float32)
     covered = jnp.max(picked, axis=1, keepdims=True) > 0.5
-    for step in (1, 3, 2):
-        text_copy(step).wait()
     for copies_of in started:
         for copy in copies_of:
             copy.wait_send()
     for step in (1, 3, 2):
         home_copy(step).wait()
-    placed = jnp.dot(
-        picked.astype(jnp.bfloat16), arrived[...], preferred_element_type=jnp.float32
-    )
     half = block // 2
 
     def state_copy(kind, incoming):
@@ -421,22 +432,34 @@
         else:
             back = (0, 0, 0, 0, 3, 1)[kind]
         at = lax.rem(me + back, parts) * block + (0, 1, 1, 0, 0, 1)[kind] * half
-        ref = whole.at[:, pl.ds(pl.multiple_of(at, half), half)]
+        ref = images.at[:, pl.ds(pl.multiple_of(at, half), half)]
         return remote(ref, ref, hs.at[kind], hr.at[kind], along_x((1, 1, 3, 3, 1, 3)[kind]))
 
-    first_state = jnp.where(covered, placed, txt[...].astype(jnp.float32)).astype(jnp.bfloat16)
-    whole[:, pl.ds(pl.multiple_of(me * block, block), block)] = first_state
+    images[:, pl.ds(pl.multiple_of(me * block, block), block)] = arrived[...]
     for kind in (0, 2, 1, 3):
         state_copy(kind, False).start()
     state_copy(0, True).wait_recv()
     state_copy(4, False).start()
     state_copy(2, True).wait_recv()
     state_copy(5, False).start()
-    for kind in (1, 3, 4, 5):
+    picked = picked.astype(jnp.bfloat16)
+
+    def settle(back):
+        cols = pl.ds(pl.multiple_of(lax.rem(me + back, parts) * block, block), block)
+        placed = jnp.dot(picked, images[:, cols], preferred_element_type=jnp.float32)
+        kept = jnp.where(covered, placed, whole[:, cols].astype(jnp.float32))
+        state_ref[:, cols] = kept.astype(jnp.bfloat16)
+
+    settle(0)
+    state_copy(1, True).wait_recv()
+    settle(3)
+    state_copy(3, True).wait_recv()
+    settle(1)
+    for kind in (4, 5):
         state_copy(kind, True).wait_recv()
+    settle(2)
     for kind in range(6):
         state_copy(kind, False).wait_send()
-    state_ref[...] = whole[...]
 
 
 def encode(patches, vis_gain, vis_bias, text, mask, own, place, small, proj):
@@ -468,7 +491,7 @@
             pltpu.VMEM((tiles * POOL, 4 * width), bf16),
             pltpu.VMEM((4 * POOL, block), bf16),
             pltpu.VMEM((4 * POOL, block), bf16),
-            pltpu.VMEM((length, block), bf16),
+            pltpu.VMEM((4 * POOL, 4 * block), bf16),
             pltpu.VMEM((4, 4, 8, 128), jnp.float32),
             dma((2, 31)),
             dma((2, 31)),
@@ -476,8 +499,8 @@
             dma((4, tiles, 3)),
             dma((3,)),
             dma((3,)),
-            dma((3,)),
-            dma((3,)),
+            dma((6,)),
+            dma((6,)),
             dma((4, 3)),
             dma((4, 3)),
             dma((2,)),
@@ -702,6 +725,16 @@
         sent(2, *m_args, par, h).start()
         sent(1, *m_args, par, h).start()
 
+    def shared(target, source):
+        return pltpu.make_async_remote_copy(
+            src_ref=fin.at[pl.ds(target * token_share, token_share), :],
+            dst_ref=hid.at[:, pl.ds(pl.multiple_of(source * block, block), block)],
+            send_sem=fs.at[target],
+            recv_sem=fr.at[source],
+            device_id={"mp": target},
+            device_id_type=MESH,
+        )
+
     def leave(par, h, layer):
         rows = pl.ds(h * half, half)
 
@@ -736,6 +769,15 @@
         @pl.when(layer == layers - 1)
         def _():
             fin[rows, :] = result
+            for target in (2 * h, 2 * h + 1):
+
+                @pl.when(target != me)
+                def _():
+                    shared(target, me).start()
+
+                @pl.when(target == me)
+                def _():
+                    hid[:, own_cols] = fin[target * token_share : (target + 1) * token_share, :]
 
     def one_layer(layer, carry):
         par = lax.rem(layer, 2)
@@ -766,24 +808,15 @@
     lax.fori_loop(0, layers, one_layer, 0)
     last = (layers - 1) % 2
 
-    def shared(step):
-        target = lax.rem(me + step, parts)
-        return pltpu.make_async_remote_copy(
-            src_ref=fin.at[pl.ds(pl.multiple_of(target * token_share, token_share), token_share), :],
-            dst_ref=hid.at[:, own_cols],
-            send_sem=fs.at[step - 1],
-            recv_sem=fr.at[step - 1],
-            device_id={"mp": target},
-            device_id_type=MESH,
-        )
-
-    for step in (2, 1, 3):
-        shared(step).start()
-    hid[:, own_cols] = fin[pl.ds(pl.multiple_of(me * token_share, token_share), token_share), :]
     for h in range(2):
         wait_sends(m_args, last, h)
-    for step in (2, 1, 3):
-        shared(step).wait()
+    for target in range(parts):
+
+        @pl.when(target != me)
+        def _():
+            shared(target, me).wait_send()
+            shared(target, target).wait_recv()
+
     out_ref[...] = hid[...]
 
 
@@ -819,8 +852,8 @@
             dma((2, 2, 6)),
             dma((2, copies)),
             dma((2, copies * parts)),
-            dma((3,)),
-            dma((3,)),
+            dma((4,)),
+            dma((4,)),
             dma((1,)),
         ],
         compiler_params=pltpu.CompilerParams(
@@ -860,12 +893,14 @@
     own_rows = (own_rows.astype(jnp.float32) * own_gain[:, None]).astype(jnp.bfloat16)
     block_width = model_width // parts
     col_share = block_width // copies
-    own_out = w_out[0].reshape(w_out.shape[1], parts, copies, col_share)
-    own_out = lax.dynamic_slice_in_dim(own_out, copy_at, 1, 2)[:, :, 0]
+    own_out = [
+        lax.dynamic_slice_in_dim(w_out[0], part * block_width + copy_at * col_share, col_share, 1)
+        for part in range(parts)
+    ]
     own_out = lax.all_to_all(
-        jnp.moveaxis(own_out, 1, 0), "mp", split_axis=0, concat_axis=0, tiled=True
+        jnp.stack(own_out), "mp", split_axis=0, concat_axis=0, tiled=True
     )
-    own_out = jnp.moveaxis(own_out, 0, 1).reshape(w_out.shape[1], parts * col_share)
+    own_out = jnp.concatenate([own_out[part] for part in range(parts)], axis=1)
     own = jnp.concatenate([own_rows, own_out], axis=1)
     own, v_out, v_down = lax.optimization_barrier((own, v_out, v_down))
     small = jnp.concatenate([v_qkv[0], v_qkv[1], v_qkv[2], v_out.T, v_up, v_down.T], axis=1)

time: 423 us -> 406 us (0.960)
  Pallas kernels: 372 us -> 359 us
  local copies, waits for them, and re-layouts: 19.1 us -> 12.4 us
    pallas_call x1, Pallas kernels: 169 us -> 158 us  [encode(): pl.pallas_call(vision_kernel, out_shape=(jax.ShapeDtypeStruct((length, 4...]
    unnamed x33 -> x37, local copies, waits for them, and re-layouts: 10.5 us -> 5.21 us
  transfers between devices with their start and end apart: 2 -> 2, of which waited for: 1 -> 2; matrix products, arithmetic and copies ran while one was open for 2% -> 3% of each run, Pallas kernels for 40% -> 39%
where the time goes in v5:
time: 406 us; the launch traced here: 401 us
  Pallas kernels  359 us (88%)
  between operations  14.3 us (4%)
  local copies, waits for them, and re-layouts  12.4 us (3%)
  waiting for transfers between devices  6.44 us (2%)
  other arithmetic  4.65 us (1%)
  starting transfers between devices  4.41 us (1%)
    pallas_call x1, Pallas kernels, decode(): pl.pallas_call(decoder_kernel, out_shape=jax.ShapeDtypeStruct((length //...  201 us
    pallas_call x1, Pallas kernels, encode(): pl.pallas_call(vision_kernel, out_shape=(jax.ShapeDtypeStruct((length, 4...  158 us
  transfers between devices with their start and end apart: 2, of which 2 were waited for; matrix products, arithmetic and copies ran while one was open for 3% of the time, Pallas kernels for 39%

profile of v5, /device:TPU:0, one launch (start us, length us, event | category | flops | bytes accessed | tf_op | source)
XLA Modules:
  0.0 400.9 jit_solution(13775437118475232337)
XLA Ops:
  7.2 0.0 copy-start
  7.2 0.0 copy-start.3
  7.2 1.3 constant_dynamic-slice_fusion.3
  8.5 0.9 pad_maximum_fusion
  9.4 4.4 %all-to-all-start = ((bf16[4,512,128]{2,1,0:T(8,128)(2,1)}), bf16[4,512,128]{2,1,0:T(8,128)(2,1)S(1)}, u32[]{:S(2)}, u32[]{:S(2)}) async-start(bf16[4,512,128]{2,1,0:T(8,128)(2,1)} %pad_maximum_fusion), calls=%async_computation | async-start | bytes 1048576 | tf_op jit(solution)/shard_map/all_to_all | solution.py:900
  13.8 0.0 all-gather.3.cloned.1.call-start
  13.8 0.0 copy-done.3
  13.8 1.5 fusion.9
  15.3 1.0 dynamic-slice_bitcast_fusion.1
  16.3 0.0 copy-done
  16.3 1.1 dynamic-slice_bitcast_fusion
  17.4 0.2 fusion
  17.6 0.0 copy-start.10
  17.6 0.0 copy-start.11
  17.6 0.0 copy-start.9
  17.6 5.7 %all-to-all-done = bf16[4,512,128]{2,1,0:T(8,128)(2,1)S(1)} async-done(((bf16[4,512,128]{2,1,0:T(8,128)(2,1)}), bf16[4,512,128]{2,1,0:T(8,128)(2,1)S(1)}, u32[]{:S(2)}, u32[]{:S(2)}) %all-to-all-start) | async-done | bytes 524320 | tf_op jit(solution)/shard_map/all_to_all | solution.py:900
  23.4 0.0 copy-start.2
  23.5 0.0 copy-start.7
  23.5 1.1 copy-done.2
  24.5 0.0 all-gather.3.cloned.1.call-update
  24.5 0.0 copy-start.8
  24.6 0.0 copy-start.5
  24.6 0.0 copy-start.6
  24.6 0.5 broadcast.28
  25.1 0.0 copy-done.10
  25.1 0.7 reduce.6
  25.8 0.0 copy-done.11
  25.8 0.7 reduce.7
  26.4 0.1 reshape_squeeze.6
  26.5 0.1 broadcast_in_dim.19
  26.6 0.6 broadcast_in_dim.20.own_ref
  27.2 0.1 reshape_squeeze.7
  27.3 0.1 select_reduce_fusion
  27.4 0.1 iota_add_fusion
  27.5 0.7 add.45.place_ref
  28.1 0.9 copy.19.seg_col
  29.0 1.0 fusion.7
  30.0 1.0 pad_maximum_fusion.1
  31.0 0.0 copy-done.7
  31.1 0.0 copy-done.5
  31.1 0.0 copy-done.6
  31.1 0.7 copy-done.4
  31.8 158.1 %shard_map.176 = (bf16[512,4096]{1,0:T(8,128)(2,1)}, f32[1,128]{1,0:T(1,128)}) custom-call(bf16[512,1024]{1,0:T(8,128)(2,1)} %patches_ref.1, f32[2,1024]{1,0:T(2,128)} %gain_ref.1, f32[2,1024]{1,0:T(2,128)} %bias_ref.1, bf16[128,4096]{1,0:T(8,128)(2,1)} %bitcast.42, s32[1,128]{1,0:T(1,128)} %mask_ref.1, s32[1,128]{1,0:T(1,128)} %broadcast_in_dim.20.own_ref, ...), custom_call_target="tpu_custom_call" | custom-call | tf_op jit(solution)/shard_map/pallas_call | solution.py:474
  189.9 0.8 all-gather.3.cloned.1.call-done
  190.7 200.6 %shard_map.177 = bf16[128,4096]{1,0:T(8,128)(2,1)} custom-call(s32[512,1]{1,0:T(8,128)} %copy.19.seg_col, s32[1,512]{1,0:T(1,128)} %bitcast.43, f32[512,128]{1,0:T(8,128)} %get-tuple-element.21.cos_ref, f32[512,128]{1,0:T(8,128)} %get-tuple-element.22.sin_ref, bf16[512,4096]{1,0:T(8,128)(2,1)} %get-tuple-element.9.s0_ref, bf16[32,512,1280]{2,1,0:T(8,128)(2,1)} %bitcast.40), custom_call_target="tpu_custom_call" | custom-call | tf_op jit(solution)/shard_map/pallas_call | solution.py:832
  391.3 2.3 copy.31
  393.6 0.5 copy.32
  394.1 0.0 copy-done.1
  (19 shorter events, 0.2 us)
Async XLA Ops:
  7.2 9.1 %copy-start = (f32[1,4096]{1,0:T(1,128)S(1)}, f32[1,4096]{1,0:T(1,128)}, u32[]{:S(2)}) copy-start(f32[1,4096]{1,0:T(1,128)} %param.23) | copy-start | bytes 49156
  7.2 6.6 %copy-start.3 = (bf16[1,2,4096,128]{3,2,1,0:T(8,128)(2,1)S(1)}, bf16[1,2,4096,128]{3,2,1,0:T(8,128)(2,1)}, u32[]{:S(2)}) copy-start(bf16[1,2,4096,128]{3,2,1,0:T(8,128)(2,1)} %param.25) | copy-start | bytes 6291460
  9.4 13.9 %all-to-all-start = ((bf16[4,512,128]{2,1,0:T(8,128)(2,1)}), bf16[4,512,128]{2,1,0:T(8,128)(2,1)S(1)}, u32[]{:S(2)}, u32[]{:S(2)}) async-start(bf16[4,512,128]{2,1,0:T(8,128)(2,1)} %pad_maximum_fusion), calls=%async_computation | async-start | bytes 1048576 | tf_op jit(solution)/shard_map/all_to_all | solution.py:900
  13.8 176.9 %all-gather.3.cloned.1.call-start = ((), (), s32[]{:S(2)}) async-start(), calls=%async_computation.1 | async-start | bytes 43253760 | tf_op jit(solution)/shard_map/all_gather | solution.py:914
  17.6 7.5 %copy-start.10 = (s32[1,8]{1,0:T(1,128)S(1)}, s32[1,8]{1,0:T(1,128)}, u32[]{:S(2)}) copy-start(s32[1,8]{1,0:T(1,128)} %param.21) | copy-start | bytes 100
  17.6 8.2 %copy-start.11 = (s32[1,8]{1,0:T(1,128)S(1)}, s32[1,8]{1,0:T(1,128)}, u32[]{:S(2)}) copy-start(s32[1,8]{1,0:T(1,128)} %param.22) | copy-start | bytes 100
  17.6 10.5 %copy-start.9 = (s32[1,1,512]{2,1,0:T(1,128)S(1)}, s32[1,1,512]{2,1,0:T(1,128)}, u32[]{:S(2)}) copy-start(s32[1,1,512]{2,1,0:T(1,128)} %param.19) | copy-start | bytes 6148
  23.4 1.1 copy-start.2
  23.5 7.6 %copy-start.7 = (bf16[3,32,256]{2,1,0:T(8,128)(2,1)S(1)}, bf16[3,32,256]{2,1,0:T(8,128)(2,1)}, u32[]{:S(2)}) copy-start(bf16[3,32,256]{2,1,0:T(8,128)(2,1)} %param.29) | copy-start | bytes 147460
  24.5 6.5 %copy-start.8 = (bf16[256,32]{0,1:T(8,128)(2,1)S(1)}, bf16[256,32]{0,1:T(8,128)(2,1)}, u32[]{:S(2)}) copy-start(bf16[256,32]{0,1:T(8,128)(2,1)} %param.30) | copy-start | bytes 49156
  24.6 6.5 %copy-start.5 = (bf16[32,1024]{1,0:T(8,128)(2,1)S(1)}, bf16[32,1024]{1,0:T(8,128)(2,1)}, u32[]{:S(2)}) copy-start(bf16[32,1024]{1,0:T(8,128)(2,1)} %param.31) | copy-start | bytes 196612
  24.6 6.5 %copy-start.6 = (bf16[1024,32]{0,1:T(8,128)(2,1)S(1)}, bf16[1024,32]{0,1:T(8,128)(2,1)}, u32[]{:S(2)}) copy-start(bf16[1024,32]{0,1:T(8,128)(2,1)} %param.32) | copy-start | bytes 196612
  31.1 0.7 copy-start.4
  190.7 203.4 %copy-start.1 = (f32[1,4096]{1,0:T(1,128)S(1)}, f32[1,4096]{1,0:T(1,128)}, u32[]{:S(2)}) copy-start(f32[1,4096]{1,0:T(1,128)} %param.23) | copy-start | bytes 49156
  391.3 2.3 copy-start.12
Sparse Core Ops, SparseCore 0:
  24.7 165.9 all-gather.2

commit v6 on v5

--- a/solution.py
+++ b/solution.py
@@ -558,16 +558,15 @@
     me = lax.axis_index("mp")
     right, opposite, left = (lax.rem(me + step, parts) for step in (1, 2, 3))
 
+    def joined_copy(layer, par, d):
+        return pltpu.make_async_copy(
+            w_any.at[layer * copies + d, :, pl.ds(0, joined)],
+            wjb.at[par, pl.ds(pl.multiple_of(d * depth, depth), depth), :],
+            js.at[par, d],
+        )
+
     def weight_copies(layer, par):
-        found = []
-        for d in range(copies):
-            found.append(
-                pltpu.make_async_copy(
-                    w_any.at[layer * copies + d, :, pl.ds(0, joined)],
-                    wjb.at[par, pl.ds(d * depth, depth), :],
-                    js.at[par, d],
-                )
-            )
+        found = [joined_copy(layer, par, d) for d in range(copies)]
         for d in range(copies):
             for part in range(parts):
                 found.append(
@@ -656,6 +655,9 @@
         rows = pl.ds(h * half, half)
 
         def add(source, first):
+            if h == 0:
+                for at in range(copies // parts):
+                    joined_copy(layer, par, source * (copies // parts) + at).wait()
             cols = pl.ds(pl.multiple_of(source * block, block), block)
             values = xbuf[par, rows, cols]
             product = jnp.dot(values, wjb[par, cols, :], preferred_element_type=jnp.float32)
@@ -781,18 +783,16 @@
 
     def one_layer(layer, carry):
         par = lax.rem(layer, 2)
-        joined_copies, out_copies = weight_copies(layer, par)
-        for copy in joined_copies:
-            copy.wait()
-
-        @pl.when(layer < layers - 1)
-        def _():
-            for copies_of in weight_copies(layer + 1, 1 - par):
-                for copy in copies_of:
-                    copy.start()
-
+        out_copies = weight_copies(layer, par)[1]
         for h in range(2):
             project(par, h, layer)
+            if h == 0:
+
+                @pl.when(layer < layers - 1)
+                def _():
+                    for copies_of in weight_copies(layer + 1, 1 - par):
+                        for copy in copies_of:
+                            copy.start()
 
             @pl.when(layer > 0)
             def _():

time: 406 us -> 405 us (level)
  no operation moved by 1% of the time
where the time goes in v6:
time: 405 us; the launch traced here: 401 us
  Pallas kernels  359 us (89%)
  between operations  14.3 us (4%)
  local copies, waits for them, and re-layouts  12.4 us (3%)
  waiting for transfers between devices  6.44 us (2%)
  other arithmetic  4.65 us (1%)
  starting transfers between devices  4.41 us (1%)
    pallas_call x1, Pallas kernels, decode(): pl.pallas_call(decoder_kernel, out_shape=jax.ShapeDtypeStruct((length //...  201 us
    pallas_call x1, Pallas kernels, encode(): pl.pallas_call(vision_kernel, out_shape=(jax.ShapeDtypeStruct((length, 4...  158 us
  transfers between devices with their start and end apart: 2, of which 2 were waited for; matrix products, arithmetic and copies ran while one was open for 3% of the time, Pallas kernels for 39%

profile of v6, /device:TPU:0, one launch (start us, length us, event | category | flops | bytes accessed | tf_op | source)
XLA Modules:
  0.0 400.9 jit_solution(15829215665904920365)
XLA Ops:
  7.2 0.0 copy-start
  7.2 0.0 copy-start.3
  7.2 1.3 constant_dynamic-slice_fusion.3
  8.5 0.9 pad_maximum_fusion
  9.4 4.4 %all-to-all-start = ((bf16[4,512,128]{2,1,0:T(8,128)(2,1)}), bf16[4,512,128]{2,1,0:T(8,128)(2,1)S(1)}, u32[]{:S(2)}, u32[]{:S(2)}) async-start(bf16[4,512,128]{2,1,0:T(8,128)(2,1)} %pad_maximum_fusion), calls=%async_computation | async-start | bytes 1048576 | tf_op jit(solution)/shard_map/all_to_all | solution.py:900
  13.8 0.0 all-gather.3.cloned.1.call-start
  13.8 0.0 copy-done.3
  13.8 1.5 fusion.9
  15.3 1.0 dynamic-slice_bitcast_fusion.1
  16.3 0.0 copy-done
  16.3 1.1 dynamic-slice_bitcast_fusion
  17.4 0.2 fusion
  17.6 0.0 copy-start.10
  17.6 0.0 copy-start.11
  17.6 0.0 copy-start.9
  17.6 5.7 %all-to-all-done = bf16[4,512,128]{2,1,0:T(8,128)(2,1)S(1)} async-done(((bf16[4,512,128]{2,1,0:T(8,128)(2,1)}), bf16[4,512,128]{2,1,0:T(8,128)(2,1)S(1)}, u32[]{:S(2)}, u32[]{:S(2)}) %all-to-all-start) | async-done | bytes 524320 | tf_op jit(solution)/shard_map/all_to_all | solution.py:900
  23.4 0.0 copy-start.2
  23.5 0.0 copy-start.7
  23.5 1.1 copy-done.2
  24.5 0.0 all-gather.3.cloned.1.call-update
  24.5 0.0 copy-start.8
  24.6 0.0 copy-start.5
  24.6 0.0 copy-start.6
  24.6 0.5 broadcast.28
  25.1 0.0 copy-done.10
  25.1 0.7 reduce.6
  25.8 0.0 copy-done.11
  25.8 0.7 reduce.7
  26.4 0.1 reshape_squeeze.6
  26.5 0.1 broadcast_in_dim.19
  26.6 0.6 broadcast_in_dim.20.own_ref
  27.2 0.1 reshape_squeeze.7
  27.3 0.1 select_reduce_fusion
  27.4 0.1 iota_add_fusion
  27.5 0.7 add.45.place_ref
  28.1 0.9 copy.19.seg_col
  29.0 1.0 fusion.7
  30.0 1.0 pad_maximum_fusion.1
  31.1 0.0 copy-done.8
  31.1 0.0 copy-done.5
  31.1 0.7 copy-done.4
  31.8 158.1 %shard_map.176 = (bf16[512,4096]{1,0:T(8,128)(2,1)}, f32[1,128]{1,0:T(1,128)}) custom-call(bf16[512,1024]{1,0:T(8,128)(2,1)} %patches_ref.1, f32[2,1024]{1,0:T(2,128)} %gain_ref.1, f32[2,1024]{1,0:T(2,128)} %bias_ref.1, bf16[128,4096]{1,0:T(8,128)(2,1)} %bitcast.42, s32[1,128]{1,0:T(1,128)} %mask_ref.1, s32[1,128]{1,0:T(1,128)} %broadcast_in_dim.20.own_ref, ...), custom_call_target="tpu_custom_call" | custom-call | tf_op jit(solution)/shard_map/pallas_call | solution.py:474
  189.9 0.8 all-gather.3.cloned.1.call-done
  190.7 200.5 %shard_map.177 = bf16[128,4096]{1,0:T(8,128)(2,1)} custom-call(s32[512,1]{1,0:T(8,128)} %copy.19.seg_col, s32[1,512]{1,0:T(1,128)} %bitcast.43, f32[512,128]{1,0:T(8,128)} %get-tuple-element.21.cos_ref, f32[512,128]{1,0:T(8,128)} %get-tuple-element.22.sin_ref, bf16[512,4096]{1,0:T(8,128)(2,1)} %get-tuple-element.9.s0_ref, bf16[32,512,1280]{2,1,0:T(8,128)(2,1)} %bitcast.40), custom_call_target="tpu_custom_call" | custom-call | tf_op jit(solution)/shard_map/pallas_call | solution.py:832
  391.2 0.0 copy-start.12
  391.2 2.3 copy.31
  393.5 0.0 copy-done.12
  393.5 0.5 copy.32
  (19 shorter events, 0.2 us)
Async XLA Ops:
  7.2 9.1 %copy-start = (f32[1,4096]{1,0:T(1,128)S(1)}, f32[1,4096]{1,0:T(1,128)}, u32[]{:S(2)}) copy-start(f32[1,4096]{1,0:T(1,128)} %param.23) | copy-start | bytes 49156
  7.2 6.6 %copy-start.3 = (bf16[1,2,4096,128]{3,2,1,0:T(8,128)(2,1)S(1)}, bf16[1,2,4096,128]{3,2,1,0:T(8,128)(2,1)}, u32[]{:S(2)}) copy-start(bf16[1,2,4096,128]{3,2,1,0:T(8,128)(2,1)} %param.25) | copy-start | bytes 6291460
  9.4 13.9 %all-to-all-start = ((bf16[4,512,128]{2,1,0:T(8,128)(2,1)}), bf16[4,512,128]{2,1,0:T(8,128)(2,1)S(1)}, u32[]{:S(2)}, u32[]{:S(2)}) async-start(bf16[4,512,128]{2,1,0:T(8,128)(2,1)} %pad_maximum_fusion), calls=%async_computation | async-start | bytes 1048576 | tf_op jit(solution)/shard_map/all_to_all | solution.py:900
  13.8 176.9 %all-gather.3.cloned.1.call-start = ((), (), s32[]{:S(2)}) async-start(), calls=%async_computation.1 | async-start | bytes 43253760 | tf_op jit(solution)/shard_map/all_gather | solution.py:914
  17.6 7.5 %copy-start.10 = (s32[1,8]{1,0:T(1,128)S(1)}, s32[1,8]{1,0:T(1,128)}, u32[]{:S(2)}) copy-start(s32[1,8]{1,0:T(1,128)} %param.21) | copy-start | bytes 100
  17.6 8.2 %copy-start.11 = (s32[1,8]{1,0:T(1,128)S(1)}, s32[1,8]{1,0:T(1,128)}, u32[]{:S(2)}) copy-start(s32[1,8]{1,0:T(1,128)} %param.22) | copy-start | bytes 100
  17.6 10.5 %copy-start.9 = (s32[1,1,512]{2,1,0:T(1,128)S(1)}, s32[1,1,512]{2,1,0:T(1,128)}, u32[]{:S(2)}) copy-start(s32[1,1,512]{2,1,0:T(1,128)} %param.19) | copy-start | bytes 6148
  23.4 1.1 copy-start.2
  23.5 7.6 %copy-start.7 = (bf16[3,32,256]{2,1,0:T(8,128)(2,1)S(1)}, bf16[3,32,256]{2,1,0:T(8,128)(2,1)}, u32[]{:S(2)}) copy-start(bf16[3,32,256]{2,1,0:T(8,128)(2,1)} %param.29) | copy-start | bytes 147460
  24.5 6.5 %copy-start.8 = (bf16[256,32]{0,1:T(8,128)(2,1)S(1)}, bf16[256,32]{0,1:T(8,128)(2,1)}, u32[]{:S(2)}) copy-start(bf16[256,32]{0,1:T(8,128)(2,1)} %param.30) | copy-start | bytes 49156
  24.6 6.5 %copy-start.5 = (bf16[32,1024]{1,0:T(8,128)(2,1)S(1)}, bf16[32,1024]{1,0:T(8,128)(2,1)}, u32[]{:S(2)}) copy-start(bf16[32,1024]{1,0:T(8,128)(2,1)} %param.31) | copy-start | bytes 196612
  24.6 6.5 %copy-start.6 = (bf16[1024,32]{0,1:T(8,128)(2,1)S(1)}, bf16[1024,32]{0,1:T(8,128)(2,1)}, u32[]{:S(2)}) copy-start(bf16[1024,32]{0,1:T(8,128)(2,1)} %param.32) | copy-start | bytes 196612
  31.1 0.7 copy-start.4
  190.7 203.4 %copy-start.1 = (f32[1,4096]{1,0:T(1,128)S(1)}, f32[1,4096]{1,0:T(1,128)}, u32[]{:S(2)}) copy-start(f32[1,4096]{1,0:T(1,128)} %param.23) | copy-start | bytes 49156
  391.2 2.3 copy-start.12
Sparse Core Ops, SparseCore 0:
  24.7 165.9 all-gather.2
